TPU v7x, 32 devices: a whole 2x2x4 slice. The times are simulated.
32 devices in a mesh: fy: 2 (over x), fx: 8 (over z, y), ch: 2 (over core).
Axes of the slice: x: 2, y: 2, z: 4, core: 2. Of those that a mesh axis runs over, the one named last changes fastest.
Arguments:
- image_cube: float32 [64, 512, 416], P('ch', 'fx', 'fy'), may hold values from 0 to 2
- data_grad: bfloat16 [64, 512, 416], P('ch', 'fx', 'fy'), may hold values from -6 to 6
- dual_coeffs: float32 [64, 896, 512], P('ch', 'fx', 'fy'), may hold values from -6 to 6
- reweights: float32 [896, 512], P('fx', 'fy'), may hold values from 1 to 40
Outputs:
- image_next: float32 [64, 512, 416], P('ch', 'fx', 'fy')
- dual_next: float32 [64, 896, 512], P('ch', 'fx', 'fy')
All inputs are finite; a program needn't handle non-finite values.
Results may differ from a plain program's by a relative error of at most 0.0003.
Values sent between devices are 32-bit elements; how exact they have to be, the bound alone decides.
No kernel may reach another device: no remote copies, remote signals or barrier semaphores. Data moves between devices by JAX's collectives and lax.ppermute only.
A program may use at most 64 MiB of HBM per device.

v0:
```python
import jax
import jax.numpy as jnp
import numpy as np
from jax import lax
from jax.sharding import PartitionSpec as P

LEVELS = 2


LOW_PASS = [
    -0.00011747678400228192,
    0.0006754494059985568,
    -0.0003917403729959771,
    -0.00487035299301066,
    0.008746094047015655,
    0.013981027917015516,
    -0.04408825393106472,
    -0.01736930100202211,
    0.128747426620186,
    0.00047248457399797254,
    -0.2840155429624281,
    -0.015829105256023893,
    0.5853546836548691,
    0.6756307362980128,
    0.3128715909144659,
    0.05441584224308161,
]
TAU_STEP = 0.5
LAMBDA_REG = 1.0
EPSILON = 1e-06


def passed_along(array, axis, by):
    length = lax.axis_size(axis)
    pairs = [(i, i + by) for i in range(length) if 0 <= i + by < length]
    return lax.ppermute(array, axis, pairs)


def level_matrix(length):
    halved = length // 2
    taps_count = len(LOW_PASS)
    matrix = np.zeros((length, length))
    for out_row in range(halved):
        for tap_index in range(taps_count):
            column = (2 * out_row + tap_index) % length
            matrix[out_row, column] += LOW_PASS[tap_index]
            matrix[halved + out_row, column] += (-1) ** tap_index * LOW_PASS[
                taps_count - 1 - tap_index
            ]
    return matrix


def analysis(facet_block, levels):
    result = facet_block
    width_x = facet_block.shape[1]
    width_y = facet_block.shape[2]
    for level_step in range(levels):
        matrix_x = jnp.asarray(level_matrix(width_x), dtype=jnp.float32)
        matrix_y = jnp.asarray(level_matrix(width_y), dtype=jnp.float32)
        corner_part = result[:, :width_x, :width_y]
        corner_part = jnp.einsum(
            "cxy,vy->cxv", corner_part, matrix_y, precision=lax.Precision.HIGHEST
        )
        corner_part = jnp.einsum(
            "ux,cxv->cuv", matrix_x, corner_part, precision=lax.Precision.HIGHEST
        )
        result = result.at[:, :width_x, :width_y].set(corner_part)
        width_x = width_x // 2
        width_y = width_y // 2
    return result


def synthesis(coeff_block, levels):
    result = coeff_block
    for level_step in range(levels - 1, -1, -1):
        width_x = coeff_block.shape[1] // 2**level_step
        width_y = coeff_block.shape[2] // 2**level_step
        matrix_x = jnp.asarray(level_matrix(width_x), dtype=jnp.float32)
        matrix_y = jnp.asarray(level_matrix(width_y), dtype=jnp.float32)
        corner_part = result[:, :width_x, :width_y]
        corner_part = jnp.einsum(
            "ux,cuv->cxv", matrix_x, corner_part, precision=lax.Precision.HIGHEST
        )
        corner_part = jnp.einsum(
            "cxv,vy->cxy", corner_part, matrix_y, precision=lax.Precision.HIGHEST
        )
        result = result.at[:, :width_x, :width_y].set(corner_part)
    return result


def tile_weights(length, intersection, position_index, count):
    positions = jnp.arange(length, dtype=jnp.int32)
    edge = (positions >= length - intersection) & (position_index < count - 1)
    return jnp.where(edge, 0.5**0.5, 1.0).astype(jnp.float32)


def add_tail(base, tail, along):
    length = base.shape[along]
    keep = length - tail.shape[along]
    head = lax.slice_in_dim(base, 0, keep, axis=along)
    rest = lax.slice_in_dim(base, keep, length, axis=along)
    return jnp.concatenate([head, rest + tail], axis=along)


def shards(image_cube, data_grad, dual_coeffs, reweights):
    tile_x = image_cube.shape[1]
    tile_y = image_cube.shape[2]
    intersection = dual_coeffs.shape[1] - tile_x
    weight_map = (
        tile_weights(tile_x, intersection, lax.axis_index("fx"), lax.axis_size("fx"))[:, None]
        * tile_weights(tile_y, intersection, lax.axis_index("fy"), lax.axis_size("fy"))[None, :]
    )
    synthesized = synthesis(dual_coeffs, LEVELS)
    incoming = passed_along(synthesized[:, :intersection, :], "fx", -1)
    own_cols = add_tail(synthesized[:, intersection:, :], incoming, 1)
    incoming_rows = passed_along(own_cols[:, :, :intersection], "fy", -1)
    summed = add_tail(own_cols[:, :, intersection:], incoming_rows, 2)
    adjoint = summed * weight_map
    image_next = jnp.maximum(image_cube - TAU_STEP * (data_grad.astype(jnp.float32) + adjoint), 0.0)
    extrap = (2.0 * image_next - image_cube) * weight_map
    border = passed_along(extrap[:, tile_x - intersection :, :], "fx", 1)
    rows_block = jnp.concatenate([border, extrap], axis=1)
    border_rows = passed_along(rows_block[:, :, tile_y - intersection :], "fy", 1)
    extended = jnp.concatenate([border_rows, rows_block], axis=2)
    updated = dual_coeffs + analysis(extended, LEVELS)
    squared_sum = jnp.sum(updated * updated, axis=0)
    totals = lax.psum_scatter(squared_sum, "ch", scatter_dimension=0, tiled=True)
    share = totals.shape[0]
    local_weights = lax.dynamic_slice_in_dim(reweights, lax.axis_index("ch") * share, share, 0)
    factor_part = jnp.minimum(1.0, LAMBDA_REG * local_weights / jnp.sqrt(totals + EPSILON))
    factor = lax.all_gather(factor_part, "ch", axis=0, tiled=True)
    dual_next = updated * factor[None]
    return (image_next, dual_next)


def solution(mesh):
    return jax.shard_map(
        shards,
        mesh=mesh,
        in_specs=(P("ch", "fx", "fy"), P("ch", "fx", "fy"), P("ch", "fx", "fy"), P("fx", "fy")),
        out_specs=(P("ch", "fx", "fy"), P("ch", "fx", "fy")),
        check_vma=False,
    )
```

profile of v0, /device:TPU:0, one launch (start us, length us, event | category | flops | bytes accessed | tf_op | source)
XLA Modules:
  0.0 186.8 jit_solution(14609696124560412976)
XLA Ops:
  7.2 0.0 copy-start.11
  7.2 0.0 copy-start.8
  7.2 0.0 reduce-scatter.2.cloned.1.call-start
  7.3 0.7 copy-done.11
  7.9 1.4 copy-done
  9.3 0.9 convolution_bitcast_fusion.2
  10.2 0.2 copy-done.2
  10.4 0.9 convolution_dynamic-update-slice_fusion
  11.3 0.0 copy-start.7
  11.3 3.6 %fusion.21 = f32[32,256,112]{1,2,0:T(8,128)S(1)} fusion(f32[32,112,256]{2,1,0:T(8,128)S(1)} %convolution_dynamic-update-slice_fusion, f32[112,112,1]{1,0,2:T(8,128)S(1)} %copy-done.9), kind=kOutput, calls=%fused_computation.39 | convolution fusion | flops 1233125376 | bytes 7390208 | tf_op jit(solution)/shard_map/ux,cuv->cxv/dot_general | solution.py:81
  14.9 3.2 %fusion.6 = f32[32,112,256]{2,1,0:T(8,128)S(1)} fusion(f32[256,256,1]{1,0,2:T(8,128)S(1)} %copy-done.7, f32[32,256,112]{1,2,0:T(8,128)S(1)} %fusion.21), kind=kOutput, calls=%fused_computation.6 | convolution fusion | flops 2818572288 | bytes 7602176 | tf_op jit(solution)/shard_map/cxv,vy->cxy/dot_general | solution.py:84
  18.2 0.1 slice.138
  18.3 1.3 collective-permute-start
  19.6 0.4 copy-done.3
  20.0 37.6 %collective-permute-done = f32[32,48,256]{2,1,0:T(8,128)} collective-permute-done((f32[32,48,256]{2,1,0:T(8,128)S(1)}, f32[32,48,256]{2,1,0:T(8,128)}, u32[]{:S(2)}, u32[]{:S(2)}) %collective-permute-start) | collective-permute-done | bytes 1572896 | tf_op jit(solution)/shard_map/ppermute | solution.py:36
  57.7 2.1 %slice_add_fusion = f32[32,48,256]{2,1,0:T(8,128)S(1)} fusion(f32[32,48,256]{2,1,0:T(8,128)} %collective-permute-done, f32[32,112,256]{2,1,0:T(8,128)} %copy-done.3), kind=kLoop, calls=%fused_computation.23 | loop fusion | flops 393216 | bytes 4718592 | tf_op jit(solution)/shard_map/add | solution.py:102
  59.8 0.1 pad_maximum_fusion.1
  59.8 1.2 copy.14
  61.1 1.3 collective-permute-start.1
  62.4 0.1 broadcast_multiply_fusion.1
  62.4 1.9 %fusion.8 = f32[32,64,160]{2,1,0:T(8,128)} fusion(f32[32,48,256]{2,1,0:T(8,128)S(1)} %slice_add_fusion, f32[32,16,256]{2,1,0:T(8,128)S(1)} %slice.136), kind=kLoop, calls=%fused_computation.13 | loop fusion | flops 327680 | bytes 3407872 | tf_op jit(solution)/shard_map/concatenate | solution.py:102
  64.4 17.6 %collective-permute-done.1 = f32[32,64,48]{1,2,0:T(8,128)} collective-permute-done((f32[32,64,48]{1,2,0:T(8,128)}, f32[32,64,48]{1,2,0:T(8,128)}, u32[]{:S(2)}, u32[]{:S(2)}) %collective-permute-start.1) | collective-permute-done | bytes 393248 | tf_op jit(solution)/shard_map/ppermute | solution.py:36
  82.0 1.5 copy.15
  83.5 0.3 fusion.15
  83.8 1.2 copy-done.4
  85.0 0.6 copy-done.6
  85.7 3.4 %subtract_multiply_fusion = (f32[32,64,208]{2,1,0:T(8,128)S(1)}, f32[32,64,208]{2,1,0:T(8,128)}) fusion(f32[32,64,208]{2,1,0:T(8,128)S(1)} %copy-done.6, f32[64,208]{1,0:T(8,128)S(1)} %broadcast_multiply_fusion.1, f32[32,64,48]{2,1,0:T(8,128)S(1)} %fusion.15, f32[32,64,160]{2,1,0:T(8,128)S(1)} %copy-done.4, bf16[32,64,208]{2,1,0:T(8,128)(2,1)} %param.25), kind=kLoop, calls=%fused_computation.19 | loop fusion | flops 4259840 | bytes 7720960 | tf_op jit(solution)/shard_map/mul | solution.py:120
  89.1 0.1 slice.143
  89.2 4.5 %collective-permute-start.2 = (f32[32,48,208]{2,1,0:T(8,128)S(1)}, f32[32,48,208]{2,1,0:T(8,128)S(1)}, u32[]{:S(2)}, u32[]{:S(2)}) collective-permute-start(f32[32,48,208]{2,1,0:T(8,128)S(1)} %slice.143), channel_id=1, source_target_pairs={{0,2},{2,4},{4,6},{6,8},{8,10},{10,12},{12,14},{1,3},{3,5},{5,7},{... | collective-permute-start | bytes 3833864 | tf_op jit(solution)/shard_map/ppermute | solution.py:36
  93.8 31.6 %collective-permute-done.2 = f32[32,48,208]{2,1,0:T(8,128)S(1)} collective-permute-done((f32[32,48,208]{2,1,0:T(8,128)S(1)}, f32[32,48,208]{2,1,0:T(8,128)S(1)}, u32[]{:S(2)}, u32[]{:S(2)}) %collective-permute-start.2) | collective-permute-done | bytes 1277984 | tf_op jit(solution)/shard_map/ppermute | solution.py:36
  125.4 1.2 copy-done.5
  126.6 1.8 pad_maximum_fusion
  128.3 2.0 %copy.16 = f32[32,112,48]{1,2,0:T(8,128)S(1)} copy(f32[32,112,48]{2,1,0:T(8,128)} %pad_maximum_fusion) | data formatting | bytes 1376256 | tf_op jit(solution)/shard_map/slice | solution.py:123
  130.3 2.4 %collective-permute-start.3 = (f32[32,112,48]{1,2,0:T(8,128)S(1)}, f32[32,112,48]{1,2,0:T(8,128)}, u32[]{:S(2)}, u32[]{:S(2)}) collective-permute-start(f32[32,112,48]{1,2,0:T(8,128)S(1)} %copy.16), channel_id=1, source_target_pairs={{0,16},{1,17},{2,18},{3,19},{4,20},{5,21},{6,22},{7,23},{8,24},{9,... | collective-permute-start | bytes 2064392 | tf_op jit(solution)/shard_map/ppermute | solution.py:36
  132.7 13.5 %collective-permute-done.3 = f32[32,112,48]{1,2,0:T(8,128)} collective-permute-done((f32[32,112,48]{1,2,0:T(8,128)S(1)}, f32[32,112,48]{1,2,0:T(8,128)}, u32[]{:S(2)}, u32[]{:S(2)}) %collective-permute-start.3) | collective-permute-done | bytes 688160 | tf_op jit(solution)/shard_map/ppermute | solution.py:36
  146.2 2.9 %copy.17 = f32[32,112,48]{2,1,0:T(8,128)} copy(f32[32,112,48]{1,2,0:T(8,128)} %collective-permute-done.3) | data formatting | bytes 1376256 | tf_op jit(solution)/shard_map/ppermute | solution.py:36
  149.1 5.1 %fusion = f32[32,112,256]{2,1,0:T(8,128)S(1)} fusion(f32[256,256,1]{1,0,2:T(8,128)S(1)} %copy-done.7, f32[32,64,208]{2,1,0:T(8,128)S(1)} %get-tuple-element.68, f32[32,48,208]{2,1,0:T(8,128)} %copy-done.5, f32[32,112,48]{2,1,0:T(8,128)} %copy.17), kind=kOutput, calls=%fused_computation | convolution fusion | flops 2820407296 | bytes 7602176 | tf_op jit(solution)/shard_map/cxy,vy->cxv/dot_general | solution.py:61
  154.2 0.0 copy-start.12
  154.2 3.6 %convolution_bitcast_fusion = f32[32,112,256]{2,1,0:T(8,128)S(1)} fusion(f32[32,112,256]{2,1,0:T(8,128)S(1)} %fusion, f32[112,112,1]{1,0,2:T(8,128)S(1)} %copy-done.10), kind=kOutput, calls=%fused_computation.20 | convolution fusion | flops 1233125376 | bytes 7390208 | tf_op jit(solution)/shard_map/ux,cxv->cuv/dot_general | solution.py:64
  157.8 0.9 fusion.16
  158.7 0.9 fusion.13
  159.7 0.2 copy-done.1
  159.9 3.1 %multiply_reduce_fusion = (f32[112,256]{1,0:T(8,128)}, f32[32,112,256]{2,1,0:T(8,128)}) fusion(f32[32,112,256]{2,1,0:T(8,128)S(1)} %copy-done.1, f32[32,112,256]{2,1,0:T(8,128)S(1)} %fusion.13), kind=kLoop, calls=%fused_computation.8 | loop fusion | flops 2723840 | bytes 11124736 | tf_op jit(solution)/shard_map/reduce_sum | solution.py:126
  163.0 0.0 reduce-scatter.2.cloned.1.call-update
  163.0 10.1 %reduce-scatter.2.cloned.1.call-done = f32[56,256]{1,0:T(8,128)} async-done(((f32[112,256]{1,0:T(8,128)}), f32[56,256]{1,0:T(8,128)}) %reduce-scatter.2.cloned.1.call-update) | async-done | bytes 57360 | tf_op jit(solution)/shard_map/reduce_scatter | solution.py:127
  173.1 0.8 multiply_minimum_fusion
  173.9 1.9 %all_gather.3 = f32[112,256]{1,0:T(8,128)S(1)} all-gather(f32[56,256]{1,0:T(8,128)S(1)} %multiply_minimum_fusion), channel_id=1, replica_groups=mesh['fy'=2,'fx'=8,'ch'=2] {'ch'}, dimensions={0}, use_global_device_ids=true | all-gather | bytes 172032 | tf_op jit(solution)/shard_map/all_gather | solution.py:131
  175.8 4.1 %broadcast_multiply_fusion = f32[32,112,256]{2,1,0:T(8,128)} fusion(f32[32,112,256]{2,1,0:T(8,128)} %get-tuple-element.67, f32[112,256]{1,0:T(8,128)S(1)} %all_gather.3), kind=kLoop, calls=%fused_computation.22 | loop fusion | flops 917504 | bytes 7454720 | tf_op jit(solution)/shard_map/mul | solution.py:132
  (19 shorter events, 0.1 us)
Async XLA Ops:
  7.2 0.8 copy-start.11
  7.2 3.0 %copy-start.8 = (f32[128,128,1]{1,0,2:T(8,128)S(1)}, f32[128,128,1]{1,0,2:T(8,128)}, u32[]{:S(2)}) copy-start(f32[128,128,1]{1,0,2:T(8,128)} %constant.169) | copy-start | bytes 196612
  7.2 165.9 %reduce-scatter.2.cloned.1.call-start = ((), (), s32[]{:S(2)}) async-start(), calls=%async_computation.1 | async-start | bytes 172032 | tf_op jit(solution)/shard_map/reduce_scatter | solution.py:127
  7.2 2.0 %copy-start = (f32[32,112,256]{2,1,0:T(8,128)S(1)}, f32[32,112,256]{2,1,0:T(8,128)}, u32[]{:S(2)}) copy-start(f32[32,112,256]{2,1,0:T(8,128)} %param.26) | copy-start | bytes 11010052
  7.2 3.1 %copy-start.2 = (f32[32,112,256]{2,1,0:T(8,128)S(1)}, f32[32,112,256]{2,1,0:T(8,128)}, u32[]{:S(2)}) copy-start(f32[32,112,256]{2,1,0:T(8,128)} %param.26) | copy-start | bytes 11010052
  9.3 2.0 %copy-start.9 = (f32[112,112,1]{1,0,2:T(8,128)S(1)}, f32[112,112,1]{1,0,2:T(8,128)}, u32[]{:S(2)}) copy-start(f32[112,112,1]{1,0,2:T(8,128)} %constant.170) | copy-start | bytes 150532
  11.3 3.6 %copy-start.7 = (f32[256,256,1]{1,0,2:T(8,128)S(1)}, f32[256,256,1]{1,0,2:T(8,128)}, u32[]{:S(2)}) copy-start(f32[256,256,1]{1,0,2:T(8,128)} %constant.171) | copy-start | bytes 786436
  18.1 1.8 copy-start.3
  18.3 39.4 %collective-permute-start = (f32[32,48,256]{2,1,0:T(8,128)S(1)}, f32[32,48,256]{2,1,0:T(8,128)}, u32[]{:S(2)}, u32[]{:S(2)}) collective-permute-start(f32[32,48,256]{2,1,0:T(8,128)S(1)} %slice.138), channel_id=1, source_target_pairs={{2,0},{4,2},{6,4},{8,6},{10,8},{12,10},{14,12},{3,1},{5,3},{7,5},{... | collective-permute-start | bytes 4718600 | tf_op jit(solution)/shard_map/ppermute | solution.py:36
  61.1 20.9 %collective-permute-start.1 = (f32[32,64,48]{1,2,0:T(8,128)}, f32[32,64,48]{1,2,0:T(8,128)}, u32[]{:S(2)}, u32[]{:S(2)}) collective-permute-start(f32[32,64,48]{1,2,0:T(8,128)} %copy.14), channel_id=1, source_target_pairs={{16,0},{17,1},{18,2},{19,3},{20,4},{21,5},{22,6},{23,7},{24,8},{25... | collective-permute-start | bytes 1179656 | tf_op jit(solution)/shard_map/ppermute | solution.py:36
  83.5 1.6 copy-start.4
  83.5 2.2 %copy-start.6 = (f32[32,64,208]{2,1,0:T(8,128)S(1)}, f32[32,64,208]{2,1,0:T(8,128)}, u32[]{:S(2)}) copy-start(f32[32,64,208]{2,1,0:T(8,128)} %param.24) | copy-start | bytes 5111812
  89.2 36.2 %collective-permute-start.2 = (f32[32,48,208]{2,1,0:T(8,128)S(1)}, f32[32,48,208]{2,1,0:T(8,128)S(1)}, u32[]{:S(2)}, u32[]{:S(2)}) collective-permute-start(f32[32,48,208]{2,1,0:T(8,128)S(1)} %slice.143), channel_id=1, source_target_pairs={{0,2},{2,4},{4,6},{6,8},{8,10},{10,12},{12,14},{1,3},{3,5},{5,7},{... | collective-permute-start | bytes 3833864 | tf_op jit(solution)/shard_map/ppermute | solution.py:36
  125.4 1.2 copy-start.5
  130.3 15.8 %collective-permute-start.3 = (f32[32,112,48]{1,2,0:T(8,128)S(1)}, f32[32,112,48]{1,2,0:T(8,128)}, u32[]{:S(2)}, u32[]{:S(2)}) collective-permute-start(f32[32,112,48]{1,2,0:T(8,128)S(1)} %copy.16), channel_id=1, source_target_pairs={{0,16},{1,17},{2,18},{3,19},{4,20},{5,21},{6,22},{7,23},{8,24},{9,... | collective-permute-start | bytes 2064392 | tf_op jit(solution)/shard_map/ppermute | solution.py:36
  149.1 5.1 %copy-start.10 = (f32[112,112,1]{1,0,2:T(8,128)S(1)}, f32[112,112,1]{1,0,2:T(8,128)}, u32[]{:S(2)}) copy-start(f32[112,112,1]{1,0,2:T(8,128)} %constant.170) | copy-start | bytes 150532
  154.2 4.6 %copy-start.12 = (f32[56,56,1]{1,0,2:T(8,128)S(1)}, f32[56,56,1]{1,0,2:T(8,128)}, u32[]{:S(2)}) copy-start(f32[56,56,1]{1,0,2:T(8,128)} %constant.168) | copy-start | bytes 37636
  157.8 2.0 %copy-start.1 = (f32[32,112,256]{2,1,0:T(8,128)S(1)}, f32[32,112,256]{2,1,0:T(8,128)}, u32[]{:S(2)}) copy-start(f32[32,112,256]{2,1,0:T(8,128)} %param.26) | copy-start | bytes 11010052
  159.9 13.2 %copy-start.13 = (f32[112,256]{1,0:T(8,128)S(1)}, f32[112,256]{1,0:T(8,128)}, u32[]{:S(2)}) copy-start(f32[112,256]{1,0:T(8,128)} %param.27) | copy-start | bytes 344068
Sparse Core Ops, SparseCore 0:
  163.1 9.8 reduce-scatter.1
where the time goes:
time: 187 us
  waiting for transfers between devices  110 us (59%)
  matrix products  19.2 us (10%)
  other arithmetic  17.8 us (10%)
  between operations  14.3 us (8%)
  local copies, waits for them, and re-layouts  13.7 us (7%)
  starting transfers between devices  9.5 us (5%)
  blocking collectives  1.89 us (1%)
    ppermute x4, waiting for transfers between devices, passed_along(): return lax.ppermute(array, axis, pairs)  100 us
    reduce_scatter x1, waiting for transfers between devices, shards(): lax.psum_scatter(squared_sum, 'ch', scatter_dimension=0, tiled=True)  10.1 us
    ppermute x4, starting transfers between devices, passed_along(): return lax.ppermute(array, axis, pairs)  9.46 us
    dot_general x2, matrix products, analysis(): jnp.einsum('cxy,vy->cxv', corner_part, matrix_y, precision=lax.Precision....  5.96 us
    unnamed x28, local copies, waits for them, and re-layouts  5.86 us
    dot_general x2, matrix products, analysis(): jnp.einsum('ux,cxv->cuv', matrix_x, corner_part, precision=lax.Precision....  4.59 us
    dot_general x2, matrix products, synthesis(): jnp.einsum('ux,cuv->cxv', matrix_x, corner_part, precision=lax.Precision....  4.54 us
    ppermute x2, local copies, waits for them, and re-layouts, passed_along(): return lax.ppermute(array, axis, pairs)  4.38 us
  transfers between devices with their start and end apart: 5, of which 5 were waited for; matrix products, arithmetic and copies ran while one was open for 1% of the time, Pallas kernels for 0%

commit v1 on v0

v1 whole, which is shorter than its diff:
```python
import jax
import jax.numpy as jnp
import numpy as np
from jax import lax
from jax.sharding import PartitionSpec as P

LEVELS = 2


LOW_PASS = [
    -0.00011747678400228192,
    0.0006754494059985568,
    -0.0003917403729959771,
    -0.00487035299301066,
    0.008746094047015655,
    0.013981027917015516,
    -0.04408825393106472,
    -0.01736930100202211,
    0.128747426620186,
    0.00047248457399797254,
    -0.2840155429624281,
    -0.015829105256023893,
    0.5853546836548691,
    0.6756307362980128,
    0.3128715909144659,
    0.05441584224308161,
]
TAU_STEP = 0.5
LAMBDA_REG = 1.0
EPSILON = 1e-06


def passed_along(array, axis, by):
    length = lax.axis_size(axis)
    pairs = [(i, i + by) for i in range(length) if 0 <= i + by < length]
    return lax.ppermute(array, axis, pairs)


def level_matrix(length):
    halved = length // 2
    taps_count = len(LOW_PASS)
    matrix = np.zeros((length, length))
    for out_row in range(halved):
        for tap_index in range(taps_count):
            column = (2 * out_row + tap_index) % length
            matrix[out_row, column] += LOW_PASS[tap_index]
            matrix[halved + out_row, column] += (-1) ** tap_index * LOW_PASS[
                taps_count - 1 - tap_index
            ]
    return matrix


def level_einsum(spec, first, second):
    return jnp.einsum(spec, first, second, precision=lax.Precision.HIGH)


def analysis(facet_block, levels):
    result = facet_block
    width_x = facet_block.shape[1]
    width_y = facet_block.shape[2]
    for _ in range(levels):
        matrix_x = jnp.asarray(level_matrix(width_x), dtype=jnp.float32)
        matrix_y = jnp.asarray(level_matrix(width_y), dtype=jnp.float32)
        corner_part = result[:, :width_x, :width_y]
        corner_part = level_einsum("cxy,vy->cxv", corner_part, matrix_y)
        corner_part = level_einsum("ux,cxv->cuv", matrix_x, corner_part)
        result = result.at[:, :width_x, :width_y].set(corner_part)
        width_x = width_x // 2
        width_y = width_y // 2
    return result


def synthesis(coeff_block, levels):
    result = coeff_block
    for level_step in range(levels - 1, -1, -1):
        width_x = coeff_block.shape[1] // 2**level_step
        width_y = coeff_block.shape[2] // 2**level_step
        matrix_x = jnp.asarray(level_matrix(width_x), dtype=jnp.float32)
        matrix_y = jnp.asarray(level_matrix(width_y), dtype=jnp.float32)
        corner_part = result[:, :width_x, :width_y]
        corner_part = level_einsum("ux,cuv->cxv", matrix_x, corner_part)
        corner_part = level_einsum("cxv,vy->cxy", corner_part, matrix_y)
        result = result.at[:, :width_x, :width_y].set(corner_part)
    return result


def tile_weights(length, intersection, position_index, count):
    positions = jnp.arange(length, dtype=jnp.int32)
    edge = (positions >= length - intersection) & (position_index < count - 1)
    return jnp.where(edge, 0.5**0.5, 1.0).astype(jnp.float32)


def group_count(columns, rows):
    best = 1
    for groups in range(1, columns + 1):
        if columns % groups == 0 and (columns // groups) % 8 == 0:
            if padded_size(columns, rows, groups) < padded_size(columns, rows, best):
                best = groups
    return best


def padded_size(columns, rows, groups):
    return (columns // groups) * (-(-(rows * groups) // 128))


def pack(part):
    columns, rows = part.shape[1], part.shape[2]
    groups = group_count(columns, rows)
    step = columns // groups
    return jnp.concatenate([part[:, g * step : (g + 1) * step] for g in range(groups)], axis=2)


def unpack(packed, columns, rows):
    groups = group_count(columns, rows)
    return jnp.concatenate([packed[:, :, g * rows : (g + 1) * rows] for g in range(groups)], axis=1)


def shards(image_cube, data_grad, dual_coeffs, reweights):
    tile_x = image_cube.shape[1]
    tile_y = image_cube.shape[2]
    border = dual_coeffs.shape[1] - tile_x
    head = (tile_y - border) // 128 * 128
    tail = tile_y - head
    weight_map = (
        tile_weights(tile_x, border, lax.axis_index("fx"), lax.axis_size("fx"))[:, None]
        * tile_weights(tile_y, border, lax.axis_index("fy"), lax.axis_size("fy"))[None, :]
    )
    synthesized = synthesis(dual_coeffs, LEVELS)
    upper = jnp.swapaxes(synthesized[:, :, :border], 1, 2)
    from_below = passed_along(upper, "fy", -1)
    own_head = synthesized[:, :, border : border + head]
    from_right_head = passed_along(own_head[:, :border], "fx", -1)
    own_tail = synthesized[:, :, border + head :]
    from_below = jnp.swapaxes(from_below, 1, 2)
    own_tail = own_tail + jnp.pad(from_below, ((0, 0), (0, 0), (tail - border, 0)))
    from_right_tail = unpack(passed_along(pack(own_tail[:, :border]), "fx", -1), border, tail)

    def step(own, incoming, lo, hi):
        summed = own[:, border:] + jnp.pad(incoming, ((0, 0), (tile_x - border, 0), (0, 0)))
        weights = weight_map[:, lo:hi]
        cube = image_cube[:, :, lo:hi]
        grad = data_grad[:, :, lo:hi].astype(jnp.float32)
        image = jnp.maximum(cube - TAU_STEP * (grad + summed * weights), 0.0)
        return image, (2.0 * image - cube) * weights

    image_head, extrap_head = step(own_head, from_right_head, 0, head)
    image_tail, extrap_tail = step(own_tail, from_right_tail, head, tile_y)
    left_tail = unpack(passed_along(pack(extrap_tail[:, tile_x - border :]), "fx", 1), border, tail)
    left_head = passed_along(extrap_head[:, tile_x - border :], "fx", 1)
    rows_tail = jnp.concatenate([left_tail, extrap_tail], axis=1)
    lower = jnp.swapaxes(rows_tail[:, :, tail - border :], 1, 2)
    from_above = jnp.swapaxes(passed_along(lower, "fy", 1), 1, 2)
    rows_head = jnp.concatenate([left_head, extrap_head], axis=1)
    extended = jnp.concatenate([from_above, rows_head, rows_tail], axis=2)
    updated = dual_coeffs + analysis(extended, LEVELS)
    squared_sum = jnp.sum(updated * updated, axis=0)
    pairs = [(i, i ^ 1) for i in range(lax.axis_size("ch"))]
    totals = squared_sum + lax.ppermute(squared_sum, "ch", pairs)
    factor = jnp.minimum(1.0, LAMBDA_REG * reweights / jnp.sqrt(totals + EPSILON))
    image_next = jnp.concatenate([image_head, image_tail], axis=2)
    return (image_next, updated * factor[None])


def solution(mesh):
    return jax.shard_map(
        shards,
        mesh=mesh,
        in_specs=(P("ch", "fx", "fy"), P("ch", "fx", "fy"), P("ch", "fx", "fy"), P("fx", "fy")),
        out_specs=(P("ch", "fx", "fy"), P("ch", "fx", "fy")),
        check_vma=False,
    )
```

time: 187 us -> 124 us (0.66)
  the two profiles are of different devices: /device:TPU:0 before, /device:TPU:14 now
where the time goes in v1:
time: 124 us; the launch traced here: 123 us
  waiting for transfers between devices  61.4 us (50%)
  starting transfers between devices  17.8 us (14%)
  local copies, waits for them, and re-layouts  16.5 us (13%)
  other arithmetic  14.2 us (11%)
  matrix products  12.2 us (10%)
    ppermute x6, waiting for transfers between devices, passed_along(): return lax.ppermute(array, axis, pairs)  61.4 us
    ppermute x6, starting transfers between devices, passed_along(): return lax.ppermute(array, axis, pairs)  17.7 us
    dot_general x8, matrix products, level_einsum(): return jnp.einsum(spec, first, second, precision=lax.Precision.HIGH)  12.2 us
    unnamed x36, local copies, waits for them, and re-layouts  8.11 us
    mul x2, other arithmetic, step(): return (image, (2.0 * image - cube) * weights)  6.21 us
    slice x1, local copies, waits for them, and re-layouts, shards(): from_right_head = passed_along(own_head[:, :border], 'fx', -1)  2.58 us
    add x1, other arithmetic, shards(): own_tail + jnp.pad(from_below, ((0, 0), (0, 0), (tail - border, 0)))  2.51 us
  transfers between devices with their start and end apart: 7, of which 4 were waited for; matrix products, arithmetic and copies ran while one was open for 13% of the time, Pallas kernels for 0%

profile of v1, /device:TPU:14, one launch (start us, length us, event | category | flops | bytes accessed | tf_op | source)
XLA Modules:
  0.0 123.1 jit_solution(16583798901473515255)
XLA Ops:
  0.7 0.7 copy-done.15
  1.4 1.3 %copy-done.1 = f32[32,112,256]{2,1,0:T(8,128)S(1)} copy-done((f32[32,112,256]{2,1,0:T(8,128)S(1)}, f32[32,112,256]{2,1,0:T(8,128)}, u32[]{:S(2)}) %copy-start.1) | copy-done | bytes 3670040
  2.7 0.6 convolution_bitcast_fusion.2
  3.3 0.5 copy-done.3
  3.8 0.5 convolution_dynamic-update-slice_fusion
  4.4 1.8 %fusion.39 = f32[32,256,112]{1,2,0:T(8,128)S(1)} fusion(f32[32,112,256]{2,1,0:T(8,128)S(1)} %convolution_dynamic-update-slice_fusion, f32[112,112,1]{1,0,2:T(8,128)S(1)} %copy-done.14), kind=kOutput, calls=%fused_computation.61 | convolution fusion | flops 616562688 | bytes 7390208 | tf_op jit(solution)/shard_map/ux,cuv->cxv/dot_general | solution.py:54
  6.2 1.7 %fusion.14 = f32[32,112,256]{2,1,0:T(8,128)S(1)} fusion(f32[256,256,1]{1,0,2:T(8,128)S(1)} %copy-done.12, f32[32,256,112]{1,2,0:T(8,128)S(1)} %fusion.39), kind=kOutput, calls=%fused_computation.14 | convolution fusion | flops 1409286144 | bytes 7602176 | tf_op jit(solution)/shard_map/cxv,vy->cxy/dot_general | solution.py:54
  7.8 1.8 %copy-done = f32[32,112,256]{2,1,0:T(8,128)} copy-done((f32[32,112,256]{2,1,0:T(8,128)}, f32[32,112,256]{2,1,0:T(8,128)S(1)}, u32[]{:S(2)}) %copy-start) | copy-done | bytes 3670040
  9.7 0.1 slice_bitcast_fusion
  9.8 0.5 copy.14
  10.3 2.5 %collective-permute-start.1 = (f32[32,48,112]{2,1,0:T(8,128)S(1)}, f32[32,48,112]{2,1,0:T(8,128)S(1)}, u32[]{:S(2)}, u32[]{:S(2)}) collective-permute-start(f32[32,48,112]{2,1,0:T(8,128)S(1)} %copy.14), channel_id=1, source_target_pairs={{16,0},{17,1},{18,2},{19,3},{20,4},{21,5},{22,6},{23,7},{24,8},{25... | collective-permute-start | bytes 2064392 | tf_op jit(solution)/shard_map/ppermute | solution.py:36
  12.8 16.7 %collective-permute-done.1 = f32[32,48,112]{2,1,0:T(8,128)S(1)} collective-permute-done((f32[32,48,112]{2,1,0:T(8,128)S(1)}, f32[32,48,112]{2,1,0:T(8,128)S(1)}, u32[]{:S(2)}, u32[]{:S(2)}) %collective-permute-start.1) | collective-permute-done | bytes 688160 | tf_op jit(solution)/shard_map/ppermute | solution.py:36
  29.5 0.5 copy.15
  30.1 2.5 %slice_add_fusion = f32[32,112,80]{2,1,0:T(8,128)S(1)} fusion(f32[32,112,256]{2,1,0:T(8,128)} %copy-done, f32[32,112,48]{2,1,0:T(8,128)S(1)} %bitcast.34), kind=kLoop, calls=%fused_computation.24 | loop fusion | flops 286720 | bytes 2981888 | tf_op jit(solution)/shard_map/add | solution.py:135
  32.6 1.2 copy-done.4
  33.9 0.3 pad_maximum_fusion.4
  34.2 2.5 %collective-permute-start.2 = (f32[32,16,240]{2,1,0:T(8,128)S(1)}, f32[32,16,240]{2,1,0:T(8,128)S(1)}, u32[]{:S(2)}, u32[]{:S(2)}) collective-permute-start(f32[32,16,240]{2,1,0:T(8,128)S(1)} %pad_maximum_fusion.4), channel_id=1, source_target_pairs={{2,0},{4,2},{6,4},{8,6},{10,8},{12,10},{14,12},{3,1},{5,3},{7,5},{... | collective-permute-start | bytes 1474568 | tf_op jit(solution)/shard_map/ppermute | solution.py:36
  36.7 2.6 %slice.210 = f32[32,48,128]{2,1,0:T(8,128)} slice(f32[32,112,256]{2,1,0:T(8,128)} %copy-done), slice={[0:32], [0:48], [48:176]} | slice | bytes 1572864 | tf_op jit(solution)/shard_map/slice | solution.py:132
  39.3 3.3 %collective-permute-start = (f32[32,48,128]{2,1,0:T(8,128)}, f32[32,48,128]{2,1,0:T(8,128)}, u32[]{:S(2)}, u32[]{:S(2)}) collective-permute-start(f32[32,48,128]{2,1,0:T(8,128)} %slice.210), channel_id=1, source_target_pairs={{2,0},{4,2},{6,4},{8,6},{10,8},{12,10},{14,12},{3,1},{5,3},{7,5},{... | collective-permute-start | bytes 2359304 | tf_op jit(solution)/shard_map/ppermute | solution.py:36
  42.7 0.1 broadcast_multiply_fusion.1
  42.7 9.1 %collective-permute-done.2 = f32[32,16,240]{2,1,0:T(8,128)S(1)} collective-permute-done((f32[32,16,240]{2,1,0:T(8,128)S(1)}, f32[32,16,240]{2,1,0:T(8,128)S(1)}, u32[]{:S(2)}, u32[]{:S(2)}) %collective-permute-start.2) | collective-permute-done | bytes 491552 | tf_op jit(solution)/shard_map/ppermute | solution.py:36
  51.9 0.2 fusion.38
  52.1 2.9 %subtract_multiply_fusion.1 = (f32[32,64,80]{2,1,0:T(8,128)S(1)}, f32[32,64,80]{2,1,0:T(8,128)}) fusion(f32[32,64,208]{2,1,0:T(8,128)} %param.24, f32[64,80]{1,0:T(8,128)S(1)} %slice.221, f32[32,16,80]{2,1,0:T(8,128)S(1)} %get-tuple-element.82, f32[32,16,80]{2,1,0:T(8,128)S(1)} %get-tuple-element.83, f32[32,16,80]{2,1,0:T(8,128)S(1)} %get-tuple-element.81, ...), kind=kLoop, calls=%fused_computation.46 | loop fusion | flops 2621440 | bytes 3461120 | tf_op jit(solution)/shard_map/mul | solution.py:144
  55.0 0.1 fusion.36
  55.1 0.3 pad_maximum_fusion.5
  55.3 2.5 %collective-permute-start.3 = (f32[32,16,240]{2,1,0:T(8,128)S(1)}, f32[32,16,240]{2,1,0:T(8,128)S(1)}, u32[]{:S(2)}, u32[]{:S(2)}) collective-permute-start(f32[32,16,240]{2,1,0:T(8,128)S(1)} %pad_maximum_fusion.5), channel_id=1, source_target_pairs={{0,2},{2,4},{4,6},{6,8},{8,10},{10,12},{12,14},{1,3},{3,5},{5,7},{... | collective-permute-start | bytes 1474568 | tf_op jit(solution)/shard_map/ppermute | solution.py:36
  57.9 17.3 %collective-permute-done = f32[32,48,128]{2,1,0:T(8,128)} collective-permute-done((f32[32,48,128]{2,1,0:T(8,128)}, f32[32,48,128]{2,1,0:T(8,128)}, u32[]{:S(2)}, u32[]{:S(2)}) %collective-permute-start) | collective-permute-done | bytes 786464 | tf_op jit(solution)/shard_map/ppermute | solution.py:36
  75.2 3.3 %subtract_multiply_fusion = (f32[32,64,128]{2,1,0:T(8,128)S(1)}, f32[32,64,128]{2,1,0:T(8,128)}) fusion(f32[32,64,208]{2,1,0:T(8,128)S(1)} %copy-done.9, f32[64,128]{1,0:T(8,128)S(1)} %slice.211, f32[32,48,128]{2,1,0:T(8,128)} %collective-permute-done, f32[32,112,256]{2,1,0:T(8,128)} %copy-done, bf16[32,64,208]{2,1,0:T(8,128)(2,1)S(1)} %copy-done.11), kind=kLoop, calls=%fused_computation.45 | loop fusion | flops 2621440 | bytes 5537792 | tf_op jit(solution)/shard_map/mul | solution.py:144
  78.6 1.0 slice.228
  79.6 5.4 %collective-permute-start.5 = (f32[32,48,128]{2,1,0:T(8,128)}, f32[32,48,128]{2,1,0:T(8,128)}, u32[]{:S(2)}, u32[]{:S(2)}) collective-permute-start(f32[32,48,128]{2,1,0:T(8,128)} %slice.228), channel_id=1, source_target_pairs={{0,2},{2,4},{4,6},{6,8},{8,10},{10,12},{12,14},{1,3},{3,5},{5,7},{... | collective-permute-start | bytes 2359304 | tf_op jit(solution)/shard_map/ppermute | solution.py:36
  85.0 0.2 fusion.37
  85.2 0.7 copy-done.10
  85.9 0.5 fusion.16
  86.5 1.4 %copy.16 = f32[32,48,112]{2,1,0:T(8,128)} copy(f32[32,48,112]{1,2,0:T(8,128)S(1)} %fusion.16) | data formatting | bytes 1376256 | tf_op jit(solution)/shard_map/transpose | solution.py:151
  87.9 1.5 %collective-permute-start.4 = (f32[32,48,112]{2,1,0:T(8,128)}, f32[32,48,112]{2,1,0:T(8,128)}, u32[]{:S(2)}, u32[]{:S(2)}) collective-permute-start(f32[32,48,112]{2,1,0:T(8,128)} %copy.16), channel_id=1, source_target_pairs={{0,16},{1,17},{2,18},{3,19},{4,20},{5,21},{6,22},{7,23},{8,24},{9,... | collective-permute-start | bytes 2064392 | tf_op jit(solution)/shard_map/ppermute | solution.py:36
  89.3 18.1 %collective-permute-done.4 = f32[32,48,112]{2,1,0:T(8,128)} collective-permute-done((f32[32,48,112]{2,1,0:T(8,128)}, f32[32,48,112]{2,1,0:T(8,128)}, u32[]{:S(2)}, u32[]{:S(2)}) %collective-permute-start.4) | collective-permute-done | bytes 688160 | tf_op jit(solution)/shard_map/ppermute | solution.py:36
  107.5 1.7 %copy.17 = f32[32,48,112]{1,2,0:T(8,128)S(1)} copy(f32[32,48,112]{2,1,0:T(8,128)} %collective-permute-done.4) | data formatting | bytes 1376256 | tf_op jit(solution)/shard_map/ppermute | solution.py:36
  109.2 5.0 %fusion = f32[32,112,256]{2,1,0:T(8,128)S(1)} fusion(f32[256,256,1]{1,0,2:T(8,128)} %constant.175, f32[32,64,80]{2,1,0:T(8,128)S(1)} %get-tuple-element.70, f32[32,16,80]{2,1,0:T(8,128)S(1)} %get-tuple-element.79, f32[32,16,80]{2,1,0:T(8,128)} %copy-done.10, f32[32,16,80]{2,1,0:T(8,128)S(1)} %get-tuple-element.78, f32[32,64,128]{2,1,0:T(8,128)} %copy-done.8, ...), kind=kOutput, calls=%fused_computation | convolution fusion | flops 1414791168 | bytes 7602176 | tf_op jit(solution)/shard_map/cxy,vy->cxv/dot_general | solution.py:54
  114.1 1.7 %convolution_bitcast_fusion = f32[32,112,256]{2,1,0:T(8,128)S(1)} fusion(f32[32,112,256]{2,1,0:T(8,128)S(1)} %fusion, f32[112,112,1]{1,0,2:T(8,128)S(1)} %copy-done.14), kind=kOutput, calls=%fused_computation.18 | convolution fusion | flops 616562688 | bytes 7390208 | tf_op jit(solution)/shard_map/ux,cxv->cuv/dot_general | solution.py:54
  115.9 0.5 fusion.29
  116.4 0.5 fusion.17
  117.0 1.0 copy-done.2
  117.9 0.7 multiply_reduce_fusion
  118.6 0.1 collective-permute-start.6
  118.7 0.5 copy-done.6
  119.1 0.3 copy-done.7
  119.5 1.5 %pad_maximum_fusion = f32[32,64,208]{2,1,0:T(8,128)} fusion(f32[32,64,80]{2,1,0:T(8,128)S(1)} %copy-done.6, f32[32,64,128]{2,1,0:T(8,128)S(1)} %copy-done.7), kind=kLoop, calls=%fused_computation.17 | loop fusion | flops 425984 | bytes 3407872 | tf_op jit(solution)/shard_map/concatenate | solution.py:160
  121.0 2.1 %broadcast_multiply_fusion = f32[32,112,256]{2,1,0:T(8,128)} fusion(f32[32,112,256]{2,1,0:T(8,128)S(1)} %get-tuple-element.67, f32[112,256]{1,0:T(8,128)S(1)} %multiply_minimum_fusion), kind=kLoop, calls=%fused_computation.25 | loop fusion | flops 917504 | bytes 7454720 | tf_op jit(solution)/shard_map/mul | solution.py:161
  (36 shorter events, 0.2 us)
Async XLA Ops:
  0.6 0.8 copy-start.15
  0.6 2.7 %copy-start.13 = (f32[128,128,1]{1,0,2:T(8,128)S(1)}, f32[128,128,1]{1,0,2:T(8,128)}, u32[]{:S(2)}) copy-start(f32[128,128,1]{1,0,2:T(8,128)} %constant.173) | copy-start | bytes 196612
  0.7 2.1 %copy-start.1 = (f32[32,112,256]{2,1,0:T(8,128)S(1)}, f32[32,112,256]{2,1,0:T(8,128)}, u32[]{:S(2)}) copy-start(f32[32,112,256]{2,1,0:T(8,128)} %param.26) | copy-start | bytes 11010052
  0.7 3.2 %copy-start.3 = (f32[32,112,256]{2,1,0:T(8,128)S(1)}, f32[32,112,256]{2,1,0:T(8,128)}, u32[]{:S(2)}) copy-start(f32[32,112,256]{2,1,0:T(8,128)} %param.26) | copy-start | bytes 11010052
  2.7 1.6 %copy-start.14 = (f32[112,112,1]{1,0,2:T(8,128)S(1)}, f32[112,112,1]{1,0,2:T(8,128)}, u32[]{:S(2)}) copy-start(f32[112,112,1]{1,0,2:T(8,128)} %constant.174) | copy-start | bytes 150532
  4.4 1.8 %copy-start.12 = (f32[256,256,1]{1,0,2:T(8,128)S(1)}, f32[256,256,1]{1,0,2:T(8,128)}, u32[]{:S(2)}) copy-start(f32[256,256,1]{1,0,2:T(8,128)} %constant.175) | copy-start | bytes 786436
  7.8 1.8 %copy-start = (f32[32,112,256]{2,1,0:T(8,128)}, f32[32,112,256]{2,1,0:T(8,128)S(1)}, u32[]{:S(2)}) copy-start(f32[32,112,256]{2,1,0:T(8,128)S(1)} %fusion.14) | copy-start | bytes 11010052
  10.3 19.2 %collective-permute-start.1 = (f32[32,48,112]{2,1,0:T(8,128)S(1)}, f32[32,48,112]{2,1,0:T(8,128)S(1)}, u32[]{:S(2)}, u32[]{:S(2)}) collective-permute-start(f32[32,48,112]{2,1,0:T(8,128)S(1)} %copy.14), channel_id=1, source_target_pairs={{16,0},{17,1},{18,2},{19,3},{20,4},{21,5},{22,6},{23,7},{24,8},{25... | collective-permute-start | bytes 2064392 | tf_op jit(solution)/shard_map/ppermute | solution.py:36
  32.6 1.2 copy-start.4
  33.9 18.2 %copy-start.5 = (f32[32,112,80]{2,1,0:T(8,128)S(1)}, f32[32,112,80]{2,1,0:T(8,128)}, u32[]{:S(2)}) copy-start(f32[32,112,80]{2,1,0:T(8,128)} %copy-done.4) | copy-start | bytes 3440644
  34.2 17.7 %collective-permute-start.2 = (f32[32,16,240]{2,1,0:T(8,128)S(1)}, f32[32,16,240]{2,1,0:T(8,128)S(1)}, u32[]{:S(2)}, u32[]{:S(2)}) collective-permute-start(f32[32,16,240]{2,1,0:T(8,128)S(1)} %pad_maximum_fusion.4), channel_id=1, source_target_pairs={{2,0},{4,2},{6,4},{8,6},{10,8},{12,10},{14,12},{3,1},{5,3},{7,5},{... | collective-permute-start | bytes 1474568 | tf_op jit(solution)/shard_map/ppermute | solution.py:36
  39.3 35.9 %collective-permute-start = (f32[32,48,128]{2,1,0:T(8,128)}, f32[32,48,128]{2,1,0:T(8,128)}, u32[]{:S(2)}, u32[]{:S(2)}) collective-permute-start(f32[32,48,128]{2,1,0:T(8,128)} %slice.210), channel_id=1, source_target_pairs={{2,0},{4,2},{6,4},{8,6},{10,8},{12,10},{14,12},{3,1},{5,3},{7,5},{... | collective-permute-start | bytes 2359304 | tf_op jit(solution)/shard_map/ppermute | solution.py:36
  52.1 23.1 %copy-start.9 = (f32[32,64,208]{2,1,0:T(8,128)S(1)}, f32[32,64,208]{2,1,0:T(8,128)}, u32[]{:S(2)}) copy-start(f32[32,64,208]{2,1,0:T(8,128)} %param.24) | copy-start | bytes 5111812
  52.1 23.1 %copy-start.11 = (bf16[32,64,208]{2,1,0:T(8,128)(2,1)S(1)}, bf16[32,64,208]{2,1,0:T(8,128)(2,1)}, u32[]{:S(2)}) copy-start(bf16[32,64,208]{2,1,0:T(8,128)(2,1)} %param.25) | copy-start | bytes 2555908
  55.3 29.7 %collective-permute-start.3 = (f32[32,16,240]{2,1,0:T(8,128)S(1)}, f32[32,16,240]{2,1,0:T(8,128)S(1)}, u32[]{:S(2)}, u32[]{:S(2)}) collective-permute-start(f32[32,16,240]{2,1,0:T(8,128)S(1)} %pad_maximum_fusion.5), channel_id=1, source_target_pairs={{0,2},{2,4},{4,6},{6,8},{8,10},{10,12},{12,14},{1,3},{3,5},{5,7},{... | collective-permute-start | bytes 1474568 | tf_op jit(solution)/shard_map/ppermute | solution.py:36
  78.6 6.7 %copy-start.8 = (f32[32,64,128]{2,1,0:T(8,128)}, f32[32,64,128]{2,1,0:T(8,128)S(1)}, u32[]{:S(2)}) copy-start(f32[32,64,128]{2,1,0:T(8,128)S(1)} %get-tuple-element.68) | copy-start | bytes 3145732
  79.6 29.6 %collective-permute-start.5 = (f32[32,48,128]{2,1,0:T(8,128)}, f32[32,48,128]{2,1,0:T(8,128)}, u32[]{:S(2)}, u32[]{:S(2)}) collective-permute-start(f32[32,48,128]{2,1,0:T(8,128)} %slice.228), channel_id=1, source_target_pairs={{0,2},{2,4},{4,6},{6,8},{8,10},{10,12},{12,14},{1,3},{3,5},{5,7},{... | collective-permute-start | bytes 2359304 | tf_op jit(solution)/shard_map/ppermute | solution.py:36
  85.2 0.7 copy-start.10
  87.9 19.6 %collective-permute-start.4 = (f32[32,48,112]{2,1,0:T(8,128)}, f32[32,48,112]{2,1,0:T(8,128)}, u32[]{:S(2)}, u32[]{:S(2)}) collective-permute-start(f32[32,48,112]{2,1,0:T(8,128)} %copy.16), channel_id=1, source_target_pairs={{0,16},{1,17},{2,18},{3,19},{4,20},{5,21},{6,22},{7,23},{8,24},{9,... | collective-permute-start | bytes 2064392 | tf_op jit(solution)/shard_map/ppermute | solution.py:36
  114.1 2.3 %copy-start.16 = (f32[56,56,1]{1,0,2:T(8,128)S(1)}, f32[56,56,1]{1,0,2:T(8,128)}, u32[]{:S(2)}) copy-start(f32[56,56,1]{1,0,2:T(8,128)} %constant.172) | copy-start | bytes 37636
  115.9 2.0 %copy-start.2 = (f32[32,112,256]{2,1,0:T(8,128)S(1)}, f32[32,112,256]{2,1,0:T(8,128)}, u32[]{:S(2)}) copy-start(f32[32,112,256]{2,1,0:T(8,128)} %param.26) | copy-start | bytes 11010052
  117.9 1.2 copy-start.6
  117.9 1.5 %copy-start.7 = (f32[32,64,128]{2,1,0:T(8,128)S(1)}, f32[32,64,128]{2,1,0:T(8,128)}, u32[]{:S(2)}) copy-start(f32[32,64,128]{2,1,0:T(8,128)} %get-tuple-element.69) | copy-start | bytes 3145732
  118.6 2.4 %copy-start.17 = (f32[112,256]{1,0:T(8,128)S(1)}, f32[112,256]{1,0:T(8,128)}, u32[]{:S(2)}) copy-start(f32[112,256]{1,0:T(8,128)} %param.27) | copy-start | bytes 344068
  118.6 2.4 %collective-permute-start.6 = (f32[112,256]{1,0:T(8,128)S(1)}, f32[112,256]{1,0:T(8,128)S(1)}, u32[]{:S(2)}, u32[]{:S(2)}) collective-permute-start(f32[112,256]{1,0:T(8,128)S(1)} %get-tuple-element.66), channel_id=1, source_target_pairs={{0,1},{1,0},{2,3},{3,2},{4,5},{5,4},{6,7},{7,6},{8,9},{9,8},{10,11... | collective-permute-start | bytes 344072 | tf_op jit(solution)/shard_map/ppermute | solution.py:158

commit v2 on v1

--- a/solution.py
+++ b/solution.py
@@ -5,6 +5,7 @@
 from jax.sharding import PartitionSpec as P
 
 LEVELS = 2
+CHUNKS = 2
 
 
 LOW_PASS = [
@@ -116,6 +117,7 @@
 
 
 def shards(image_cube, data_grad, dual_coeffs, reweights):
+    channels = image_cube.shape[0]
     tile_x = image_cube.shape[1]
     tile_y = image_cube.shape[2]
     border = dual_coeffs.shape[1] - tile_x
@@ -125,40 +127,48 @@
         tile_weights(tile_x, border, lax.axis_index("fx"), lax.axis_size("fx"))[:, None]
         * tile_weights(tile_y, border, lax.axis_index("fy"), lax.axis_size("fy"))[None, :]
     )
-    synthesized = synthesis(dual_coeffs, LEVELS)
-    upper = jnp.swapaxes(synthesized[:, :, :border], 1, 2)
-    from_below = passed_along(upper, "fy", -1)
-    own_head = synthesized[:, :, border : border + head]
-    from_right_head = passed_along(own_head[:, :border], "fx", -1)
-    own_tail = synthesized[:, :, border + head :]
-    from_below = jnp.swapaxes(from_below, 1, 2)
-    own_tail = own_tail + jnp.pad(from_below, ((0, 0), (0, 0), (tail - border, 0)))
-    from_right_tail = unpack(passed_along(pack(own_tail[:, :border]), "fx", -1), border, tail)
+    group = channels // CHUNKS
 
-    def step(own, incoming, lo, hi):
+    def step(own, incoming, held, chunk, lo, hi):
         summed = own[:, border:] + jnp.pad(incoming, ((0, 0), (tile_x - border, 0), (0, 0)))
-        weights = weight_map[:, lo:hi]
-        cube = image_cube[:, :, lo:hi]
-        grad = data_grad[:, :, lo:hi].astype(jnp.float32)
+        weights = held[2][:, lo:hi]
+        cube = held[0][chunk, :, lo:hi]
+        grad = held[1][chunk, :, lo:hi].astype(jnp.float32)
         image = jnp.maximum(cube - TAU_STEP * (grad + summed * weights), 0.0)
         return image, (2.0 * image - cube) * weights
 
-    image_head, extrap_head = step(own_head, from_right_head, 0, head)
-    image_tail, extrap_tail = step(own_tail, from_right_tail, head, tile_y)
-    left_tail = unpack(passed_along(pack(extrap_tail[:, tile_x - border :]), "fx", 1), border, tail)
-    left_head = passed_along(extrap_head[:, tile_x - border :], "fx", 1)
-    rows_tail = jnp.concatenate([left_tail, extrap_tail], axis=1)
-    lower = jnp.swapaxes(rows_tail[:, :, tail - border :], 1, 2)
-    from_above = jnp.swapaxes(passed_along(lower, "fy", 1), 1, 2)
-    rows_head = jnp.concatenate([left_head, extrap_head], axis=1)
-    extended = jnp.concatenate([from_above, rows_head, rows_tail], axis=2)
-    updated = dual_coeffs + analysis(extended, LEVELS)
+    images = []
+    updates = []
+    for n in range(CHUNKS):
+        chunk = slice(n * group, (n + 1) * group)
+        held = lax.optimization_barrier((image_cube, data_grad, weight_map, dual_coeffs))
+        synthesized = synthesis(held[3][chunk], LEVELS)
+        own_head = synthesized[:, :, border : border + head]
+        from_right_head = passed_along(own_head[:, :border], "fx", -1)
+        upper = jnp.swapaxes(synthesized[:, :, :border], 1, 2)
+        from_below = jnp.swapaxes(passed_along(upper, "fy", -1), 1, 2)
+        own_tail = synthesized[:, :, border + head :]
+        own_tail = own_tail + jnp.pad(from_below, ((0, 0), (0, 0), (tail - border, 0)))
+        packed = passed_along(pack(own_tail[:, :border]), "fx", -1)
+        from_right_tail = unpack(packed, border, tail)
+        image_head, extrap_head = step(own_head, from_right_head, held, chunk, 0, head)
+        image_tail, extrap_tail = step(own_tail, from_right_tail, held, chunk, head, tile_y)
+        packed = passed_along(pack(extrap_tail[:, tile_x - border :]), "fx", 1)
+        left_tail = unpack(packed, border, tail)
+        left_head = passed_along(extrap_head[:, tile_x - border :], "fx", 1)
+        rows_tail = jnp.concatenate([left_tail, extrap_tail], axis=1)
+        lower = jnp.swapaxes(rows_tail[:, :, tail - border :], 1, 2)
+        from_above = jnp.swapaxes(passed_along(lower, "fy", 1), 1, 2)
+        rows_head = jnp.concatenate([left_head, extrap_head], axis=1)
+        extended = jnp.concatenate([from_above, rows_head, rows_tail], axis=2)
+        updates.append(analysis(extended, LEVELS))
+        images.append(jnp.concatenate([image_head, image_tail], axis=2))
+    updated = dual_coeffs + jnp.concatenate(updates, axis=0)
     squared_sum = jnp.sum(updated * updated, axis=0)
     pairs = [(i, i ^ 1) for i in range(lax.axis_size("ch"))]
     totals = squared_sum + lax.ppermute(squared_sum, "ch", pairs)
     factor = jnp.minimum(1.0, LAMBDA_REG * reweights / jnp.sqrt(totals + EPSILON))
-    image_next = jnp.concatenate([image_head, image_tail], axis=2)
-    return (image_next, updated * factor[None])
+    return (jnp.concatenate(images, axis=0), updated * factor[None])
 
 
 def solution(mesh):

time: 124 us -> 121 us (0.976)
  the two profiles are of different devices: /device:TPU:14 before, /device:TPU:11 now
where the time goes in v2:
time: 121 us; the launch traced here: 120 us
  starting transfers between devices  33.1 us (27%)
  waiting for transfers between devices  30 us (25%)
  local copies, waits for them, and re-layouts  22.1 us (18%)
  matrix products  20.3 us (17%)
  other arithmetic  13.2 us (11%)
  between operations  1.34 us (1%)
    ppermute x12, waiting for transfers between devices, passed_along(): return lax.ppermute(array, axis, pairs)  30 us
    ppermute x12, starting transfers between devices, passed_along(): return lax.ppermute(array, axis, pairs)  27.7 us
    dot_general x16, matrix products, level_einsum(): return jnp.einsum(spec, first, second, precision=lax.Precision.HIGH)  20.3 us
    ppermute x4, local copies, waits for them, and re-layouts, passed_along(): return lax.ppermute(array, axis, pairs)  6.11 us
    ppermute x1, starting transfers between devices, shards(): totals = squared_sum + lax.ppermute(squared_sum, 'ch', pairs)  5.4 us
    slice x1, local copies, waits for them, and re-layouts, shards(): synthesized = synthesis(held[3][chunk], LEVELS)  3.57 us
    mul x2, other arithmetic, step(): return (image, (2.0 * image - cube) * weights)  3.31 us
    unnamed x58, local copies, waits for them, and re-layouts  2.68 us
  transfers between devices with their start and end apart: 13, of which 6 were waited for; matrix products, arithmetic and copies ran while one was open for 30% of the time, Pallas kernels for 0%

profile of v2, /device:TPU:11, one launch (start us, length us, event | category | flops | bytes accessed | tf_op | source)
XLA Modules:
  0.0 119.9 jit_solution(12012083943292792731)
XLA Ops:
  0.8 3.6 %fusion.70 = (f32[16,112,256]{2,1,0:T(8,128)}, f32[16,112,256]{2,1,0:T(8,128)S(1)}) fusion(f32[32,112,256]{2,1,0:T(8,128)} %param.46), kind=kLoop, calls=%fused_computation.107 | loop fusion | bytes 7340032 | tf_op jit(solution)/shard_map/slice | solution.py:145
  4.3 2.0 %convolution_bitcast_fusion.2 = f32[16,56,128]{1,2,0:T(8,128)S(1)} fusion(f32[56,56,1]{1,0,2:T(8,128)S(1)} %copy-done.25, f32[32,112,256]{2,1,0:T(8,128)} %param.46), kind=kOutput, calls=%fused_computation.38 | convolution fusion | flops 38535168 | bytes 930048 | tf_op jit(solution)/shard_map/ux,cuv->cxv/dot_general | solution.py:55
  6.4 1.0 convolution_dynamic-update-slice_fusion
  7.4 0.9 fusion.80
  8.3 0.9 fusion.28
  9.3 1.0 copy.24
  10.4 2.9 %collective-permute-start.4 = (f32[16,48,112]{2,1,0:T(8,128)}, f32[16,48,112]{2,1,0:T(8,128)}, u32[]{:S(2)}, u32[]{:S(2)}) collective-permute-start(f32[16,48,112]{2,1,0:T(8,128)} %copy.24), channel_id=1, source_target_pairs={{16,0},{17,1},{18,2},{19,3},{20,4},{21,5},{22,6},{23,7},{24,8},{25... | collective-permute-start | bytes 1032200 | tf_op jit(solution)/shard_map/ppermute | solution.py:37
  13.3 2.0 %convolution_bitcast_fusion.3 = f32[16,56,128]{1,2,0:T(8,128)S(1)} fusion(f32[56,56,1]{1,0,2:T(8,128)S(1)} %copy-done.25, f32[32,112,256]{2,1,0:T(8,128)} %param.46), kind=kOutput, calls=%fused_computation.39 | convolution fusion | flops 38535168 | bytes 930048 | tf_op jit(solution)/shard_map/ux,cuv->cxv/dot_general | solution.py:55
  15.3 1.8 %convolution_dynamic-update-slice_fusion.1 = f32[16,112,256]{2,1,0:T(8,128)} fusion(f32[16,112,256]{2,1,0:T(8,128)} %get-tuple-element.146, f32[16,56,128]{1,2,0:T(8,128)S(1)} %convolution_bitcast_fusion.3, f32[128,128,1]{1,0,2:T(8,128)S(1)} %copy-done.10), kind=kOutput, calls=%fused_computation.41 | convolution fusion | flops 88080384 | bytes 983040 | tf_op jit(solution)/shard_map/cxv,vy->cxy/dot_general | solution.py:55
  17.1 2.4 %fusion.79 = f32[16,256,112]{1,2,0:T(8,128)S(1)} fusion(f32[16,112,256]{2,1,0:T(8,128)} %convolution_dynamic-update-slice_fusion.1, f32[112,112,1]{1,0,2:T(8,128)S(1)} %copy-done.14), kind=kOutput, calls=%fused_computation.116 | convolution fusion | flops 308281344 | bytes 3720192 | tf_op jit(solution)/shard_map/ux,cuv->cxv/dot_general | solution.py:55
  19.5 0.9 fusion.30
  20.6 3.0 %collective-permute-start = (f32[16,48,128]{2,1,0:T(8,128)S(1)}, f32[16,48,128]{2,1,0:T(8,128)}, u32[]{:S(2)}, u32[]{:S(2)}) collective-permute-start(f32[16,48,128]{2,1,0:T(8,128)S(1)} %slice.425), channel_id=1, source_target_pairs={{2,0},{4,2},{6,4},{8,6},{10,8},{12,10},{14,12},{3,1},{5,3},{7,5},{... | collective-permute-start | bytes 1179656 | tf_op jit(solution)/shard_map/ppermute | solution.py:37
  23.6 0.9 slice.436
  24.6 1.9 %collective-permute-start.3 = (f32[16,48,128]{2,1,0:T(8,128)}, f32[16,48,128]{2,1,0:T(8,128)}, u32[]{:S(2)}, u32[]{:S(2)}) collective-permute-start(f32[16,48,128]{2,1,0:T(8,128)} %slice.436), channel_id=1, source_target_pairs={{2,0},{4,2},{6,4},{8,6},{10,8},{12,10},{14,12},{3,1},{5,3},{7,5},{... | collective-permute-start | bytes 1179656 | tf_op jit(solution)/shard_map/ppermute | solution.py:37
  26.6 1.0 copy.22
  27.6 2.1 %collective-permute-start.1 = (f32[16,48,112]{2,1,0:T(8,128)}, f32[16,48,112]{2,1,0:T(8,128)}, u32[]{:S(2)}, u32[]{:S(2)}) collective-permute-start(f32[16,48,112]{2,1,0:T(8,128)} %copy.22), channel_id=1, source_target_pairs={{16,0},{17,1},{18,2},{19,3},{20,4},{21,5},{22,6},{23,7},{24,8},{25... | collective-permute-start | bytes 1032200 | tf_op jit(solution)/shard_map/ppermute | solution.py:37
  29.7 1.3 %copy.25 = f32[16,48,112]{1,2,0:T(8,128)S(1)} copy(f32[16,48,112]{2,1,0:T(8,128)} %collective-permute-done.4) | data formatting | bytes 688128 | tf_op jit(solution)/shard_map/ppermute | solution.py:37
  31.6 1.0 pad_maximum_fusion.7
  32.5 1.9 %collective-permute-start.5 = (f32[16,16,240]{2,1,0:T(8,128)}, f32[16,16,240]{2,1,0:T(8,128)}, u32[]{:S(2)}, u32[]{:S(2)}) collective-permute-start(f32[16,16,240]{2,1,0:T(8,128)} %pad_maximum_fusion.7), channel_id=1, source_target_pairs={{2,0},{4,2},{6,4},{8,6},{10,8},{12,10},{14,12},{3,1},{5,3},{7,5},{... | collective-permute-start | bytes 737288 | tf_op jit(solution)/shard_map/ppermute | solution.py:37
  34.4 2.3 %collective-permute-done.1 = f32[16,48,112]{2,1,0:T(8,128)} collective-permute-done((f32[16,48,112]{2,1,0:T(8,128)}, f32[16,48,112]{2,1,0:T(8,128)}, u32[]{:S(2)}, u32[]{:S(2)}) %collective-permute-start.1) | collective-permute-done | bytes 344096 | tf_op jit(solution)/shard_map/ppermute | solution.py:37
  36.7 1.3 %copy.23 = f32[16,48,112]{1,2,0:T(8,128)S(1)} copy(f32[16,48,112]{2,1,0:T(8,128)} %collective-permute-done.1) | data formatting | bytes 688128 | tf_op jit(solution)/shard_map/ppermute | solution.py:37
  38.0 1.9 %slice_add_fusion.1 = f32[16,112,80]{2,1,0:T(8,128)S(1)} fusion(f32[16,112,256]{2,1,0:T(8,128)} %copy-done.1, f32[16,112,48]{2,1,0:T(8,128)S(1)} %bitcast.63), kind=kLoop, calls=%fused_computation.57 | loop fusion | flops 143360 | bytes 1490944 | tf_op jit(solution)/shard_map/add | solution.py:151
  40.1 2.2 %collective-permute-start.2 = (f32[16,16,240]{2,1,0:T(8,128)S(1)}, f32[16,16,240]{2,1,0:T(8,128)S(1)}, u32[]{:S(2)}, u32[]{:S(2)}) collective-permute-start(f32[16,16,240]{2,1,0:T(8,128)S(1)} %pad_maximum_fusion.6), channel_id=1, source_target_pairs={{2,0},{4,2},{6,4},{8,6},{10,8},{12,10},{14,12},{3,1},{5,3},{7,5},{... | collective-permute-start | bytes 737288 | tf_op jit(solution)/shard_map/ppermute | solution.py:37
  42.4 1.9 %subtract_multiply_fusion.2 = (f32[16,64,128]{2,1,0:T(8,128)S(1)}, f32[16,64,128]{2,1,0:T(8,128)S(1)}, f32[16,64,128]{2,1,0:T(8,128)S(1)}, f32[16,64,128]{2,1,0:T(8,128)S(1)}) fusion(f32[32,64,208]{2,1,0:T(8,128)S(1)} %copy-done.4, f32[64,128]{1,0:T(8,128)S(1)} %slice-done.1, f32[16,48,128]{2,1,0:T(8,128)} %collective-permute-done, ...), kind=kLoop, calls=%fused_computation.89 | loop fusion | flops 2621440 | bytes 5537792 | tf_op jit(solution)/shard_map/mul | solution.py:138
  45.9 3.1 %collective-permute-start.11 = (f32[16,48,128]{2,1,0:T(8,128)}, f32[16,48,128]{2,1,0:T(8,128)}, u32[]{:S(2)}, u32[]{:S(2)}) collective-permute-start(f32[16,48,128]{2,1,0:T(8,128)} %slice.460), channel_id=1, source_target_pairs={{0,2},{2,4},{4,6},{6,8},{8,10},{10,12},{12,14},{1,3},{3,5},{5,7},{... | collective-permute-start | bytes 1179656 | tf_op jit(solution)/shard_map/ppermute | solution.py:37
  49.0 4.2 %collective-permute-start.8 = (f32[16,48,128]{2,1,0:T(8,128)}, f32[16,48,128]{2,1,0:T(8,128)}, u32[]{:S(2)}, u32[]{:S(2)}) collective-permute-start(f32[16,48,128]{2,1,0:T(8,128)} %slice.452), channel_id=1, source_target_pairs={{0,2},{2,4},{4,6},{6,8},{8,10},{10,12},{12,14},{1,3},{3,5},{5,7},{... | collective-permute-start | bytes 1179656 | tf_op jit(solution)/shard_map/ppermute | solution.py:37
  53.2 1.2 %fusion.78 = (f32[16,16,80]{2,1,0:T(8,128)S(1)}, f32[16,16,80]{2,1,0:T(8,128)S(1)}, f32[16,16,80]{2,1,0:T(8,128)S(1)}) fusion(f32[16,16,240]{2,1,0:T(8,128)} %collective-permute-done.5), kind=kLoop, calls=%fused_computation.115 | loop fusion | bytes 491520 | tf_op jit(solution)/shard_map/slice | solution.py:116
  54.4 14.3 %collective-permute-done.2 = f32[16,16,240]{2,1,0:T(8,128)S(1)} collective-permute-done((f32[16,16,240]{2,1,0:T(8,128)S(1)}, f32[16,16,240]{2,1,0:T(8,128)S(1)}, u32[]{:S(2)}, u32[]{:S(2)}) %collective-permute-start.2) | collective-permute-done | bytes 245792 | tf_op jit(solution)/shard_map/ppermute | solution.py:37
  68.9 1.4 %subtract_multiply_fusion.3 = (f32[16,64,80]{2,1,0:T(8,128)S(1)}, f32[16,64,80]{2,1,0:T(8,128)}, f32[16,64,80]{2,1,0:T(8,128)S(1)}, f32[16,64,80]{2,1,0:T(8,128)}) fusion(f32[32,64,208]{2,1,0:T(8,128)S(1)} %copy-done.4, f32[64,80]{1,0:T(8,128)S(1)} %slice-done, f32[16,16,80]{2,1,0:T(8,128)S(1)} %get-tuple-element.171, ...), kind=kLoop, calls=%fused_computation.90 | loop fusion | flops 2539520 | bytes 3461120 | tf_op jit(solution)/shard_map/mul | solution.py:138
  70.5 1.9 %collective-permute-start.9 = (f32[16,16,240]{2,1,0:T(8,128)S(1)}, f32[16,16,240]{2,1,0:T(8,128)S(1)}, u32[]{:S(2)}, u32[]{:S(2)}) collective-permute-start(f32[16,16,240]{2,1,0:T(8,128)S(1)} %pad_maximum_fusion.9), channel_id=1, source_target_pairs={{0,2},{2,4},{4,6},{6,8},{8,10},{10,12},{12,14},{1,3},{3,5},{5,7},{... | collective-permute-start | bytes 737288 | tf_op jit(solution)/shard_map/ppermute | solution.py:37
  72.4 0.9 pad_maximum_fusion.8
  73.3 1.9 %collective-permute-start.6 = (f32[16,16,240]{2,1,0:T(8,128)}, f32[16,16,240]{2,1,0:T(8,128)}, u32[]{:S(2)}, u32[]{:S(2)}) collective-permute-start(f32[16,16,240]{2,1,0:T(8,128)} %pad_maximum_fusion.8), channel_id=1, source_target_pairs={{0,2},{2,4},{4,6},{6,8},{8,10},{10,12},{12,14},{1,3},{3,5},{5,7},{... | collective-permute-start | bytes 737288 | tf_op jit(solution)/shard_map/ppermute | solution.py:37
  75.2 4.1 %collective-permute-done.9 = f32[16,16,240]{2,1,0:T(8,128)S(1)} collective-permute-done((f32[16,16,240]{2,1,0:T(8,128)S(1)}, f32[16,16,240]{2,1,0:T(8,128)S(1)}, u32[]{:S(2)}, u32[]{:S(2)}) %collective-permute-start.9) | collective-permute-done | bytes 245792 | tf_op jit(solution)/shard_map/ppermute | solution.py:37
  80.5 1.0 copy.28
  81.6 1.3 %collective-permute-start.10 = (f32[16,48,112]{2,1,0:T(8,128)}, f32[16,48,112]{2,1,0:T(8,128)}, u32[]{:S(2)}, u32[]{:S(2)}) collective-permute-start(f32[16,48,112]{2,1,0:T(8,128)} %copy.28), channel_id=1, source_target_pairs={{0,16},{1,17},{2,18},{3,19},{4,20},{5,21},{6,22},{7,23},{8,24},{9,... | collective-permute-start | bytes 1032200 | tf_op jit(solution)/shard_map/ppermute | solution.py:37
  82.8 2.2 %collective-permute-done.6 = f32[16,16,240]{2,1,0:T(8,128)} collective-permute-done((f32[16,16,240]{2,1,0:T(8,128)}, f32[16,16,240]{2,1,0:T(8,128)}, u32[]{:S(2)}, u32[]{:S(2)}) %collective-permute-start.6) | collective-permute-done | bytes 245792 | tf_op jit(solution)/shard_map/ppermute | solution.py:37
  85.0 1.2 %fusion.75 = (f32[16,16,80]{2,1,0:T(8,128)S(1)}, f32[16,16,80]{2,1,0:T(8,128)S(1)}, f32[16,16,80]{2,1,0:T(8,128)S(1)}) fusion(f32[16,16,240]{2,1,0:T(8,128)} %collective-permute-done.6), kind=kLoop, calls=%fused_computation.112 | loop fusion | bytes 491520 | tf_op jit(solution)/shard_map/slice | solution.py:116
  87.3 1.0 copy.26
  88.4 1.3 %collective-permute-start.7 = (f32[16,48,112]{2,1,0:T(8,128)}, f32[16,48,112]{2,1,0:T(8,128)}, u32[]{:S(2)}, u32[]{:S(2)}) collective-permute-start(f32[16,48,112]{2,1,0:T(8,128)} %copy.26), channel_id=1, source_target_pairs={{0,16},{1,17},{2,18},{3,19},{4,20},{5,21},{6,22},{7,23},{8,24},{9,... | collective-permute-start | bytes 1032200 | tf_op jit(solution)/shard_map/ppermute | solution.py:37
  90.4 1.3 %copy.29 = f32[16,48,112]{1,2,0:T(8,128)S(1)} copy(f32[16,48,112]{2,1,0:T(8,128)} %collective-permute-done.10) | data formatting | bytes 688128 | tf_op jit(solution)/shard_map/ppermute | solution.py:37
  91.7 2.7 %fusion.14 = f32[16,112,256]{2,1,0:T(8,128)S(1)} fusion(f32[256,256,1]{1,0,2:T(8,128)} %constant.285, f32[16,64,80]{2,1,0:T(8,128)S(1)} %get-tuple-element.150, f32[16,16,80]{2,1,0:T(8,128)} %copy-done.23, f32[16,16,80]{2,1,0:T(8,128)} %copy-done.24, f32[16,16,80]{2,1,0:T(8,128)} %copy-done.22, f32[16,64,128]{2,1,0:T(8,128)S(1)} %get-tuple-element.148, ...), kind=kOutput, calls=%fused_computation.17 | convolution fusion | flops 707395584 | bytes 3932160 | tf_op jit(solution)/shard_map/cxy,vy->cxv/dot_general | solution.py:55
  95.3 6.4 %collective-permute-done.7 = f32[16,48,112]{2,1,0:T(8,128)} collective-permute-done((f32[16,48,112]{2,1,0:T(8,128)}, f32[16,48,112]{2,1,0:T(8,128)}, u32[]{:S(2)}, u32[]{:S(2)}) %collective-permute-start.7) | collective-permute-done | bytes 344096 | tf_op jit(solution)/shard_map/ppermute | solution.py:37
  101.7 2.2 %copy.27 = f32[16,48,112]{1,2,0:T(8,128)} copy(f32[16,48,112]{2,1,0:T(8,128)} %collective-permute-done.7) | data formatting | bytes 688128 | tf_op jit(solution)/shard_map/ppermute | solution.py:37
  105.3 2.5 %fusion = f32[16,112,256]{2,1,0:T(8,128)S(1)} fusion(f32[256,256,1]{1,0,2:T(8,128)S(1)} %copy-done.13, f32[16,64,80]{2,1,0:T(8,128)S(1)} %get-tuple-element.140, f32[16,16,80]{2,1,0:T(8,128)} %copy-done.20, f32[16,16,80]{2,1,0:T(8,128)} %copy-done.21, f32[16,16,80]{2,1,0:T(8,128)S(1)} %copy-done.19, f32[16,64,128]{2,1,0:T(8,128)S(1)} %copy-done.8, ...), kind=kOutput, calls=%fused_computation.3 | convolution fusion | flops 707395584 | bytes 3932160 | tf_op jit(solution)/shard_map/cxy,vy->cxv/dot_general | solution.py:55
  107.9 0.9 convolution_bitcast_fusion.1
  110.6 5.4 %collective-permute-start.12 = (f32[112,256]{1,0:T(8,128)S(1)}, f32[112,256]{1,0:T(8,128)S(1)}, u32[]{:S(2)}, u32[]{:S(2)}) collective-permute-start(f32[112,256]{1,0:T(8,128)S(1)} %multiply_reduce_fusion), channel_id=1, source_target_pairs={{0,1},{1,0},{2,3},{3,2},{4,5},{5,4},{6,7},{7,6},{8,9},{9,8},{10,11... | collective-permute-start | bytes 344072 | tf_op jit(solution)/shard_map/ppermute | solution.py:169
  116.0 1.5 %maximum_maximum_fusion = f32[32,64,208]{2,1,0:T(8,128)} fusion(f32[16,64,80]{2,1,0:T(8,128)S(1)} %copy-done.6, f32[16,64,128]{2,1,0:T(8,128)S(1)} %get-tuple-element.149, f32[16,64,80]{2,1,0:T(8,128)S(1)} %copy-done.5, f32[16,64,128]{2,1,0:T(8,128)S(1)} %get-tuple-element.139), kind=kLoop, calls=%fused_computation.2 | loop fusion | flops 1277952 | bytes 3407872 | tf_op jit(solution)/shard_map/concatenate | solution.py:171
  117.5 2.4 %broadcast_multiply_fusion = f32[32,112,256]{2,1,0:T(8,128)} fusion(f32[112,256]{1,0:T(8,128)S(1)} %multiply_minimum_fusion, f32[32,112,256]{2,1,0:T(8,128)S(1)} %copy-done, f32[16,112,256]{2,1,0:T(8,128)S(1)} %fusion.32, f32[16,112,256]{2,1,0:T(8,128)S(1)} %fusion.33), kind=kLoop, calls=%fused_computation.35 | loop fusion | flops 2752512 | bytes 11124736 | tf_op jit(solution)/shard_map/mul | solution.py:171
  (96 shorter events, 10.2 us)
Async XLA Ops:
  0.7 28.9 %copy-start.27 = (f32[64,208]{1,0:T(8,128)}, f32[64,208]{1,0:T(8,128)S(1)}, u32[]{:S(2)}) copy-start(f32[64,208]{1,0:T(8,128)S(1)} %broadcast_multiply_fusion.1) | copy-start | bytes 159748
  0.7 3.6 %copy-start.25 = (f32[56,56,1]{1,0,2:T(8,128)S(1)}, f32[56,56,1]{1,0,2:T(8,128)}, u32[]{:S(2)}) copy-start(f32[56,56,1]{1,0,2:T(8,128)} %constant.282) | copy-start | bytes 37636
  0.8 5.6 %copy-start.10 = (f32[128,128,1]{1,0,2:T(8,128)S(1)}, f32[128,128,1]{1,0,2:T(8,128)}, u32[]{:S(2)}) copy-start(f32[128,128,1]{1,0,2:T(8,128)} %constant.283) | copy-start | bytes 196612
  4.3 3.0 %copy-start.14 = (f32[112,112,1]{1,0,2:T(8,128)S(1)}, f32[112,112,1]{1,0,2:T(8,128)}, u32[]{:S(2)}) copy-start(f32[112,112,1]{1,0,2:T(8,128)} %constant.284) | copy-start | bytes 150532
  7.4 1.0 copy-start.12
  10.4 19.3 %collective-permute-start.4 = (f32[16,48,112]{2,1,0:T(8,128)}, f32[16,48,112]{2,1,0:T(8,128)}, u32[]{:S(2)}, u32[]{:S(2)}) collective-permute-start(f32[16,48,112]{2,1,0:T(8,128)} %copy.24), channel_id=1, source_target_pairs={{16,0},{17,1},{18,2},{19,3},{20,4},{21,5},{22,6},{23,7},{24,8},{25... | collective-permute-start | bytes 1032200 | tf_op jit(solution)/shard_map/ppermute | solution.py:37
  20.4 6.1 %copy-start.1 = (f32[16,112,256]{2,1,0:T(8,128)}, f32[16,112,256]{2,1,0:T(8,128)S(1)}, u32[]{:S(2)}) copy-start(f32[16,112,256]{2,1,0:T(8,128)S(1)} %fusion.30) | copy-start | bytes 5505028
  20.6 21.7 %collective-permute-start = (f32[16,48,128]{2,1,0:T(8,128)S(1)}, f32[16,48,128]{2,1,0:T(8,128)}, u32[]{:S(2)}, u32[]{:S(2)}) collective-permute-start(f32[16,48,128]{2,1,0:T(8,128)S(1)} %slice.425), channel_id=1, source_target_pairs={{2,0},{4,2},{6,4},{8,6},{10,8},{12,10},{14,12},{3,1},{5,3},{7,5},{... | collective-permute-start | bytes 1179656 | tf_op jit(solution)/shard_map/ppermute | solution.py:37
  24.6 17.8 %collective-permute-start.3 = (f32[16,48,128]{2,1,0:T(8,128)}, f32[16,48,128]{2,1,0:T(8,128)}, u32[]{:S(2)}, u32[]{:S(2)}) collective-permute-start(f32[16,48,128]{2,1,0:T(8,128)} %slice.436), channel_id=1, source_target_pairs={{2,0},{4,2},{6,4},{8,6},{10,8},{12,10},{14,12},{3,1},{5,3},{7,5},{... | collective-permute-start | bytes 1179656 | tf_op jit(solution)/shard_map/ppermute | solution.py:37
  27.6 9.1 %collective-permute-start.1 = (f32[16,48,112]{2,1,0:T(8,128)}, f32[16,48,112]{2,1,0:T(8,128)}, u32[]{:S(2)}, u32[]{:S(2)}) collective-permute-start(f32[16,48,112]{2,1,0:T(8,128)} %copy.22), channel_id=1, source_target_pairs={{16,0},{17,1},{18,2},{19,3},{20,4},{21,5},{22,6},{23,7},{24,8},{25... | collective-permute-start | bytes 1032200 | tf_op jit(solution)/shard_map/ppermute | solution.py:37
  31.5 2.9 %copy-start.2 = (f32[16,112,80]{2,1,0:T(8,128)}, f32[16,112,80]{2,1,0:T(8,128)S(1)}, u32[]{:S(2)}) copy-start(f32[16,112,80]{2,1,0:T(8,128)S(1)} %slice_add_fusion) | copy-start | bytes 1720324
  32.5 20.6 %collective-permute-start.5 = (f32[16,16,240]{2,1,0:T(8,128)}, f32[16,16,240]{2,1,0:T(8,128)}, u32[]{:S(2)}, u32[]{:S(2)}) collective-permute-start(f32[16,16,240]{2,1,0:T(8,128)} %pad_maximum_fusion.7), channel_id=1, source_target_pairs={{2,0},{4,2},{6,4},{8,6},{10,8},{12,10},{14,12},{3,1},{5,3},{7,5},{... | collective-permute-start | bytes 737288 | tf_op jit(solution)/shard_map/ppermute | solution.py:37
  38.0 4.4 %copy-start.4 = (f32[32,64,208]{2,1,0:T(8,128)S(1)}, f32[32,64,208]{2,1,0:T(8,128)}, u32[]{:S(2)}) copy-start(f32[32,64,208]{2,1,0:T(8,128)} %param.44) | copy-start | bytes 5111812
  38.0 4.4 %copy-start.9 = (bf16[32,64,208]{2,1,0:T(8,128)(2,1)S(1)}, bf16[32,64,208]{2,1,0:T(8,128)(2,1)}, u32[]{:S(2)}) copy-start(bf16[32,64,208]{2,1,0:T(8,128)(2,1)} %param.45) | copy-start | bytes 2555908
  38.0 4.4 %slice-start.1 = ((f32[64,208]{1,0:T(8,128)}), f32[64,128]{1,0:T(8,128)S(1)}, s32[]{:S(2)}) async-start(f32[64,208]{1,0:T(8,128)} %copy-done.27), calls=%async_computation.1 | async-start | bytes 65536 | tf_op jit(solution)/shard_map/slice | solution.py:134
  40.1 28.6 %collective-permute-start.2 = (f32[16,16,240]{2,1,0:T(8,128)S(1)}, f32[16,16,240]{2,1,0:T(8,128)S(1)}, u32[]{:S(2)}, u32[]{:S(2)}) collective-permute-start(f32[16,16,240]{2,1,0:T(8,128)S(1)} %pad_maximum_fusion.6), channel_id=1, source_target_pairs={{2,0},{4,2},{6,4},{8,6},{10,8},{12,10},{14,12},{3,1},{5,3},{7,5},{... | collective-permute-start | bytes 737288 | tf_op jit(solution)/shard_map/ppermute | solution.py:37
  44.3 24.5 %copy-start.7 = (f32[16,64,128]{2,1,0:T(8,128)}, f32[16,64,128]{2,1,0:T(8,128)S(1)}, u32[]{:S(2)}) copy-start(f32[16,64,128]{2,1,0:T(8,128)S(1)} %get-tuple-element.138) | copy-start | bytes 1572868
  44.3 24.5 %copy-start.3 = (f32[16,112,80]{2,1,0:T(8,128)S(1)}, f32[16,112,80]{2,1,0:T(8,128)}, u32[]{:S(2)}) copy-start(f32[16,112,80]{2,1,0:T(8,128)} %copy-done.2) | copy-start | bytes 1720324
  44.3 24.5 %slice-start = ((f32[64,208]{1,0:T(8,128)}), f32[64,80]{1,0:T(8,128)S(1)}, s32[]{:S(2)}) async-start(f32[64,208]{1,0:T(8,128)} %copy-done.27), calls=%async_computation | async-start | bytes 65536 | tf_op jit(solution)/shard_map/slice | solution.py:134
  45.9 45.8 %collective-permute-start.11 = (f32[16,48,128]{2,1,0:T(8,128)}, f32[16,48,128]{2,1,0:T(8,128)}, u32[]{:S(2)}, u32[]{:S(2)}) collective-permute-start(f32[16,48,128]{2,1,0:T(8,128)} %slice.460), channel_id=1, source_target_pairs={{0,2},{2,4},{4,6},{6,8},{8,10},{10,12},{12,14},{1,3},{3,5},{5,7},{... | collective-permute-start | bytes 1179656 | tf_op jit(solution)/shard_map/ppermute | solution.py:37
  49.0 55.7 %collective-permute-start.8 = (f32[16,48,128]{2,1,0:T(8,128)}, f32[16,48,128]{2,1,0:T(8,128)}, u32[]{:S(2)}, u32[]{:S(2)}) collective-permute-start(f32[16,48,128]{2,1,0:T(8,128)} %slice.452), channel_id=1, source_target_pairs={{0,2},{2,4},{4,6},{6,8},{8,10},{10,12},{12,14},{1,3},{3,5},{5,7},{... | collective-permute-start | bytes 1179656 | tf_op jit(solution)/shard_map/ppermute | solution.py:37
  70.5 8.9 %collective-permute-start.9 = (f32[16,16,240]{2,1,0:T(8,128)S(1)}, f32[16,16,240]{2,1,0:T(8,128)S(1)}, u32[]{:S(2)}, u32[]{:S(2)}) collective-permute-start(f32[16,16,240]{2,1,0:T(8,128)S(1)} %pad_maximum_fusion.9), channel_id=1, source_target_pairs={{0,2},{2,4},{4,6},{6,8},{8,10},{10,12},{12,14},{1,3},{3,5},{5,7},{... | collective-permute-start | bytes 737288 | tf_op jit(solution)/shard_map/ppermute | solution.py:37
  73.3 11.7 %collective-permute-start.6 = (f32[16,16,240]{2,1,0:T(8,128)}, f32[16,16,240]{2,1,0:T(8,128)}, u32[]{:S(2)}, u32[]{:S(2)}) collective-permute-start(f32[16,16,240]{2,1,0:T(8,128)} %pad_maximum_fusion.8), channel_id=1, source_target_pairs={{0,2},{2,4},{4,6},{6,8},{8,10},{10,12},{12,14},{1,3},{3,5},{5,7},{... | collective-permute-start | bytes 737288 | tf_op jit(solution)/shard_map/ppermute | solution.py:37
  79.4 0.7 copy-start.22
  79.5 0.7 copy-start.23
  79.5 0.8 copy-start.24
  81.6 8.8 %collective-permute-start.10 = (f32[16,48,112]{2,1,0:T(8,128)}, f32[16,48,112]{2,1,0:T(8,128)}, u32[]{:S(2)}, u32[]{:S(2)}) collective-permute-start(f32[16,48,112]{2,1,0:T(8,128)} %copy.28), channel_id=1, source_target_pairs={{0,16},{1,17},{2,18},{3,19},{4,20},{5,21},{6,22},{7,23},{8,24},{9,... | collective-permute-start | bytes 1032200 | tf_op jit(solution)/shard_map/ppermute | solution.py:37
  86.3 0.7 copy-start.18
  86.3 0.7 copy-start.20
  86.3 0.8 copy-start.21
  88.4 13.3 %collective-permute-start.7 = (f32[16,48,112]{2,1,0:T(8,128)}, f32[16,48,112]{2,1,0:T(8,128)}, u32[]{:S(2)}, u32[]{:S(2)}) collective-permute-start(f32[16,48,112]{2,1,0:T(8,128)} %copy.26), channel_id=1, source_target_pairs={{0,16},{1,17},{2,18},{3,19},{4,20},{5,21},{6,22},{7,23},{8,24},{9,... | collective-permute-start | bytes 1032200 | tf_op jit(solution)/shard_map/ppermute | solution.py:37
  91.7 2.7 %copy-start.15 = (f32[112,112,1]{1,0,2:T(8,128)S(1)}, f32[112,112,1]{1,0,2:T(8,128)}, u32[]{:S(2)}) copy-start(f32[112,112,1]{1,0,2:T(8,128)} %constant.284) | copy-start | bytes 150532
  94.4 9.5 %copy-start.11 = (f32[128,128,1]{1,0,2:T(8,128)S(1)}, f32[128,128,1]{1,0,2:T(8,128)}, u32[]{:S(2)}) copy-start(f32[128,128,1]{1,0,2:T(8,128)} %constant.283) | copy-start | bytes 196612
  95.3 9.0 %copy-start.26 = (f32[56,56,1]{1,0,2:T(8,128)S(1)}, f32[56,56,1]{1,0,2:T(8,128)}, u32[]{:S(2)}) copy-start(f32[56,56,1]{1,0,2:T(8,128)} %constant.282) | copy-start | bytes 37636
  103.9 1.0 copy-start.8
  103.9 1.1 copy-start.13
  103.9 1.4 %copy-start.17 = (f32[16,48,112]{1,2,0:T(8,128)S(1)}, f32[16,48,112]{1,2,0:T(8,128)}, u32[]{:S(2)}) copy-start(f32[16,48,112]{1,2,0:T(8,128)} %copy.27) | copy-start | bytes 1032196
  103.9 1.4 %copy-start.19 = (f32[16,16,80]{2,1,0:T(8,128)S(1)}, f32[16,16,80]{2,1,0:T(8,128)}, u32[]{:S(2)}) copy-start(f32[16,16,80]{2,1,0:T(8,128)} %copy-done.18) | copy-start | bytes 245764
  105.3 2.5 %copy-start.16 = (f32[112,112,1]{1,0,2:T(8,128)S(1)}, f32[112,112,1]{1,0,2:T(8,128)}, u32[]{:S(2)}) copy-start(f32[112,112,1]{1,0,2:T(8,128)} %constant.284) | copy-start | bytes 150532
  107.9 2.0 %copy-start = (f32[32,112,256]{2,1,0:T(8,128)S(1)}, f32[32,112,256]{2,1,0:T(8,128)}, u32[]{:S(2)}) copy-start(f32[32,112,256]{2,1,0:T(8,128)} %param.46) | copy-start | bytes 11010052
  109.9 6.1 %copy-start.5 = (f32[16,64,80]{2,1,0:T(8,128)S(1)}, f32[16,64,80]{2,1,0:T(8,128)}, u32[]{:S(2)}) copy-start(f32[16,64,80]{2,1,0:T(8,128)} %get-tuple-element.141) | copy-start | bytes 983044
  109.9 6.1 %copy-start.6 = (f32[16,64,80]{2,1,0:T(8,128)S(1)}, f32[16,64,80]{2,1,0:T(8,128)}, u32[]{:S(2)}) copy-start(f32[16,64,80]{2,1,0:T(8,128)} %get-tuple-element.151) | copy-start | bytes 983044
  110.6 6.9 %collective-permute-start.12 = (f32[112,256]{1,0:T(8,128)S(1)}, f32[112,256]{1,0:T(8,128)S(1)}, u32[]{:S(2)}, u32[]{:S(2)}) collective-permute-start(f32[112,256]{1,0:T(8,128)S(1)} %multiply_reduce_fusion), channel_id=1, source_target_pairs={{0,1},{1,0},{2,3},{3,2},{4,5},{5,4},{6,7},{7,6},{8,9},{9,8},{10,11... | collective-permute-start | bytes 344072 | tf_op jit(solution)/shard_map/ppermute | solution.py:169
  116.0 1.5 %copy-start.28 = (f32[112,256]{1,0:T(8,128)S(1)}, f32[112,256]{1,0:T(8,128)}, u32[]{:S(2)}) copy-start(f32[112,256]{1,0:T(8,128)} %param.47) | copy-start | bytes 344068

commit v3 on v1

--- a/solution.py
+++ b/solution.py
@@ -54,11 +54,10 @@
     return jnp.einsum(spec, first, second, precision=lax.Precision.HIGH)
 
 
-def analysis(facet_block, levels):
-    result = facet_block
-    width_x = facet_block.shape[1]
-    width_y = facet_block.shape[2]
-    for _ in range(levels):
+def refine(result, levels):
+    width_x = result.shape[1] // 2
+    width_y = result.shape[2] // 2
+    for _ in range(1, levels):
         matrix_x = jnp.asarray(level_matrix(width_x), dtype=jnp.float32)
         matrix_y = jnp.asarray(level_matrix(width_y), dtype=jnp.float32)
         corner_part = result[:, :width_x, :width_y]
@@ -115,6 +114,16 @@
     return jnp.concatenate([packed[:, :, g * rows : (g + 1) * rows] for g in range(groups)], axis=1)
 
 
+def after(array, earlier):
+    array, _ = lax.optimization_barrier((array, earlier))
+    return array
+
+
+def sent_packed(part, axis, by):
+    columns, rows = part.shape[1], part.shape[2]
+    return passed_along(pack(part), axis, by), columns, rows
+
+
 def shards(image_cube, data_grad, dual_coeffs, reweights):
     tile_x = image_cube.shape[1]
     tile_y = image_cube.shape[2]
@@ -126,38 +135,51 @@
         * tile_weights(tile_y, border, lax.axis_index("fy"), lax.axis_size("fy"))[None, :]
     )
     synthesized = synthesis(dual_coeffs, LEVELS)
-    upper = jnp.swapaxes(synthesized[:, :, :border], 1, 2)
-    from_below = passed_along(upper, "fy", -1)
     own_head = synthesized[:, :, border : border + head]
     from_right_head = passed_along(own_head[:, :border], "fx", -1)
-    own_tail = synthesized[:, :, border + head :]
-    from_below = jnp.swapaxes(from_below, 1, 2)
-    own_tail = own_tail + jnp.pad(from_below, ((0, 0), (0, 0), (tail - border, 0)))
-    from_right_tail = unpack(passed_along(pack(own_tail[:, :border]), "fx", -1), border, tail)
+    corner = sent_packed(synthesized[:, :border, :border], "fy", -1)
+    rest = sent_packed(synthesized[:, border:, :border], "fy", -1)
+
+    def with_rows(own, incoming):
+        return own + jnp.pad(incoming, ((0, 0), (0, 0), (tail - border, 0)))
+
+    edge_tail = with_rows(synthesized[:, :border, border + head :], unpack(*corner))
+    packed_tail = sent_packed(edge_tail, "fx", -1)
 
     def step(own, incoming, lo, hi):
-        summed = own[:, border:] + jnp.pad(incoming, ((0, 0), (tile_x - border, 0), (0, 0)))
+        summed = own + jnp.pad(incoming, ((0, 0), (tile_x - border, 0), (0, 0)))
         weights = weight_map[:, lo:hi]
         cube = image_cube[:, :, lo:hi]
         grad = data_grad[:, :, lo:hi].astype(jnp.float32)
         image = jnp.maximum(cube - TAU_STEP * (grad + summed * weights), 0.0)
         return image, (2.0 * image - cube) * weights
 
-    image_head, extrap_head = step(own_head, from_right_head, 0, head)
+    image_head, extrap_head = step(own_head[:, border:], from_right_head, 0, head)
+    edge_head = extrap_head[:, tile_x - border :]
+    own_tail = with_rows(synthesized[:, border:, border + head :], unpack(*rest))
+    from_right_tail = unpack(after(packed_tail[0], (edge_head, own_tail)), border, tail)
     image_tail, extrap_tail = step(own_tail, from_right_tail, head, tile_y)
-    left_tail = unpack(passed_along(pack(extrap_tail[:, tile_x - border :]), "fx", 1), border, tail)
-    left_head = passed_along(extrap_head[:, tile_x - border :], "fx", 1)
-    rows_tail = jnp.concatenate([left_tail, extrap_tail], axis=1)
-    lower = jnp.swapaxes(rows_tail[:, :, tail - border :], 1, 2)
-    from_above = jnp.swapaxes(passed_along(lower, "fy", 1), 1, 2)
-    rows_head = jnp.concatenate([left_head, extrap_head], axis=1)
-    extended = jnp.concatenate([from_above, rows_head, rows_tail], axis=2)
-    updated = dual_coeffs + analysis(extended, LEVELS)
+    packed_tail = sent_packed(extrap_tail[:, tile_x - border :], "fx", 1)
+    left_head = passed_along(edge_head, "fx", 1)
+    above_own = sent_packed(extrap_tail[:, :, tail - border :], "fy", 1)
+    left_tail = unpack(*packed_tail)
+    above_corner = sent_packed(left_tail[:, :, tail - border :], "fy", 1)
+
+    matrix_x = jnp.asarray(level_matrix(tile_x + border), dtype=jnp.float32)
+    matrix_y = jnp.asarray(level_matrix(tile_y + border), dtype=jnp.float32)
+    own = jnp.concatenate([unpack(*above_own), extrap_head, extrap_tail], axis=2)
+    own = level_einsum("cxy,vy->cxv", own, matrix_y)
+    own = level_einsum("ux,cxv->cuv", matrix_x[:, border:], own)
+    image_next = jnp.concatenate([image_head, image_tail], axis=2)
+    left_head = after(left_head, (own, image_next))
+    edge = jnp.concatenate([unpack(*above_corner), left_head, left_tail], axis=2)
+    edge = level_einsum("cxy,vy->cxv", edge, matrix_y)
+    edge = level_einsum("ux,cxv->cuv", matrix_x[:, :border], edge)
+    updated = dual_coeffs + refine(own + edge, LEVELS)
     squared_sum = jnp.sum(updated * updated, axis=0)
     pairs = [(i, i ^ 1) for i in range(lax.axis_size("ch"))]
     totals = squared_sum + lax.ppermute(squared_sum, "ch", pairs)
     factor = jnp.minimum(1.0, LAMBDA_REG * reweights / jnp.sqrt(totals + EPSILON))
-    image_next = jnp.concatenate([image_head, image_tail], axis=2)
     return (image_next, updated * factor[None])
 
 

time: 124 us -> 104 us (0.84)
  the two profiles are of different devices: /device:TPU:14 before, /device:TPU:27 now
where the time goes in v3:
time: 104 us
  waiting for transfers between devices  47 us (45%)
  starting transfers between devices  19.9 us (19%)
  matrix products  12.9 us (12%)
  other arithmetic  12 us (12%)
  local copies, waits for them, and re-layouts  11.1 us (11%)
  between operations  1.23 us (1%)
    ppermute x8, waiting for transfers between devices, passed_along(): return lax.ppermute(array, axis, pairs)  46 us
    ppermute x8, starting transfers between devices, passed_along(): return lax.ppermute(array, axis, pairs)  16.3 us
    dot_general x10, matrix products, level_einsum(): return jnp.einsum(spec, first, second, precision=lax.Precision.HIGH)  12.9 us
    unnamed x48, local copies, waits for them, and re-layouts  4.76 us
    ppermute x1, starting transfers between devices, shards(): totals = squared_sum + lax.ppermute(squared_sum, 'ch', pairs)  3.59 us
    mul x2, other arithmetic, step(): return (image, (2.0 * image - cube) * weights)  2.95 us
    concatenate x1, other arithmetic, shards(): image_next = jnp.concatenate([image_head, image_tail], axis=2)  2.73 us
    concatenate x2, local copies, waits for them, and re-layouts, pack(): jnp.concatenate([part[:, g * step:(g + 1) * step] for g in range(groups)]...  2.66 us
  transfers between devices with their start and end apart: 9, of which 8 were waited for; matrix products, arithmetic and copies ran while one was open for 19% of the time, Pallas kernels for 0%

profile of v3, /device:TPU:27, one launch (start us, length us, event | category | flops | bytes accessed | tf_op | source)
XLA Modules:
  0.0 103.9 jit_solution(4309363569324384804)
XLA Ops:
  0.7 0.7 copy-done.11
  1.4 1.3 %copy-done.2 = f32[32,112,256]{2,1,0:T(8,128)S(1)} copy-done((f32[32,112,256]{2,1,0:T(8,128)S(1)}, f32[32,112,256]{2,1,0:T(8,128)}, u32[]{:S(2)}) %copy-start.2) | copy-done | bytes 3670040
  2.7 0.6 convolution_bitcast_fusion.2
  3.3 0.5 copy-done.4
  3.8 0.5 convolution_dynamic-update-slice_fusion
  4.4 1.8 %fusion.50 = f32[32,256,112]{1,2,0:T(8,128)S(1)} fusion(f32[32,112,256]{2,1,0:T(8,128)S(1)} %convolution_dynamic-update-slice_fusion, f32[112,112,1]{1,0,2:T(8,128)S(1)} %copy-done.14), kind=kOutput, calls=%fused_computation.91 | convolution fusion | flops 616562688 | bytes 7390208 | tf_op jit(solution)/shard_map/ux,cuv->cxv/dot_general | solution.py:54
  6.2 1.7 %fusion = f32[32,112,256]{2,1,0:T(8,128)S(1)} fusion(f32[256,256,1]{1,0,2:T(8,128)S(1)} %copy-done.7, f32[32,256,112]{1,2,0:T(8,128)S(1)} %fusion.50), kind=kOutput, calls=%fused_computation.1 | convolution fusion | flops 1409286144 | bytes 7602176 | tf_op jit(solution)/shard_map/cxv,vy->cxy/dot_general | solution.py:54
  8.1 2.2 %collective-permute-start.2 = (f32[32,24,96]{2,1,0:T(8,128)S(1)}, f32[32,24,96]{2,1,0:T(8,128)S(1)}, u32[]{:S(2)}, u32[]{:S(2)}) collective-permute-start(f32[32,24,96]{2,1,0:T(8,128)S(1)} %pad_maximum_fusion.4), channel_id=1, source_target_pairs={{16,0},{17,1},{18,2},{19,3},{20,4},{21,5},{22,6},{23,7},{24,8},{25... | collective-permute-start | bytes 884744 | tf_op jit(solution)/shard_map/ppermute | solution.py:36
  10.3 0.3 slice.373
  10.5 3.0 %collective-permute-start = (f32[32,48,128]{2,1,0:T(8,128)S(1)}, f32[32,48,128]{2,1,0:T(8,128)}, u32[]{:S(2)}, u32[]{:S(2)}) collective-permute-start(f32[32,48,128]{2,1,0:T(8,128)S(1)} %slice.373), channel_id=1, source_target_pairs={{2,0},{4,2},{6,4},{8,6},{10,8},{12,10},{14,12},{3,1},{5,3},{7,5},{... | collective-permute-start | bytes 2359304 | tf_op jit(solution)/shard_map/ppermute | solution.py:36
  13.7 0.4 concatenate.57
  14.0 1.3 %collective-permute-start.1 = (f32[32,8,384]{2,1,0:T(8,128)S(1)}, f32[32,8,384]{2,1,0:T(8,128)S(1)}, u32[]{:S(2)}, u32[]{:S(2)}) collective-permute-start(f32[32,8,384]{2,1,0:T(8,128)S(1)} %concatenate.57), channel_id=1, source_target_pairs={{16,0},{17,1},{18,2},{19,3},{20,4},{21,5},{22,6},{23,7},{24,8},{25... | collective-permute-start | bytes 1179656 | tf_op jit(solution)/shard_map/ppermute | solution.py:36
  15.5 2.6 %collective-permute-done.2 = f32[32,24,96]{2,1,0:T(8,128)S(1)} collective-permute-done((f32[32,24,96]{2,1,0:T(8,128)S(1)}, f32[32,24,96]{2,1,0:T(8,128)S(1)}, u32[]{:S(2)}, u32[]{:S(2)}) %collective-permute-start.2) | collective-permute-done | bytes 294944 | tf_op jit(solution)/shard_map/ppermute | solution.py:36
  18.2 1.8 %fusion.35 = f32[32,48,80]{2,1,0:T(8,128)S(1)} fusion(f32[32,24,48]{2,1,0:T(8,128)S(1)} %get-tuple-element.89, f32[32,24,48]{2,1,0:T(8,128)S(1)} %get-tuple-element.88, f32[32,112,256]{2,1,0:T(8,128)} %copy-done), kind=kLoop, calls=%fused_computation.51 | loop fusion | flops 614400 | bytes 1277952 | tf_op jit(solution)/shard_map/add | solution.py:144
  20.1 0.3 pad_maximum_fusion.1
  20.4 3.2 %collective-permute-start.3 = (f32[32,16,240]{2,1,0:T(8,128)S(1)}, f32[32,16,240]{2,1,0:T(8,128)S(1)}, u32[]{:S(2)}, u32[]{:S(2)}) collective-permute-start(f32[32,16,240]{2,1,0:T(8,128)S(1)} %pad_maximum_fusion.1), channel_id=1, source_target_pairs={{2,0},{4,2},{6,4},{8,6},{10,8},{12,10},{14,12},{3,1},{5,3},{7,5},{... | collective-permute-start | bytes 1474568 | tf_op jit(solution)/shard_map/ppermute | solution.py:36
  23.5 2.9 %collective-permute-done.1 = f32[32,8,384]{2,1,0:T(8,128)S(1)} collective-permute-done((f32[32,8,384]{2,1,0:T(8,128)S(1)}, f32[32,8,384]{2,1,0:T(8,128)S(1)}, u32[]{:S(2)}, u32[]{:S(2)}) %collective-permute-start.1) | collective-permute-done | bytes 393248 | tf_op jit(solution)/shard_map/ppermute | solution.py:36
  27.2 0.6 slice_add_fusion
  27.9 2.8 %collective-permute-done = f32[32,48,128]{2,1,0:T(8,128)} collective-permute-done((f32[32,48,128]{2,1,0:T(8,128)S(1)}, f32[32,48,128]{2,1,0:T(8,128)}, u32[]{:S(2)}, u32[]{:S(2)}) %collective-permute-start) | collective-permute-done | bytes 786464 | tf_op jit(solution)/shard_map/ppermute | solution.py:36
  30.7 1.6 %subtract_multiply_fusion.1 = (f32[32,64,128]{2,1,0:T(8,128)S(1)}, f32[32,64,128]{2,1,0:T(8,128)S(1)}) fusion(f32[32,64,208]{2,1,0:T(8,128)S(1)} %copy-done.5, f32[64,128]{1,0:T(8,128)S(1)} %slice-done.1, f32[32,48,128]{2,1,0:T(8,128)} %collective-permute-done, f32[32,112,256]{2,1,0:T(8,128)S(1)} %copy-done.1, bf16[32,64,208]{2,1,0:T(8,128)(2,1)S(1)} %copy-done.6), kind=kLoop, calls=%fused_computation.46 | loop fusion | flops 2621440 | bytes 5537792 | tf_op jit(solution)/shard_map/mul | solution.py:155
  32.3 0.9 slice.400
  33.3 1.9 %collective-permute-start.7 = (f32[32,48,128]{2,1,0:T(8,128)}, f32[32,48,128]{2,1,0:T(8,128)}, u32[]{:S(2)}, u32[]{:S(2)}) collective-permute-start(f32[32,48,128]{2,1,0:T(8,128)} %slice.400), channel_id=1, source_target_pairs={{0,2},{2,4},{4,6},{6,8},{8,10},{10,12},{12,14},{1,3},{3,5},{5,7},{... | collective-permute-start | bytes 2359304 | tf_op jit(solution)/shard_map/ppermute | solution.py:36
  35.2 23.5 %collective-permute-done.3 = f32[32,16,240]{2,1,0:T(8,128)S(1)} collective-permute-done((f32[32,16,240]{2,1,0:T(8,128)S(1)}, f32[32,16,240]{2,1,0:T(8,128)S(1)}, u32[]{:S(2)}, u32[]{:S(2)}) %collective-permute-start.3) | collective-permute-done | bytes 491552 | tf_op jit(solution)/shard_map/ppermute | solution.py:36
  58.7 0.2 fusion.47
  58.9 1.3 %subtract_multiply_fusion = (f32[32,64,80]{2,1,0:T(8,128)S(1)}, f32[32,64,80]{2,1,0:T(8,128)}) fusion(f32[32,64,208]{2,1,0:T(8,128)S(1)} %copy-done.5, f32[64,80]{1,0:T(8,128)S(1)} %slice-done, f32[32,64,80]{2,1,0:T(8,128)S(1)} %slice_add_fusion, f32[32,16,80]{2,1,0:T(8,128)S(1)} %get-tuple-element.84, f32[32,16,80]{2,1,0:T(8,128)S(1)} %get-tuple-element.85, ...), kind=kLoop, calls=%fused_computation.45 | loop fusion | flops 2621440 | bytes 3461120 | tf_op jit(solution)/shard_map/mul | solution.py:155
  60.2 1.2 %fusion.44 = (f32[32,8,48]{2,1,0:T(8,128)S(1)}, f32[32,8,48]{2,1,0:T(8,128)}, f32[32,8,48]{2,1,0:T(8,128)}, f32[32,8,48]{2,1,0:T(8,128)}, f32[32,8,48]{2,1,0:T(8...) fusion(f32[32,64,80]{2,1,0:T(8,128)S(1)} %get-tuple-element.52), kind=kLoop, calls=%fused_computation.85 | loop fusion | bytes 786432 | tf_op jit(solution)/shard_map/slice | solution.py:109
  61.4 2.3 %concatenate.64 = f32[32,8,384]{2,1,0:T(8,128)} concatenate(f32[32,8,48]{2,1,0:T(8,128)} %get-tuple-element.76, f32[32,8,48]{2,1,0:T(8,128)} %get-tuple-element.75, f32[32,8,48]{2,1,0:T(8,128)} %get-tuple-element.74, f32[32,8,48]{2,1,0:T(8,128)} %get-tuple-element.73, f32[32,8,48]{2,1,0:T(8,128)} %get-tuple-element.72, f32[32,8,48]{2,1,0:T(8,128)} %get-tuple-element.71, ...), dimensions={2} | concatenate | bytes 786432 | tf_op jit(solution)/shard_map/concatenate | solution.py:109
  63.7 1.3 %collective-permute-start.4 = (f32[32,8,384]{2,1,0:T(8,128)}, f32[32,8,384]{2,1,0:T(8,128)S(1)}, u32[]{:S(2)}, u32[]{:S(2)}) collective-permute-start(f32[32,8,384]{2,1,0:T(8,128)} %concatenate.64), channel_id=1, source_target_pairs={{0,16},{1,17},{2,18},{3,19},{4,20},{5,21},{6,22},{7,23},{8,24},{9,... | collective-permute-start | bytes 1179656 | tf_op jit(solution)/shard_map/ppermute | solution.py:36
  65.1 0.3 pad_maximum_fusion.2
  65.4 2.1 %collective-permute-start.5 = (f32[32,16,240]{2,1,0:T(8,128)S(1)}, f32[32,16,240]{2,1,0:T(8,128)S(1)}, u32[]{:S(2)}, u32[]{:S(2)}) collective-permute-start(f32[32,16,240]{2,1,0:T(8,128)S(1)} %pad_maximum_fusion.2), channel_id=1, source_target_pairs={{0,2},{2,4},{4,6},{6,8},{8,10},{10,12},{12,14},{1,3},{3,5},{5,7},{... | collective-permute-start | bytes 1474568 | tf_op jit(solution)/shard_map/ppermute | solution.py:36
  67.5 2.7 %pad_maximum_fusion = f32[32,64,208]{2,1,0:T(8,128)} fusion(f32[32,64,80]{2,1,0:T(8,128)} %get-tuple-element.53, f32[32,64,128]{2,1,0:T(8,128)S(1)} %get-tuple-element.55), kind=kLoop, calls=%fused_computation.4 | loop fusion | flops 425984 | bytes 3407872 | tf_op jit(solution)/shard_map/concatenate | solution.py:173
  70.2 4.5 %collective-permute-done.4 = f32[32,8,384]{2,1,0:T(8,128)S(1)} collective-permute-done((f32[32,8,384]{2,1,0:T(8,128)}, f32[32,8,384]{2,1,0:T(8,128)S(1)}, u32[]{:S(2)}, u32[]{:S(2)}) %collective-permute-start.4) | collective-permute-done | bytes 393248 | tf_op jit(solution)/shard_map/ppermute | solution.py:36
  75.4 1.6 %fusion.2 = f32[32,64,256]{2,1,0:T(8,128)S(1)} fusion(f32[256,256,1]{1,0,2:T(8,128)S(1)} %copy-done.7, f32[32,64,80]{2,1,0:T(8,128)S(1)} %get-tuple-element.52, f32[32,64,128]{2,1,0:T(8,128)S(1)} %get-tuple-element.54, f32[32,64,48]{2,1,0:T(8,128)S(1)} %slice_dynamic-update-slice_fusion), kind=kOutput, calls=%fused_computation.5 | convolution fusion | flops 806354944 | bytes 4456448 | tf_op jit(solution)/shard_map/cxy,vy->cxv/dot_general | solution.py:54
  77.0 2.8 %collective-permute-done.5 = f32[32,16,240]{2,1,0:T(8,128)S(1)} collective-permute-done((f32[32,16,240]{2,1,0:T(8,128)S(1)}, f32[32,16,240]{2,1,0:T(8,128)S(1)}, u32[]{:S(2)}, u32[]{:S(2)}) %collective-permute-start.5) | collective-permute-done | bytes 491552 | tf_op jit(solution)/shard_map/ppermute | solution.py:36
  79.8 0.2 fusion.46
  80.0 0.3 fusion.36
  80.3 1.3 %collective-permute-start.6 = (f32[32,24,96]{2,1,0:T(8,128)S(1)}, f32[32,24,96]{2,1,0:T(8,128)S(1)}, u32[]{:S(2)}, u32[]{:S(2)}) collective-permute-start(f32[32,24,96]{2,1,0:T(8,128)S(1)} %fusion.36), channel_id=1, source_target_pairs={{0,16},{1,17},{2,18},{3,19},{4,20},{5,21},{6,22},{7,23},{8,24},{9,... | collective-permute-start | bytes 884744 | tf_op jit(solution)/shard_map/ppermute | solution.py:36
  81.6 1.7 %convolution_bitcast_fusion = f32[32,112,256]{2,1,0:T(8,128)S(1)} fusion(f32[32,64,256]{2,1,0:T(8,128)S(1)} %fusion.2, f32[112,64,1]{0,1,2:T(8,128)S(1)} %copy-done.15), kind=kOutput, calls=%fused_computation.11 | convolution fusion | flops 352321536 | bytes 5795840 | tf_op jit(solution)/shard_map/ux,cxv->cuv/dot_general | solution.py:54
  83.3 6.9 %collective-permute-done.6 = f32[32,24,96]{2,1,0:T(8,128)S(1)} collective-permute-done((f32[32,24,96]{2,1,0:T(8,128)S(1)}, f32[32,24,96]{2,1,0:T(8,128)S(1)}, u32[]{:S(2)}, u32[]{:S(2)}) %collective-permute-start.6) | collective-permute-done | bytes 294944 | tf_op jit(solution)/shard_map/ppermute | solution.py:36
  90.4 2.4 %fusion.8 = f32[32,48,256]{2,1,0:T(8,128)S(1)} fusion(f32[256,256,1]{1,0,2:T(8,128)S(1)} %copy-done.7, f32[32,16,80]{2,1,0:T(8,128)S(1)} %get-tuple-element.81, f32[32,16,80]{2,1,0:T(8,128)S(1)} %get-tuple-element.82, f32[32,16,80]{2,1,0:T(8,128)S(1)} %get-tuple-element.80, f32[32,48,128]{2,1,0:T(8,128)} %collective-permute-done.7, ...), kind=kOutput, calls=%fused_computation.13 | convolution fusion | flops 605945856 | bytes 3407872 | tf_op jit(solution)/shard_map/cxy,vy->cxv/dot_general | solution.py:54
  92.8 1.7 %bitcast_add_fusion = f32[32,112,256]{2,1,0:T(8,128)S(1)} fusion(f32[32,112,256]{2,1,0:T(8,128)S(1)} %convolution_bitcast_fusion, f32[32,48,256]{2,1,0:T(8,128)S(1)} %fusion.8, f32[112,48,1]{0,1,2:T(8,128)S(1)} %copy-done.16), kind=kOutput, calls=%fused_computation | convolution fusion | flops 265158656 | bytes 8934400 | tf_op jit(solution)/shard_map/ux,cxv->cuv/dot_general | solution.py:54
  94.5 0.5 fusion.32
  95.1 0.5 fusion.20
  95.6 1.0 copy-done.3
  96.6 0.7 multiply_reduce_fusion
  97.2 3.6 %collective-permute-start.8 = (f32[112,256]{1,0:T(8,128)S(1)}, f32[112,256]{1,0:T(8,128)S(1)}, u32[]{:S(2)}, u32[]{:S(2)}) collective-permute-start(f32[112,256]{1,0:T(8,128)S(1)} %get-tuple-element.50), channel_id=1, source_target_pairs={{0,1},{1,0},{2,3},{3,2},{4,5},{5,4},{6,7},{7,6},{8,9},{9,8},{10,11... | collective-permute-start | bytes 344072 | tf_op jit(solution)/shard_map/ppermute | solution.py:181
  100.8 1.0 collective-permute-done.8
  101.8 2.1 %broadcast_multiply_fusion = f32[32,112,256]{2,1,0:T(8,128)} fusion(f32[32,112,256]{2,1,0:T(8,128)S(1)} %get-tuple-element.51, f32[112,256]{1,0:T(8,128)S(1)} %multiply_minimum_fusion), kind=kLoop, calls=%fused_computation.12 | loop fusion | flops 917504 | bytes 7454720 | tf_op jit(solution)/shard_map/mul | solution.py:183
  (62 shorter events, 2.3 us)
Async XLA Ops:
  0.6 0.8 copy-start.11
  0.6 2.7 %copy-start.9 = (f32[128,128,1]{1,0,2:T(8,128)S(1)}, f32[128,128,1]{1,0,2:T(8,128)}, u32[]{:S(2)}) copy-start(f32[128,128,1]{1,0,2:T(8,128)} %constant.146) | copy-start | bytes 196612
  0.7 2.1 %copy-start.2 = (f32[32,112,256]{2,1,0:T(8,128)S(1)}, f32[32,112,256]{2,1,0:T(8,128)}, u32[]{:S(2)}) copy-start(f32[32,112,256]{2,1,0:T(8,128)} %param.22) | copy-start | bytes 11010052
  0.7 3.2 %copy-start.4 = (f32[32,112,256]{2,1,0:T(8,128)S(1)}, f32[32,112,256]{2,1,0:T(8,128)}, u32[]{:S(2)}) copy-start(f32[32,112,256]{2,1,0:T(8,128)} %param.22) | copy-start | bytes 11010052
  2.7 1.6 %copy-start.14 = (f32[112,112,1]{1,0,2:T(8,128)S(1)}, f32[112,112,1]{1,0,2:T(8,128)}, u32[]{:S(2)}) copy-start(f32[112,112,1]{1,0,2:T(8,128)} %constant.147) | copy-start | bytes 150532
  4.4 1.8 %copy-start.7 = (f32[256,256,1]{1,0,2:T(8,128)S(1)}, f32[256,256,1]{1,0,2:T(8,128)}, u32[]{:S(2)}) copy-start(f32[256,256,1]{1,0,2:T(8,128)} %constant.148) | copy-start | bytes 786436
  7.8 5.8 %copy-start = (f32[32,112,256]{2,1,0:T(8,128)}, f32[32,112,256]{2,1,0:T(8,128)S(1)}, u32[]{:S(2)}) copy-start(f32[32,112,256]{2,1,0:T(8,128)S(1)} %fusion) | copy-start | bytes 11010052
  8.1 10.0 %collective-permute-start.2 = (f32[32,24,96]{2,1,0:T(8,128)S(1)}, f32[32,24,96]{2,1,0:T(8,128)S(1)}, u32[]{:S(2)}, u32[]{:S(2)}) collective-permute-start(f32[32,24,96]{2,1,0:T(8,128)S(1)} %pad_maximum_fusion.4), channel_id=1, source_target_pairs={{16,0},{17,1},{18,2},{19,3},{20,4},{21,5},{22,6},{23,7},{24,8},{25... | collective-permute-start | bytes 884744 | tf_op jit(solution)/shard_map/ppermute | solution.py:36
  10.5 20.1 %collective-permute-start = (f32[32,48,128]{2,1,0:T(8,128)S(1)}, f32[32,48,128]{2,1,0:T(8,128)}, u32[]{:S(2)}, u32[]{:S(2)}) collective-permute-start(f32[32,48,128]{2,1,0:T(8,128)S(1)} %slice.373), channel_id=1, source_target_pairs={{2,0},{4,2},{6,4},{8,6},{10,8},{12,10},{14,12},{3,1},{5,3},{7,5},{... | collective-permute-start | bytes 2359304 | tf_op jit(solution)/shard_map/ppermute | solution.py:36
  14.0 12.4 %collective-permute-start.1 = (f32[32,8,384]{2,1,0:T(8,128)S(1)}, f32[32,8,384]{2,1,0:T(8,128)S(1)}, u32[]{:S(2)}, u32[]{:S(2)}) collective-permute-start(f32[32,8,384]{2,1,0:T(8,128)S(1)} %concatenate.57), channel_id=1, source_target_pairs={{16,0},{17,1},{18,2},{19,3},{20,4},{21,5},{22,6},{23,7},{24,8},{25... | collective-permute-start | bytes 1179656 | tf_op jit(solution)/shard_map/ppermute | solution.py:36
  15.5 11.1 %copy-start.8 = (f32[64,208]{1,0:T(8,128)}, f32[64,208]{1,0:T(8,128)S(1)}, u32[]{:S(2)}) copy-start(f32[64,208]{1,0:T(8,128)S(1)} %broadcast_multiply_fusion.1) | copy-start | bytes 159748
  18.2 9.0 %copy-start.1 = (f32[32,112,256]{2,1,0:T(8,128)S(1)}, f32[32,112,256]{2,1,0:T(8,128)}, u32[]{:S(2)}) copy-start(f32[32,112,256]{2,1,0:T(8,128)} %copy-done) | copy-start | bytes 11010052
  20.1 10.6 %copy-start.5 = (f32[32,64,208]{2,1,0:T(8,128)S(1)}, f32[32,64,208]{2,1,0:T(8,128)}, u32[]{:S(2)}) copy-start(f32[32,64,208]{2,1,0:T(8,128)} %param.20) | copy-start | bytes 5111812
  20.1 10.6 %copy-start.6 = (bf16[32,64,208]{2,1,0:T(8,128)(2,1)S(1)}, bf16[32,64,208]{2,1,0:T(8,128)(2,1)}, u32[]{:S(2)}) copy-start(bf16[32,64,208]{2,1,0:T(8,128)(2,1)} %param.21) | copy-start | bytes 2555908
  20.4 38.3 %collective-permute-start.3 = (f32[32,16,240]{2,1,0:T(8,128)S(1)}, f32[32,16,240]{2,1,0:T(8,128)S(1)}, u32[]{:S(2)}, u32[]{:S(2)}) collective-permute-start(f32[32,16,240]{2,1,0:T(8,128)S(1)} %pad_maximum_fusion.1), channel_id=1, source_target_pairs={{2,0},{4,2},{6,4},{8,6},{10,8},{12,10},{14,12},{3,1},{5,3},{7,5},{... | collective-permute-start | bytes 1474568 | tf_op jit(solution)/shard_map/ppermute | solution.py:36
  26.7 4.0 %slice-start.1 = ((f32[64,208]{1,0:T(8,128)}), f32[64,128]{1,0:T(8,128)S(1)}, s32[]{:S(2)}) async-start(f32[64,208]{1,0:T(8,128)} %copy-done.8), calls=%async_computation.1 | async-start | bytes 65536 | tf_op jit(solution)/shard_map/slice | solution.py:151
  27.9 31.0 %slice-start = ((f32[64,208]{1,0:T(8,128)}), f32[64,80]{1,0:T(8,128)S(1)}, s32[]{:S(2)}) async-start(f32[64,208]{1,0:T(8,128)} %copy-done.8), calls=%async_computation | async-start | bytes 65536 | tf_op jit(solution)/shard_map/slice | solution.py:151
  33.3 50.1 %collective-permute-start.7 = (f32[32,48,128]{2,1,0:T(8,128)}, f32[32,48,128]{2,1,0:T(8,128)}, u32[]{:S(2)}, u32[]{:S(2)}) collective-permute-start(f32[32,48,128]{2,1,0:T(8,128)} %slice.400), channel_id=1, source_target_pairs={{0,2},{2,4},{4,6},{6,8},{8,10},{10,12},{12,14},{1,3},{3,5},{5,7},{... | collective-permute-start | bytes 2359304 | tf_op jit(solution)/shard_map/ppermute | solution.py:36
  63.7 11.0 %collective-permute-start.4 = (f32[32,8,384]{2,1,0:T(8,128)}, f32[32,8,384]{2,1,0:T(8,128)S(1)}, u32[]{:S(2)}, u32[]{:S(2)}) collective-permute-start(f32[32,8,384]{2,1,0:T(8,128)} %concatenate.64), channel_id=1, source_target_pairs={{0,16},{1,17},{2,18},{3,19},{4,20},{5,21},{6,22},{7,23},{8,24},{9,... | collective-permute-start | bytes 1179656 | tf_op jit(solution)/shard_map/ppermute | solution.py:36
  65.4 14.5 %collective-permute-start.5 = (f32[32,16,240]{2,1,0:T(8,128)S(1)}, f32[32,16,240]{2,1,0:T(8,128)S(1)}, u32[]{:S(2)}, u32[]{:S(2)}) collective-permute-start(f32[32,16,240]{2,1,0:T(8,128)S(1)} %pad_maximum_fusion.2), channel_id=1, source_target_pairs={{0,2},{2,4},{4,6},{6,8},{8,10},{10,12},{12,14},{1,3},{3,5},{5,7},{... | collective-permute-start | bytes 1474568 | tf_op jit(solution)/shard_map/ppermute | solution.py:36
  75.4 6.2 %copy-start.15 = (f32[112,64,1]{0,1,2:T(8,128)S(1)}, f32[112,64,1]{0,1,2:T(8,128)}, u32[]{:S(2)}) copy-start(f32[112,64,1]{0,1,2:T(8,128)} %constant.149) | copy-start | bytes 86020
  80.3 9.9 %collective-permute-start.6 = (f32[32,24,96]{2,1,0:T(8,128)S(1)}, f32[32,24,96]{2,1,0:T(8,128)S(1)}, u32[]{:S(2)}, u32[]{:S(2)}) collective-permute-start(f32[32,24,96]{2,1,0:T(8,128)S(1)} %fusion.36), channel_id=1, source_target_pairs={{0,16},{1,17},{2,18},{3,19},{4,20},{5,21},{6,22},{7,23},{8,24},{9,... | collective-permute-start | bytes 884744 | tf_op jit(solution)/shard_map/ppermute | solution.py:36
  83.3 9.5 %copy-start.16 = (f32[112,48,1]{0,1,2:T(8,128)S(1)}, f32[112,48,1]{0,1,2:T(8,128)}, u32[]{:S(2)}) copy-start(f32[112,48,1]{0,1,2:T(8,128)} %constant.150) | copy-start | bytes 64516
  92.8 1.7 %copy-start.10 = (f32[128,128,1]{1,0,2:T(8,128)S(1)}, f32[128,128,1]{1,0,2:T(8,128)}, u32[]{:S(2)}) copy-start(f32[128,128,1]{1,0,2:T(8,128)} %constant.146) | copy-start | bytes 196612
  92.8 2.3 %copy-start.12 = (f32[56,56,1]{1,0,2:T(8,128)S(1)}, f32[56,56,1]{1,0,2:T(8,128)}, u32[]{:S(2)}) copy-start(f32[56,56,1]{1,0,2:T(8,128)} %constant.145) | copy-start | bytes 37636
  94.5 2.0 %copy-start.3 = (f32[32,112,256]{2,1,0:T(8,128)S(1)}, f32[32,112,256]{2,1,0:T(8,128)}, u32[]{:S(2)}) copy-start(f32[32,112,256]{2,1,0:T(8,128)} %param.22) | copy-start | bytes 11010052
  96.6 5.2 %copy-start.13 = (f32[112,256]{1,0:T(8,128)S(1)}, f32[112,256]{1,0:T(8,128)}, u32[]{:S(2)}) copy-start(f32[112,256]{1,0:T(8,128)} %param.23) | copy-start | bytes 344068
  97.2 4.6 %collective-permute-start.8 = (f32[112,256]{1,0:T(8,128)S(1)}, f32[112,256]{1,0:T(8,128)S(1)}, u32[]{:S(2)}, u32[]{:S(2)}) collective-permute-start(f32[112,256]{1,0:T(8,128)S(1)} %get-tuple-element.50), channel_id=1, source_target_pairs={{0,1},{1,0},{2,3},{3,2},{4,5},{5,4},{6,7},{7,6},{8,9},{9,8},{10,11... | collective-permute-start | bytes 344072 | tf_op jit(solution)/shard_map/ppermute | solution.py:181

commit v4 on v3

--- a/solution.py
+++ b/solution.py
@@ -156,23 +156,29 @@
 
     image_head, extrap_head = step(own_head[:, border:], from_right_head, 0, head)
     edge_head = extrap_head[:, tile_x - border :]
+    half = edge_head.shape[0] // 2
+    first_half = passed_along(edge_head[:half], "fx", 1)
     own_tail = with_rows(synthesized[:, border:, border + head :], unpack(*rest))
     from_right_tail = unpack(after(packed_tail[0], (edge_head, own_tail)), border, tail)
     image_tail, extrap_tail = step(own_tail, from_right_tail, head, tile_y)
-    packed_tail = sent_packed(extrap_tail[:, tile_x - border :], "fx", 1)
-    left_head = passed_along(edge_head, "fx", 1)
-    above_own = sent_packed(extrap_tail[:, :, tail - border :], "fy", 1)
-    left_tail = unpack(*packed_tail)
-    above_corner = sent_packed(left_tail[:, :, tail - border :], "fy", 1)
+    edge_tail = pack(extrap_tail[:, tile_x - border :])
+    left_tail = unpack(passed_along(edge_tail, "fx", 1), border, tail)
+    second_half = passed_along(edge_head[half:], "fx", 1)
+    own_rows = after(extrap_tail, edge_tail)[:, :, tail - border :]
+    above_own = passed_along(pack(own_rows), "fy", 1)
+    edge_corner = pack(left_tail[:, :, tail - border :])
+    above_corner = unpack(passed_along(edge_corner, "fy", 1), border, border)
+    above_own = unpack(after(above_own, edge_corner), tile_x, border)
 
     matrix_x = jnp.asarray(level_matrix(tile_x + border), dtype=jnp.float32)
     matrix_y = jnp.asarray(level_matrix(tile_y + border), dtype=jnp.float32)
-    own = jnp.concatenate([unpack(*above_own), extrap_head, extrap_tail], axis=2)
+    own = jnp.concatenate([above_own, extrap_head, extrap_tail], axis=2)
     own = level_einsum("cxy,vy->cxv", own, matrix_y)
     own = level_einsum("ux,cxv->cuv", matrix_x[:, border:], own)
     image_next = jnp.concatenate([image_head, image_tail], axis=2)
-    left_head = after(left_head, (own, image_next))
-    edge = jnp.concatenate([unpack(*above_corner), left_head, left_tail], axis=2)
+    second_half = after(second_half, (own, image_next))
+    left_head = jnp.concatenate([first_half, second_half], axis=0)
+    edge = jnp.concatenate([above_corner, left_head, left_tail], axis=2)
     edge = level_einsum("cxy,vy->cxv", edge, matrix_y)
     edge = level_einsum("ux,cxv->cuv", matrix_x[:, :border], edge)
     updated = dual_coeffs + refine(own + edge, LEVELS)

time: 104 us -> 92.9 us (0.89)
  the two profiles are of different devices: /device:TPU:27 before, /device:TPU:0 now
where the time goes in v4:
time: 92.9 us; the launch traced here: 92.4 us
  waiting for transfers between devices  30 us (32%)
  starting transfers between devices  23.3 us (25%)
  matrix products  12.9 us (14%)
  other arithmetic  12.8 us (14%)
  local copies, waits for them, and re-layouts  12.2 us (13%)
  between operations  1.23 us (1%)
    ppermute x9, waiting for transfers between devices, passed_along(): return lax.ppermute(array, axis, pairs)  28.7 us
    ppermute x9, starting transfers between devices, passed_along(): return lax.ppermute(array, axis, pairs)  23.2 us
    dot_general x10, matrix products, level_einsum(): return jnp.einsum(spec, first, second, precision=lax.Precision.HIGH)  12.9 us
    unnamed x48, local copies, waits for them, and re-layouts  4.76 us
    mul x2, other arithmetic, step(): return (image, (2.0 * image - cube) * weights)  2.95 us
    concatenate x1, other arithmetic, shards(): image_next = jnp.concatenate([image_head, image_tail], axis=2)  2.73 us
    concatenate x2, local copies, waits for them, and re-layouts, pack(): jnp.concatenate([part[:, g * step:(g + 1) * step] for g in range(groups)]...  2.65 us
    add x2, other arithmetic, with_rows(): return own + jnp.pad(incoming, ((0, 0), (0, 0), (tail - border, 0)))  2.42 us
  transfers between devices with their start and end apart: 10, of which 7 were waited for; matrix products, arithmetic and copies ran while one was open for 20% of the time, Pallas kernels for 0%

profile of v4, /device:TPU:0, one launch (start us, length us, event | category | flops | bytes accessed | tf_op | source)
XLA Modules:
  0.0 92.4 jit_solution(2768285105666837052)
XLA Ops:
  0.7 0.7 copy-done.11
  1.4 1.3 %copy-done.2 = f32[32,112,256]{2,1,0:T(8,128)S(1)} copy-done((f32[32,112,256]{2,1,0:T(8,128)S(1)}, f32[32,112,256]{2,1,0:T(8,128)}, u32[]{:S(2)}) %copy-start.2) | copy-done | bytes 3670040
  2.7 0.6 convolution_bitcast_fusion.2
  3.3 0.5 copy-done.4
  3.8 0.5 convolution_dynamic-update-slice_fusion
  4.4 1.8 %fusion.53 = f32[32,256,112]{1,2,0:T(8,128)S(1)} fusion(f32[32,112,256]{2,1,0:T(8,128)S(1)} %convolution_dynamic-update-slice_fusion, f32[112,112,1]{1,0,2:T(8,128)S(1)} %copy-done.14), kind=kOutput, calls=%fused_computation.94 | convolution fusion | flops 616562688 | bytes 7390208 | tf_op jit(solution)/shard_map/ux,cuv->cxv/dot_general | solution.py:54
  6.2 1.7 %fusion = f32[32,112,256]{2,1,0:T(8,128)S(1)} fusion(f32[256,256,1]{1,0,2:T(8,128)S(1)} %copy-done.7, f32[32,256,112]{1,2,0:T(8,128)S(1)} %fusion.53), kind=kOutput, calls=%fused_computation.1 | convolution fusion | flops 1409286144 | bytes 7602176 | tf_op jit(solution)/shard_map/cxv,vy->cxy/dot_general | solution.py:54
  8.1 1.3 %collective-permute-start.2 = (f32[32,24,96]{2,1,0:T(8,128)S(1)}, f32[32,24,96]{2,1,0:T(8,128)S(1)}, u32[]{:S(2)}, u32[]{:S(2)}) collective-permute-start(f32[32,24,96]{2,1,0:T(8,128)S(1)} %pad_maximum_fusion.4), channel_id=1, source_target_pairs={{16,0},{17,1},{18,2},{19,3},{20,4},{21,5},{22,6},{23,7},{24,8},{25... | collective-permute-start | bytes 884744 | tf_op jit(solution)/shard_map/ppermute | solution.py:36
  9.4 0.3 slice.380
  9.6 1.3 %collective-permute-start = (f32[32,48,128]{2,1,0:T(8,128)S(1)}, f32[32,48,128]{2,1,0:T(8,128)}, u32[]{:S(2)}, u32[]{:S(2)}) collective-permute-start(f32[32,48,128]{2,1,0:T(8,128)S(1)} %slice.380), channel_id=1, source_target_pairs={{2,0},{4,2},{6,4},{8,6},{10,8},{12,10},{14,12},{3,1},{5,3},{7,5},{... | collective-permute-start | bytes 2359304 | tf_op jit(solution)/shard_map/ppermute | solution.py:36
  11.0 0.4 concatenate.60
  11.4 1.3 %collective-permute-start.1 = (f32[32,8,384]{2,1,0:T(8,128)S(1)}, f32[32,8,384]{2,1,0:T(8,128)S(1)}, u32[]{:S(2)}, u32[]{:S(2)}) collective-permute-start(f32[32,8,384]{2,1,0:T(8,128)S(1)} %concatenate.60), channel_id=1, source_target_pairs={{16,0},{17,1},{18,2},{19,3},{20,4},{21,5},{22,6},{23,7},{24,8},{25... | collective-permute-start | bytes 1179656 | tf_op jit(solution)/shard_map/ppermute | solution.py:36
  12.8 9.5 %collective-permute-done.2 = f32[32,24,96]{2,1,0:T(8,128)S(1)} collective-permute-done((f32[32,24,96]{2,1,0:T(8,128)S(1)}, f32[32,24,96]{2,1,0:T(8,128)S(1)}, u32[]{:S(2)}, u32[]{:S(2)}) %collective-permute-start.2) | collective-permute-done | bytes 294944 | tf_op jit(solution)/shard_map/ppermute | solution.py:36
  22.3 0.2 fusion.52
  22.5 1.8 %fusion.37 = f32[32,48,80]{2,1,0:T(8,128)S(1)} fusion(f32[32,24,48]{2,1,0:T(8,128)S(1)} %get-tuple-element.95, f32[32,24,48]{2,1,0:T(8,128)S(1)} %get-tuple-element.94, f32[32,112,256]{2,1,0:T(8,128)} %copy-done), kind=kLoop, calls=%fused_computation.53 | loop fusion | flops 614400 | bytes 1277952 | tf_op jit(solution)/shard_map/add | solution.py:144
  24.4 0.3 pad_maximum_fusion.1
  24.6 1.4 %collective-permute-start.3 = (f32[32,16,240]{2,1,0:T(8,128)S(1)}, f32[32,16,240]{2,1,0:T(8,128)S(1)}, u32[]{:S(2)}, u32[]{:S(2)}) collective-permute-start(f32[32,16,240]{2,1,0:T(8,128)S(1)} %pad_maximum_fusion.1), channel_id=1, source_target_pairs={{2,0},{4,2},{6,4},{8,6},{10,8},{12,10},{14,12},{3,1},{5,3},{7,5},{... | collective-permute-start | bytes 1474568 | tf_op jit(solution)/shard_map/ppermute | solution.py:36
  26.1 3.8 %collective-permute-done.1 = f32[32,8,384]{2,1,0:T(8,128)S(1)} collective-permute-done((f32[32,8,384]{2,1,0:T(8,128)S(1)}, f32[32,8,384]{2,1,0:T(8,128)S(1)}, u32[]{:S(2)}, u32[]{:S(2)}) %collective-permute-start.1) | collective-permute-done | bytes 393248 | tf_op jit(solution)/shard_map/ppermute | solution.py:36
  30.7 0.6 slice_add_fusion
  31.3 1.7 %collective-permute-done = f32[32,48,128]{2,1,0:T(8,128)} collective-permute-done((f32[32,48,128]{2,1,0:T(8,128)S(1)}, f32[32,48,128]{2,1,0:T(8,128)}, u32[]{:S(2)}, u32[]{:S(2)}) %collective-permute-start) | collective-permute-done | bytes 786464 | tf_op jit(solution)/shard_map/ppermute | solution.py:36
  33.1 1.6 %subtract_multiply_fusion = (f32[32,64,128]{2,1,0:T(8,128)S(1)}, f32[32,64,128]{2,1,0:T(8,128)S(1)}) fusion(f32[32,64,208]{2,1,0:T(8,128)S(1)} %copy-done.5, f32[64,128]{1,0:T(8,128)S(1)} %slice-done.1, f32[32,48,128]{2,1,0:T(8,128)} %collective-permute-done, f32[32,112,256]{2,1,0:T(8,128)S(1)} %copy-done.1, bf16[32,64,208]{2,1,0:T(8,128)(2,1)S(1)} %copy-done.6), kind=kLoop, calls=%fused_computation.47 | loop fusion | flops 2621440 | bytes 5537792 | tf_op jit(solution)/shard_map/mul | solution.py:155
  34.7 8.7 %collective-permute-done.3 = f32[32,16,240]{2,1,0:T(8,128)S(1)} collective-permute-done((f32[32,16,240]{2,1,0:T(8,128)S(1)}, f32[32,16,240]{2,1,0:T(8,128)S(1)}, u32[]{:S(2)}, u32[]{:S(2)}) %collective-permute-start.3) | collective-permute-done | bytes 491552 | tf_op jit(solution)/shard_map/ppermute | solution.py:36
  43.3 0.2 fusion.50
  43.5 1.3 %subtract_multiply_fusion.1 = (f32[32,64,80]{2,1,0:T(8,128)S(1)}, f32[32,64,80]{2,1,0:T(8,128)}) fusion(f32[32,64,208]{2,1,0:T(8,128)S(1)} %copy-done.5, f32[64,80]{1,0:T(8,128)S(1)} %slice-done, f32[32,64,80]{2,1,0:T(8,128)S(1)} %slice_add_fusion, f32[32,16,80]{2,1,0:T(8,128)S(1)} %get-tuple-element.90, f32[32,16,80]{2,1,0:T(8,128)S(1)} %get-tuple-element.91, ...), kind=kLoop, calls=%fused_computation.48 | loop fusion | flops 2621440 | bytes 3461120 | tf_op jit(solution)/shard_map/mul | solution.py:155
  44.9 1.1 %pad_maximum_fusion.2 = f32[32,16,240]{2,1,0:T(8,128)} fusion(f32[32,16,80]{2,1,0:T(8,128)S(1)} %get-tuple-element.81, f32[32,16,80]{2,1,0:T(8,128)S(1)} %get-tuple-element.82, f32[32,16,80]{2,1,0:T(8,128)S(1)} %get-tuple-element.80), kind=kLoop, calls=%fused_computation.56 | loop fusion | flops 245760 | bytes 983040 | tf_op jit(solution)/shard_map/concatenate | solution.py:109
  46.0 5.4 %collective-permute-start.5 = (f32[32,16,240]{2,1,0:T(8,128)}, f32[32,16,240]{2,1,0:T(8,128)}, u32[]{:S(2)}, u32[]{:S(2)}) collective-permute-start(f32[32,16,240]{2,1,0:T(8,128)} %pad_maximum_fusion.2), channel_id=1, source_target_pairs={{0,2},{2,4},{4,6},{6,8},{8,10},{10,12},{12,14},{1,3},{3,5},{5,7},{... | collective-permute-start | bytes 1474568 | tf_op jit(solution)/shard_map/ppermute | solution.py:36
  51.3 0.9 %fusion.45 = (f32[16,48,128]{2,1,0:T(8,128)}, f32[16,48,128]{2,1,0:T(8,128)}) fusion(f32[32,64,128]{2,1,0:T(8,128)S(1)} %get-tuple-element.56), kind=kLoop, calls=%fused_computation.86 | loop fusion | bytes 1572864 | tf_op jit(solution)/shard_map/slice | solution.py:160
  52.3 2.5 %collective-permute-start.7 = (f32[16,48,128]{2,1,0:T(8,128)}, f32[16,48,128]{2,1,0:T(8,128)}, u32[]{:S(2)}, u32[]{:S(2)}) collective-permute-start(f32[16,48,128]{2,1,0:T(8,128)} %get-tuple-element.70), channel_id=1, source_target_pairs={{0,2},{2,4},{4,6},{6,8},{8,10},{10,12},{12,14},{1,3},{3,5},{5,7},{... | collective-permute-start | bytes 1179656 | tf_op jit(solution)/shard_map/ppermute | solution.py:36
  54.7 4.3 %collective-permute-start.8 = (f32[16,48,128]{2,1,0:T(8,128)}, f32[16,48,128]{2,1,0:T(8,128)}, u32[]{:S(2)}, u32[]{:S(2)}) collective-permute-start(f32[16,48,128]{2,1,0:T(8,128)} %get-tuple-element.71), channel_id=1, source_target_pairs={{0,2},{2,4},{4,6},{6,8},{8,10},{10,12},{12,14},{1,3},{3,5},{5,7},{... | collective-permute-start | bytes 1179656 | tf_op jit(solution)/shard_map/ppermute | solution.py:36
  59.1 1.2 %fusion.46 = (f32[32,8,48]{2,1,0:T(8,128)S(1)}, f32[32,8,48]{2,1,0:T(8,128)}, f32[32,8,48]{2,1,0:T(8,128)}, f32[32,8,48]{2,1,0:T(8,128)}, f32[32,8,48]{2,1,0:T(8...) fusion(f32[32,64,80]{2,1,0:T(8,128)S(1)} %get-tuple-element.51), kind=kLoop, calls=%fused_computation.87 | loop fusion | bytes 786432 | tf_op jit(solution)/shard_map/slice | solution.py:109
  60.3 2.3 %concatenate.68 = f32[32,8,384]{2,1,0:T(8,128)} concatenate(f32[32,8,48]{2,1,0:T(8,128)} %get-tuple-element.79, f32[32,8,48]{2,1,0:T(8,128)} %get-tuple-element.78, f32[32,8,48]{2,1,0:T(8,128)} %get-tuple-element.77, f32[32,8,48]{2,1,0:T(8,128)} %get-tuple-element.76, f32[32,8,48]{2,1,0:T(8,128)} %get-tuple-element.75, f32[32,8,48]{2,1,0:T(8,128)} %get-tuple-element.74, ...), dimensions={2} | concatenate | bytes 786432 | tf_op jit(solution)/shard_map/concatenate | solution.py:109
  62.6 4.3 %collective-permute-start.4 = (f32[32,8,384]{2,1,0:T(8,128)}, f32[32,8,384]{2,1,0:T(8,128)S(1)}, u32[]{:S(2)}, u32[]{:S(2)}) collective-permute-start(f32[32,8,384]{2,1,0:T(8,128)} %concatenate.68), channel_id=1, source_target_pairs={{0,16},{1,17},{2,18},{3,19},{4,20},{5,21},{6,22},{7,23},{8,24},{9,... | collective-permute-start | bytes 1179656 | tf_op jit(solution)/shard_map/ppermute | solution.py:36
  66.9 2.7 %pad_maximum_fusion = f32[32,64,208]{2,1,0:T(8,128)} fusion(f32[32,64,80]{2,1,0:T(8,128)} %get-tuple-element.59, f32[32,64,128]{2,1,0:T(8,128)S(1)} %get-tuple-element.57), kind=kLoop, calls=%fused_computation.4 | loop fusion | flops 425984 | bytes 3407872 | tf_op jit(solution)/shard_map/concatenate | solution.py:178
  69.6 1.4 %fusion.49 = (f32[32,16,80]{2,1,0:T(8,128)S(1)}, f32[32,16,80]{2,1,0:T(8,128)S(1)}, f32[32,16,80]{2,1,0:T(8,128)S(1)}) fusion(f32[32,16,240]{2,1,0:T(8,128)} %collective-permute-done.5), kind=kLoop, calls=%fused_computation.90 | loop fusion | bytes 983040 | tf_op jit(solution)/shard_map/slice | solution.py:114
  71.0 0.3 fusion.38
  71.3 1.5 %collective-permute-start.6 = (f32[32,24,96]{2,1,0:T(8,128)S(1)}, f32[32,24,96]{2,1,0:T(8,128)S(1)}, u32[]{:S(2)}, u32[]{:S(2)}) collective-permute-start(f32[32,24,96]{2,1,0:T(8,128)S(1)} %fusion.38), channel_id=1, source_target_pairs={{0,16},{1,17},{2,18},{3,19},{4,20},{5,21},{6,22},{7,23},{8,24},{9,... | collective-permute-start | bytes 884744 | tf_op jit(solution)/shard_map/ppermute | solution.py:36
  72.8 3.6 %collective-permute-done.4 = f32[32,8,384]{2,1,0:T(8,128)S(1)} collective-permute-done((f32[32,8,384]{2,1,0:T(8,128)}, f32[32,8,384]{2,1,0:T(8,128)S(1)}, u32[]{:S(2)}, u32[]{:S(2)}) %collective-permute-start.4) | collective-permute-done | bytes 393248 | tf_op jit(solution)/shard_map/ppermute | solution.py:36
  77.2 1.6 %fusion.2 = f32[32,64,256]{2,1,0:T(8,128)S(1)} fusion(f32[256,256,1]{1,0,2:T(8,128)S(1)} %copy-done.7, f32[32,64,80]{2,1,0:T(8,128)S(1)} %get-tuple-element.51, f32[32,64,128]{2,1,0:T(8,128)S(1)} %get-tuple-element.56, f32[32,64,48]{2,1,0:T(8,128)S(1)} %slice_dynamic-update-slice_fusion.8), kind=kOutput, calls=%fused_computation.5 | convolution fusion | flops 806354944 | bytes 4456448 | tf_op jit(solution)/shard_map/cxy,vy->cxv/dot_general | solution.py:54
  78.8 1.7 %convolution_bitcast_fusion = f32[32,112,256]{2,1,0:T(8,128)S(1)} fusion(f32[32,64,256]{2,1,0:T(8,128)S(1)} %fusion.2, f32[112,64,1]{0,1,2:T(8,128)S(1)} %copy-done.15), kind=kOutput, calls=%fused_computation.11 | convolution fusion | flops 352321536 | bytes 5795840 | tf_op jit(solution)/shard_map/ux,cxv->cuv/dot_general | solution.py:54
  80.5 1.4 %collective-permute-done.6 = f32[32,24,96]{2,1,0:T(8,128)S(1)} collective-permute-done((f32[32,24,96]{2,1,0:T(8,128)S(1)}, f32[32,24,96]{2,1,0:T(8,128)S(1)}, u32[]{:S(2)}, u32[]{:S(2)}) %collective-permute-start.6) | collective-permute-done | bytes 294944 | tf_op jit(solution)/shard_map/ppermute | solution.py:36
  82.1 2.3 %fusion.8 = f32[32,48,256]{2,1,0:T(8,128)S(1)} fusion(f32[256,256,1]{1,0,2:T(8,128)S(1)} %copy-done.7, f32[32,16,80]{2,1,0:T(8,128)S(1)} %get-tuple-element.87, f32[32,16,80]{2,1,0:T(8,128)S(1)} %get-tuple-element.88, f32[32,16,80]{2,1,0:T(8,128)S(1)} %get-tuple-element.86, f32[16,48,128]{2,1,0:T(8,128)} %collective-permute-done.8, ...), kind=kOutput, calls=%fused_computation.13 | convolution fusion | flops 606339072 | bytes 3407872 | tf_op jit(solution)/shard_map/cxy,vy->cxv/dot_general | solution.py:54
  84.4 1.7 %bitcast_add_fusion = f32[32,112,256]{2,1,0:T(8,128)S(1)} fusion(f32[32,112,256]{2,1,0:T(8,128)S(1)} %convolution_bitcast_fusion, f32[32,48,256]{2,1,0:T(8,128)S(1)} %fusion.8, f32[112,48,1]{0,1,2:T(8,128)S(1)} %copy-done.16), kind=kOutput, calls=%fused_computation | convolution fusion | flops 265158656 | bytes 8934400 | tf_op jit(solution)/shard_map/ux,cxv->cuv/dot_general | solution.py:54
  86.2 0.5 fusion.34
  86.7 0.5 fusion.22
  87.3 1.0 %copy-done.3 = f32[32,112,256]{2,1,0:T(8,128)S(1)} copy-done((f32[32,112,256]{2,1,0:T(8,128)S(1)}, f32[32,112,256]{2,1,0:T(8,128)}, u32[]{:S(2)}) %copy-start.3) | copy-done | bytes 3670040
  88.2 0.7 multiply_reduce_fusion
  88.9 1.3 %collective-permute-done.9 = f32[112,256]{1,0:T(8,128)S(1)} collective-permute-done((f32[112,256]{1,0:T(8,128)S(1)}, f32[112,256]{1,0:T(8,128)S(1)}, u32[]{:S(2)}, u32[]{:S(2)}) %collective-permute-start.9) | collective-permute-done | bytes 114720 | tf_op jit(solution)/shard_map/ppermute | solution.py:187
  90.3 2.1 %broadcast_multiply_fusion = f32[32,112,256]{2,1,0:T(8,128)} fusion(f32[32,112,256]{2,1,0:T(8,128)S(1)} %get-tuple-element.55, f32[112,256]{1,0:T(8,128)S(1)} %multiply_minimum_fusion), kind=kLoop, calls=%fused_computation.12 | loop fusion | flops 917504 | bytes 7454720 | tf_op jit(solution)/shard_map/mul | solution.py:189
  (64 shorter events, 2.2 us)
Async XLA Ops:
  0.6 0.8 copy-start.11
  0.6 2.7 %copy-start.9 = (f32[128,128,1]{1,0,2:T(8,128)S(1)}, f32[128,128,1]{1,0,2:T(8,128)}, u32[]{:S(2)}) copy-start(f32[128,128,1]{1,0,2:T(8,128)} %constant.146) | copy-start | bytes 196612
  0.7 2.1 %copy-start.2 = (f32[32,112,256]{2,1,0:T(8,128)S(1)}, f32[32,112,256]{2,1,0:T(8,128)}, u32[]{:S(2)}) copy-start(f32[32,112,256]{2,1,0:T(8,128)} %param.22) | copy-start | bytes 11010052
  0.7 3.2 %copy-start.4 = (f32[32,112,256]{2,1,0:T(8,128)S(1)}, f32[32,112,256]{2,1,0:T(8,128)}, u32[]{:S(2)}) copy-start(f32[32,112,256]{2,1,0:T(8,128)} %param.22) | copy-start | bytes 11010052
  2.7 1.6 %copy-start.14 = (f32[112,112,1]{1,0,2:T(8,128)S(1)}, f32[112,112,1]{1,0,2:T(8,128)}, u32[]{:S(2)}) copy-start(f32[112,112,1]{1,0,2:T(8,128)} %constant.147) | copy-start | bytes 150532
  4.4 1.8 %copy-start.7 = (f32[256,256,1]{1,0,2:T(8,128)S(1)}, f32[256,256,1]{1,0,2:T(8,128)}, u32[]{:S(2)}) copy-start(f32[256,256,1]{1,0,2:T(8,128)} %constant.148) | copy-start | bytes 786436
  7.8 3.1 %copy-start = (f32[32,112,256]{2,1,0:T(8,128)}, f32[32,112,256]{2,1,0:T(8,128)S(1)}, u32[]{:S(2)}) copy-start(f32[32,112,256]{2,1,0:T(8,128)S(1)} %fusion) | copy-start | bytes 11010052
  8.1 14.2 %collective-permute-start.2 = (f32[32,24,96]{2,1,0:T(8,128)S(1)}, f32[32,24,96]{2,1,0:T(8,128)S(1)}, u32[]{:S(2)}, u32[]{:S(2)}) collective-permute-start(f32[32,24,96]{2,1,0:T(8,128)S(1)} %pad_maximum_fusion.4), channel_id=1, source_target_pairs={{16,0},{17,1},{18,2},{19,3},{20,4},{21,5},{22,6},{23,7},{24,8},{25... | collective-permute-start | bytes 884744 | tf_op jit(solution)/shard_map/ppermute | solution.py:36
  9.6 23.4 %collective-permute-start = (f32[32,48,128]{2,1,0:T(8,128)S(1)}, f32[32,48,128]{2,1,0:T(8,128)}, u32[]{:S(2)}, u32[]{:S(2)}) collective-permute-start(f32[32,48,128]{2,1,0:T(8,128)S(1)} %slice.380), channel_id=1, source_target_pairs={{2,0},{4,2},{6,4},{8,6},{10,8},{12,10},{14,12},{3,1},{5,3},{7,5},{... | collective-permute-start | bytes 2359304 | tf_op jit(solution)/shard_map/ppermute | solution.py:36
  11.4 18.5 %collective-permute-start.1 = (f32[32,8,384]{2,1,0:T(8,128)S(1)}, f32[32,8,384]{2,1,0:T(8,128)S(1)}, u32[]{:S(2)}, u32[]{:S(2)}) collective-permute-start(f32[32,8,384]{2,1,0:T(8,128)S(1)} %concatenate.60), channel_id=1, source_target_pairs={{16,0},{17,1},{18,2},{19,3},{20,4},{21,5},{22,6},{23,7},{24,8},{25... | collective-permute-start | bytes 1179656 | tf_op jit(solution)/shard_map/ppermute | solution.py:36
  12.8 17.2 %copy-start.8 = (f32[64,208]{1,0:T(8,128)}, f32[64,208]{1,0:T(8,128)S(1)}, u32[]{:S(2)}) copy-start(f32[64,208]{1,0:T(8,128)S(1)} %broadcast_multiply_fusion.1) | copy-start | bytes 159748
  22.5 8.2 %copy-start.1 = (f32[32,112,256]{2,1,0:T(8,128)S(1)}, f32[32,112,256]{2,1,0:T(8,128)}, u32[]{:S(2)}) copy-start(f32[32,112,256]{2,1,0:T(8,128)} %copy-done) | copy-start | bytes 11010052
  24.3 8.7 %copy-start.5 = (f32[32,64,208]{2,1,0:T(8,128)S(1)}, f32[32,64,208]{2,1,0:T(8,128)}, u32[]{:S(2)}) copy-start(f32[32,64,208]{2,1,0:T(8,128)} %param.20) | copy-start | bytes 5111812
  24.3 8.7 %copy-start.6 = (bf16[32,64,208]{2,1,0:T(8,128)(2,1)S(1)}, bf16[32,64,208]{2,1,0:T(8,128)(2,1)}, u32[]{:S(2)}) copy-start(bf16[32,64,208]{2,1,0:T(8,128)(2,1)} %param.21) | copy-start | bytes 2555908
  24.6 18.7 %collective-permute-start.3 = (f32[32,16,240]{2,1,0:T(8,128)S(1)}, f32[32,16,240]{2,1,0:T(8,128)S(1)}, u32[]{:S(2)}, u32[]{:S(2)}) collective-permute-start(f32[32,16,240]{2,1,0:T(8,128)S(1)} %pad_maximum_fusion.1), channel_id=1, source_target_pairs={{2,0},{4,2},{6,4},{8,6},{10,8},{12,10},{14,12},{3,1},{5,3},{7,5},{... | collective-permute-start | bytes 1474568 | tf_op jit(solution)/shard_map/ppermute | solution.py:36
  30.1 2.9 %slice-start.1 = ((f32[64,208]{1,0:T(8,128)}), f32[64,128]{1,0:T(8,128)S(1)}, s32[]{:S(2)}) async-start(f32[64,208]{1,0:T(8,128)} %copy-done.8), calls=%async_computation.1 | async-start | bytes 65536 | tf_op jit(solution)/shard_map/slice | solution.py:151
  31.3 12.2 %slice-start = ((f32[64,208]{1,0:T(8,128)}), f32[64,80]{1,0:T(8,128)S(1)}, s32[]{:S(2)}) async-start(f32[64,208]{1,0:T(8,128)} %copy-done.8), calls=%async_computation | async-start | bytes 65536 | tf_op jit(solution)/shard_map/slice | solution.py:151
  46.0 23.6 %collective-permute-start.5 = (f32[32,16,240]{2,1,0:T(8,128)}, f32[32,16,240]{2,1,0:T(8,128)}, u32[]{:S(2)}, u32[]{:S(2)}) collective-permute-start(f32[32,16,240]{2,1,0:T(8,128)} %pad_maximum_fusion.2), channel_id=1, source_target_pairs={{0,2},{2,4},{4,6},{6,8},{8,10},{10,12},{12,14},{1,3},{3,5},{5,7},{... | collective-permute-start | bytes 1474568 | tf_op jit(solution)/shard_map/ppermute | solution.py:36
  52.3 29.8 %collective-permute-start.7 = (f32[16,48,128]{2,1,0:T(8,128)}, f32[16,48,128]{2,1,0:T(8,128)}, u32[]{:S(2)}, u32[]{:S(2)}) collective-permute-start(f32[16,48,128]{2,1,0:T(8,128)} %get-tuple-element.70), channel_id=1, source_target_pairs={{0,2},{2,4},{4,6},{6,8},{8,10},{10,12},{12,14},{1,3},{3,5},{5,7},{... | collective-permute-start | bytes 1179656 | tf_op jit(solution)/shard_map/ppermute | solution.py:36
  54.7 25.7 %collective-permute-start.8 = (f32[16,48,128]{2,1,0:T(8,128)}, f32[16,48,128]{2,1,0:T(8,128)}, u32[]{:S(2)}, u32[]{:S(2)}) collective-permute-start(f32[16,48,128]{2,1,0:T(8,128)} %get-tuple-element.71), channel_id=1, source_target_pairs={{0,2},{2,4},{4,6},{6,8},{8,10},{10,12},{12,14},{1,3},{3,5},{5,7},{... | collective-permute-start | bytes 1179656 | tf_op jit(solution)/shard_map/ppermute | solution.py:36
  62.6 13.9 %collective-permute-start.4 = (f32[32,8,384]{2,1,0:T(8,128)}, f32[32,8,384]{2,1,0:T(8,128)S(1)}, u32[]{:S(2)}, u32[]{:S(2)}) collective-permute-start(f32[32,8,384]{2,1,0:T(8,128)} %concatenate.68), channel_id=1, source_target_pairs={{0,16},{1,17},{2,18},{3,19},{4,20},{5,21},{6,22},{7,23},{8,24},{9,... | collective-permute-start | bytes 1179656 | tf_op jit(solution)/shard_map/ppermute | solution.py:36
  71.3 10.6 %collective-permute-start.6 = (f32[32,24,96]{2,1,0:T(8,128)S(1)}, f32[32,24,96]{2,1,0:T(8,128)S(1)}, u32[]{:S(2)}, u32[]{:S(2)}) collective-permute-start(f32[32,24,96]{2,1,0:T(8,128)S(1)} %fusion.38), channel_id=1, source_target_pairs={{0,16},{1,17},{2,18},{3,19},{4,20},{5,21},{6,22},{7,23},{8,24},{9,... | collective-permute-start | bytes 884744 | tf_op jit(solution)/shard_map/ppermute | solution.py:36
  76.5 2.3 %copy-start.15 = (f32[112,64,1]{0,1,2:T(8,128)S(1)}, f32[112,64,1]{0,1,2:T(8,128)}, u32[]{:S(2)}) copy-start(f32[112,64,1]{0,1,2:T(8,128)} %constant.149) | copy-start | bytes 86020
  80.5 4.0 %copy-start.16 = (f32[112,48,1]{0,1,2:T(8,128)S(1)}, f32[112,48,1]{0,1,2:T(8,128)}, u32[]{:S(2)}) copy-start(f32[112,48,1]{0,1,2:T(8,128)} %constant.150) | copy-start | bytes 64516
  84.4 1.7 %copy-start.10 = (f32[128,128,1]{1,0,2:T(8,128)S(1)}, f32[128,128,1]{1,0,2:T(8,128)}, u32[]{:S(2)}) copy-start(f32[128,128,1]{1,0,2:T(8,128)} %constant.146) | copy-start | bytes 196612
  84.4 2.3 %copy-start.12 = (f32[56,56,1]{1,0,2:T(8,128)S(1)}, f32[56,56,1]{1,0,2:T(8,128)}, u32[]{:S(2)}) copy-start(f32[56,56,1]{1,0,2:T(8,128)} %constant.145) | copy-start | bytes 37636
  86.2 2.0 %copy-start.3 = (f32[32,112,256]{2,1,0:T(8,128)S(1)}, f32[32,112,256]{2,1,0:T(8,128)}, u32[]{:S(2)}) copy-start(f32[32,112,256]{2,1,0:T(8,128)} %param.22) | copy-start | bytes 11010052
  88.2 2.0 %copy-start.13 = (f32[112,256]{1,0:T(8,128)S(1)}, f32[112,256]{1,0:T(8,128)}, u32[]{:S(2)}) copy-start(f32[112,256]{1,0:T(8,128)} %param.23) | copy-start | bytes 344068
  88.9 1.4 %collective-permute-start.9 = (f32[112,256]{1,0:T(8,128)S(1)}, f32[112,256]{1,0:T(8,128)S(1)}, u32[]{:S(2)}, u32[]{:S(2)}) collective-permute-start(f32[112,256]{1,0:T(8,128)S(1)} %get-tuple-element.54), channel_id=1, source_target_pairs={{0,1},{1,0},{2,3},{3,2},{4,5},{5,4},{6,7},{7,6},{8,9},{9,8},{10,11... | collective-permute-start | bytes 344072 | tf_op jit(solution)/shard_map/ppermute | solution.py:187

commit v5 on v4

--- a/solution.py
+++ b/solution.py
@@ -156,14 +156,12 @@
 
     image_head, extrap_head = step(own_head[:, border:], from_right_head, 0, head)
     edge_head = extrap_head[:, tile_x - border :]
-    half = edge_head.shape[0] // 2
-    first_half = passed_along(edge_head[:half], "fx", 1)
     own_tail = with_rows(synthesized[:, border:, border + head :], unpack(*rest))
     from_right_tail = unpack(after(packed_tail[0], (edge_head, own_tail)), border, tail)
     image_tail, extrap_tail = step(own_tail, from_right_tail, head, tile_y)
     edge_tail = pack(extrap_tail[:, tile_x - border :])
     left_tail = unpack(passed_along(edge_tail, "fx", 1), border, tail)
-    second_half = passed_along(edge_head[half:], "fx", 1)
+    left_head = passed_along(edge_head, "fx", 1)
     own_rows = after(extrap_tail, edge_tail)[:, :, tail - border :]
     above_own = passed_along(pack(own_rows), "fy", 1)
     edge_corner = pack(left_tail[:, :, tail - border :])
@@ -176,8 +174,7 @@
     own = level_einsum("cxy,vy->cxv", own, matrix_y)
     own = level_einsum("ux,cxv->cuv", matrix_x[:, border:], own)
     image_next = jnp.concatenate([image_head, image_tail], axis=2)
-    second_half = after(second_half, (own, image_next))
-    left_head = jnp.concatenate([first_half, second_half], axis=0)
+    left_head = after(left_head, (own, image_next))
     edge = jnp.concatenate([above_corner, left_head, left_tail], axis=2)
     edge = level_einsum("cxy,vy->cxv", edge, matrix_y)
     edge = level_einsum("ux,cxv->cuv", matrix_x[:, :border], edge)

time: 92.9 us -> 89.4 us (0.962)
  starting transfers between devices: 23.3 us -> 20.7 us
  waiting for transfers between devices: 30 us -> 28.7 us
    ppermute x9 -> x8, starting transfers between devices: 23.2 us -> 20.7 us  [passed_along(): return lax.ppermute(array, axis, pairs)]
    ppermute x9 -> x8, waiting for transfers between devices: 28.7 us -> 27.4 us  [passed_along(): return lax.ppermute(array, axis, pairs)]
  transfers between devices with their start and end apart: 10 -> 9, of which waited for: 7 -> 7; matrix products, arithmetic and copies ran while one was open for 20% -> 21% of each run, Pallas kernels for 0% -> 0%
where the time goes in v5:
time: 89.4 us; the launch traced here: 88.6 us
  waiting for transfers between devices  28.7 us (32%)
  starting transfers between devices  20.7 us (23%)
  matrix products  12.9 us (14%)
  other arithmetic  12.8 us (14%)
  local copies, waits for them, and re-layouts  12.3 us (14%)
  between operations  1.21 us (1%)
    ppermute x8, waiting for transfers between devices, passed_along(): return lax.ppermute(array, axis, pairs)  27.4 us
    ppermute x8, starting transfers between devices, passed_along(): return lax.ppermute(array, axis, pairs)  20.7 us
    dot_general x10, matrix products, level_einsum(): return jnp.einsum(spec, first, second, precision=lax.Precision.HIGH)  12.9 us
    unnamed x48, local copies, waits for them, and re-layouts  4.76 us
    mul x2, other arithmetic, step(): return (image, (2.0 * image - cube) * weights)  2.95 us
    concatenate x1, other arithmetic, shards(): image_next = jnp.concatenate([image_head, image_tail], axis=2)  2.73 us
    concatenate x2, local copies, waits for them, and re-layouts, pack(): jnp.concatenate([part[:, g * step:(g + 1) * step] for g in range(groups)]...  2.66 us
    add x2, other arithmetic, with_rows(): return own + jnp.pad(incoming, ((0, 0), (0, 0), (tail - border, 0)))  2.42 us
  transfers between devices with their start and end apart: 9, of which 7 were waited for; matrix products, arithmetic and copies ran while one was open for 21% of the time, Pallas kernels for 0%

profile of v5, /device:TPU:0, one launch (start us, length us, event | category | flops | bytes accessed | tf_op | source)
XLA Modules:
  0.0 88.6 jit_solution(15575931507783246450)
XLA Ops:
  0.7 0.7 copy-done.11
  1.4 1.3 %copy-done.2 = f32[32,112,256]{2,1,0:T(8,128)S(1)} copy-done((f32[32,112,256]{2,1,0:T(8,128)S(1)}, f32[32,112,256]{2,1,0:T(8,128)}, u32[]{:S(2)}) %copy-start.2) | copy-done | bytes 3670040
  2.7 0.6 convolution_bitcast_fusion.2
  3.3 0.5 copy-done.4
  3.8 0.5 convolution_dynamic-update-slice_fusion
  4.4 1.8 %fusion.50 = f32[32,256,112]{1,2,0:T(8,128)S(1)} fusion(f32[32,112,256]{2,1,0:T(8,128)S(1)} %convolution_dynamic-update-slice_fusion, f32[112,112,1]{1,0,2:T(8,128)S(1)} %copy-done.14), kind=kOutput, calls=%fused_computation.91 | convolution fusion | flops 616562688 | bytes 7390208 | tf_op jit(solution)/shard_map/ux,cuv->cxv/dot_general | solution.py:54
  6.2 1.7 %fusion = f32[32,112,256]{2,1,0:T(8,128)S(1)} fusion(f32[256,256,1]{1,0,2:T(8,128)S(1)} %copy-done.7, f32[32,256,112]{1,2,0:T(8,128)S(1)} %fusion.50), kind=kOutput, calls=%fused_computation.1 | convolution fusion | flops 1409286144 | bytes 7602176 | tf_op jit(solution)/shard_map/cxv,vy->cxy/dot_general | solution.py:54
  8.1 1.3 %collective-permute-start.2 = (f32[32,24,96]{2,1,0:T(8,128)S(1)}, f32[32,24,96]{2,1,0:T(8,128)S(1)}, u32[]{:S(2)}, u32[]{:S(2)}) collective-permute-start(f32[32,24,96]{2,1,0:T(8,128)S(1)} %pad_maximum_fusion.4), channel_id=1, source_target_pairs={{16,0},{17,1},{18,2},{19,3},{20,4},{21,5},{22,6},{23,7},{24,8},{25... | collective-permute-start | bytes 884744 | tf_op jit(solution)/shard_map/ppermute | solution.py:36
  9.4 0.3 slice.373
  9.6 1.3 %collective-permute-start = (f32[32,48,128]{2,1,0:T(8,128)S(1)}, f32[32,48,128]{2,1,0:T(8,128)}, u32[]{:S(2)}, u32[]{:S(2)}) collective-permute-start(f32[32,48,128]{2,1,0:T(8,128)S(1)} %slice.373), channel_id=1, source_target_pairs={{2,0},{4,2},{6,4},{8,6},{10,8},{12,10},{14,12},{3,1},{5,3},{7,5},{... | collective-permute-start | bytes 2359304 | tf_op jit(solution)/shard_map/ppermute | solution.py:36
  11.0 0.4 concatenate.57
  11.4 1.3 %collective-permute-start.1 = (f32[32,8,384]{2,1,0:T(8,128)S(1)}, f32[32,8,384]{2,1,0:T(8,128)S(1)}, u32[]{:S(2)}, u32[]{:S(2)}) collective-permute-start(f32[32,8,384]{2,1,0:T(8,128)S(1)} %concatenate.57), channel_id=1, source_target_pairs={{16,0},{17,1},{18,2},{19,3},{20,4},{21,5},{22,6},{23,7},{24,8},{25... | collective-permute-start | bytes 1179656 | tf_op jit(solution)/shard_map/ppermute | solution.py:36
  12.8 9.5 %collective-permute-done.2 = f32[32,24,96]{2,1,0:T(8,128)S(1)} collective-permute-done((f32[32,24,96]{2,1,0:T(8,128)S(1)}, f32[32,24,96]{2,1,0:T(8,128)S(1)}, u32[]{:S(2)}, u32[]{:S(2)}) %collective-permute-start.2) | collective-permute-done | bytes 294944 | tf_op jit(solution)/shard_map/ppermute | solution.py:36
  22.3 0.2 fusion.49
  22.5 1.8 %fusion.35 = f32[32,48,80]{2,1,0:T(8,128)S(1)} fusion(f32[32,24,48]{2,1,0:T(8,128)S(1)} %get-tuple-element.93, f32[32,24,48]{2,1,0:T(8,128)S(1)} %get-tuple-element.92, f32[32,112,256]{2,1,0:T(8,128)} %copy-done), kind=kLoop, calls=%fused_computation.51 | loop fusion | flops 614400 | bytes 1277952 | tf_op jit(solution)/shard_map/add | solution.py:144
  24.4 0.3 pad_maximum_fusion.1
  24.6 1.4 %collective-permute-start.3 = (f32[32,16,240]{2,1,0:T(8,128)S(1)}, f32[32,16,240]{2,1,0:T(8,128)S(1)}, u32[]{:S(2)}, u32[]{:S(2)}) collective-permute-start(f32[32,16,240]{2,1,0:T(8,128)S(1)} %pad_maximum_fusion.1), channel_id=1, source_target_pairs={{2,0},{4,2},{6,4},{8,6},{10,8},{12,10},{14,12},{3,1},{5,3},{7,5},{... | collective-permute-start | bytes 1474568 | tf_op jit(solution)/shard_map/ppermute | solution.py:36
  26.1 3.8 %collective-permute-done.1 = f32[32,8,384]{2,1,0:T(8,128)S(1)} collective-permute-done((f32[32,8,384]{2,1,0:T(8,128)S(1)}, f32[32,8,384]{2,1,0:T(8,128)S(1)}, u32[]{:S(2)}, u32[]{:S(2)}) %collective-permute-start.1) | collective-permute-done | bytes 393248 | tf_op jit(solution)/shard_map/ppermute | solution.py:36
  30.7 0.6 slice_add_fusion
  31.3 1.7 %collective-permute-done = f32[32,48,128]{2,1,0:T(8,128)} collective-permute-done((f32[32,48,128]{2,1,0:T(8,128)S(1)}, f32[32,48,128]{2,1,0:T(8,128)}, u32[]{:S(2)}, u32[]{:S(2)}) %collective-permute-start) | collective-permute-done | bytes 786464 | tf_op jit(solution)/shard_map/ppermute | solution.py:36
  33.1 1.6 %subtract_multiply_fusion.1 = (f32[32,64,128]{2,1,0:T(8,128)S(1)}, f32[32,64,128]{2,1,0:T(8,128)S(1)}) fusion(f32[32,64,208]{2,1,0:T(8,128)S(1)} %copy-done.5, f32[64,128]{1,0:T(8,128)S(1)} %slice-done.1, f32[32,48,128]{2,1,0:T(8,128)} %collective-permute-done, f32[32,112,256]{2,1,0:T(8,128)S(1)} %copy-done.1, bf16[32,64,208]{2,1,0:T(8,128)(2,1)S(1)} %copy-done.6), kind=kLoop, calls=%fused_computation.46 | loop fusion | flops 2621440 | bytes 5537792 | tf_op jit(solution)/shard_map/mul | solution.py:155
  34.7 0.9 %slice.400 = f32[32,48,128]{2,1,0:T(8,128)} slice(f32[32,64,128]{2,1,0:T(8,128)S(1)} %get-tuple-element.58), slice={[0:32], [16:64], [0:128]} | slice | bytes 1572864 | tf_op jit(solution)/shard_map/slice | solution.py:158
  35.6 7.7 %collective-permute-done.3 = f32[32,16,240]{2,1,0:T(8,128)S(1)} collective-permute-done((f32[32,16,240]{2,1,0:T(8,128)S(1)}, f32[32,16,240]{2,1,0:T(8,128)S(1)}, u32[]{:S(2)}, u32[]{:S(2)}) %collective-permute-start.3) | collective-permute-done | bytes 491552 | tf_op jit(solution)/shard_map/ppermute | solution.py:36
  43.3 0.2 fusion.47
  43.5 1.3 %subtract_multiply_fusion = (f32[32,64,80]{2,1,0:T(8,128)S(1)}, f32[32,64,80]{2,1,0:T(8,128)}) fusion(f32[32,64,208]{2,1,0:T(8,128)S(1)} %copy-done.5, f32[64,80]{1,0:T(8,128)S(1)} %slice-done, f32[32,64,80]{2,1,0:T(8,128)S(1)} %slice_add_fusion, f32[32,16,80]{2,1,0:T(8,128)S(1)} %get-tuple-element.88, f32[32,16,80]{2,1,0:T(8,128)S(1)} %get-tuple-element.89, ...), kind=kLoop, calls=%fused_computation.45 | loop fusion | flops 2621440 | bytes 3461120 | tf_op jit(solution)/shard_map/mul | solution.py:155
  44.9 1.1 %pad_maximum_fusion.2 = f32[32,16,240]{2,1,0:T(8,128)} fusion(f32[32,16,80]{2,1,0:T(8,128)S(1)} %get-tuple-element.79, f32[32,16,80]{2,1,0:T(8,128)S(1)} %get-tuple-element.80, f32[32,16,80]{2,1,0:T(8,128)S(1)} %get-tuple-element.78), kind=kLoop, calls=%fused_computation.54 | loop fusion | flops 245760 | bytes 983040 | tf_op jit(solution)/shard_map/concatenate | solution.py:109
  46.0 5.3 %collective-permute-start.5 = (f32[32,16,240]{2,1,0:T(8,128)}, f32[32,16,240]{2,1,0:T(8,128)}, u32[]{:S(2)}, u32[]{:S(2)}) collective-permute-start(f32[32,16,240]{2,1,0:T(8,128)} %pad_maximum_fusion.2), channel_id=1, source_target_pairs={{0,2},{2,4},{4,6},{6,8},{8,10},{10,12},{12,14},{1,3},{3,5},{5,7},{... | collective-permute-start | bytes 1474568 | tf_op jit(solution)/shard_map/ppermute | solution.py:36
  51.4 2.6 %collective-permute-start.7 = (f32[32,48,128]{2,1,0:T(8,128)}, f32[32,48,128]{2,1,0:T(8,128)}, u32[]{:S(2)}, u32[]{:S(2)}) collective-permute-start(f32[32,48,128]{2,1,0:T(8,128)} %slice.400), channel_id=1, source_target_pairs={{0,2},{2,4},{4,6},{6,8},{8,10},{10,12},{12,14},{1,3},{3,5},{5,7},{... | collective-permute-start | bytes 2359304 | tf_op jit(solution)/shard_map/ppermute | solution.py:36
  54.0 1.2 %fusion.43 = (f32[32,8,48]{2,1,0:T(8,128)S(1)}, f32[32,8,48]{2,1,0:T(8,128)}, f32[32,8,48]{2,1,0:T(8,128)}, f32[32,8,48]{2,1,0:T(8,128)}, f32[32,8,48]{2,1,0:T(8...) fusion(f32[32,64,80]{2,1,0:T(8,128)S(1)} %get-tuple-element.51), kind=kLoop, calls=%fused_computation.84 | loop fusion | bytes 786432 | tf_op jit(solution)/shard_map/slice | solution.py:109
  55.2 2.3 %concatenate.65 = f32[32,8,384]{2,1,0:T(8,128)} concatenate(f32[32,8,48]{2,1,0:T(8,128)} %get-tuple-element.77, f32[32,8,48]{2,1,0:T(8,128)} %get-tuple-element.76, f32[32,8,48]{2,1,0:T(8,128)} %get-tuple-element.75, f32[32,8,48]{2,1,0:T(8,128)} %get-tuple-element.74, f32[32,8,48]{2,1,0:T(8,128)} %get-tuple-element.73, f32[32,8,48]{2,1,0:T(8,128)} %get-tuple-element.72, ...), dimensions={2} | concatenate | bytes 786432 | tf_op jit(solution)/shard_map/concatenate | solution.py:109
  57.5 4.3 %collective-permute-start.4 = (f32[32,8,384]{2,1,0:T(8,128)}, f32[32,8,384]{2,1,0:T(8,128)S(1)}, u32[]{:S(2)}, u32[]{:S(2)}) collective-permute-start(f32[32,8,384]{2,1,0:T(8,128)} %concatenate.65), channel_id=1, source_target_pairs={{0,16},{1,17},{2,18},{3,19},{4,20},{5,21},{6,22},{7,23},{8,24},{9,... | collective-permute-start | bytes 1179656 | tf_op jit(solution)/shard_map/ppermute | solution.py:36
  61.8 2.7 %pad_maximum_fusion = f32[32,64,208]{2,1,0:T(8,128)} fusion(f32[32,64,80]{2,1,0:T(8,128)} %get-tuple-element.57, f32[32,64,128]{2,1,0:T(8,128)S(1)} %get-tuple-element.59), kind=kLoop, calls=%fused_computation.4 | loop fusion | flops 425984 | bytes 3407872 | tf_op jit(solution)/shard_map/concatenate | solution.py:176
  64.5 1.4 %fusion.46 = (f32[32,16,80]{2,1,0:T(8,128)S(1)}, f32[32,16,80]{2,1,0:T(8,128)S(1)}, f32[32,16,80]{2,1,0:T(8,128)S(1)}) fusion(f32[32,16,240]{2,1,0:T(8,128)} %collective-permute-done.5), kind=kLoop, calls=%fused_computation.87 | loop fusion | bytes 983040 | tf_op jit(solution)/shard_map/slice | solution.py:114
  66.0 0.3 fusion.36
  66.3 3.1 %collective-permute-start.6 = (f32[32,24,96]{2,1,0:T(8,128)S(1)}, f32[32,24,96]{2,1,0:T(8,128)S(1)}, u32[]{:S(2)}, u32[]{:S(2)}) collective-permute-start(f32[32,24,96]{2,1,0:T(8,128)S(1)} %fusion.36), channel_id=1, source_target_pairs={{0,16},{1,17},{2,18},{3,19},{4,20},{5,21},{6,22},{7,23},{8,24},{9,... | collective-permute-start | bytes 884744 | tf_op jit(solution)/shard_map/ppermute | solution.py:36
  69.4 2.2 %collective-permute-done.4 = f32[32,8,384]{2,1,0:T(8,128)S(1)} collective-permute-done((f32[32,8,384]{2,1,0:T(8,128)}, f32[32,8,384]{2,1,0:T(8,128)S(1)}, u32[]{:S(2)}, u32[]{:S(2)}) %collective-permute-start.4) | collective-permute-done | bytes 393248 | tf_op jit(solution)/shard_map/ppermute | solution.py:36
  72.3 1.6 %fusion.2 = f32[32,64,256]{2,1,0:T(8,128)S(1)} fusion(f32[256,256,1]{1,0,2:T(8,128)S(1)} %copy-done.7, f32[32,64,80]{2,1,0:T(8,128)S(1)} %get-tuple-element.51, f32[32,64,128]{2,1,0:T(8,128)S(1)} %get-tuple-element.58, f32[32,64,48]{2,1,0:T(8,128)S(1)} %slice_dynamic-update-slice_fusion.8), kind=kOutput, calls=%fused_computation.5 | convolution fusion | flops 806354944 | bytes 4456448 | tf_op jit(solution)/shard_map/cxy,vy->cxv/dot_general | solution.py:54
  73.9 1.7 %convolution_bitcast_fusion = f32[32,112,256]{2,1,0:T(8,128)S(1)} fusion(f32[32,64,256]{2,1,0:T(8,128)S(1)} %fusion.2, f32[112,64,1]{0,1,2:T(8,128)S(1)} %copy-done.15), kind=kOutput, calls=%fused_computation.11 | convolution fusion | flops 352321536 | bytes 5795840 | tf_op jit(solution)/shard_map/ux,cxv->cuv/dot_general | solution.py:54
  75.6 2.4 %collective-permute-done.7 = f32[32,48,128]{2,1,0:T(8,128)} collective-permute-done((f32[32,48,128]{2,1,0:T(8,128)}, f32[32,48,128]{2,1,0:T(8,128)}, u32[]{:S(2)}, u32[]{:S(2)}) %collective-permute-start.7) | collective-permute-done | bytes 786464 | tf_op jit(solution)/shard_map/ppermute | solution.py:36
  78.0 0.2 fusion.48
  78.2 2.4 %fusion.8 = f32[32,48,256]{2,1,0:T(8,128)S(1)} fusion(f32[256,256,1]{1,0,2:T(8,128)S(1)} %copy-done.7, f32[32,16,80]{2,1,0:T(8,128)S(1)} %get-tuple-element.85, f32[32,16,80]{2,1,0:T(8,128)S(1)} %get-tuple-element.86, f32[32,16,80]{2,1,0:T(8,128)S(1)} %get-tuple-element.84, f32[32,48,128]{2,1,0:T(8,128)} %collective-permute-done.7, ...), kind=kOutput, calls=%fused_computation.13 | convolution fusion | flops 605945856 | bytes 3407872 | tf_op jit(solution)/shard_map/cxy,vy->cxv/dot_general | solution.py:54
  80.6 1.7 %bitcast_add_fusion = f32[32,112,256]{2,1,0:T(8,128)S(1)} fusion(f32[32,112,256]{2,1,0:T(8,128)S(1)} %convolution_bitcast_fusion, f32[32,48,256]{2,1,0:T(8,128)S(1)} %fusion.8, f32[112,48,1]{0,1,2:T(8,128)S(1)} %copy-done.16), kind=kOutput, calls=%fused_computation | convolution fusion | flops 265158656 | bytes 8934400 | tf_op jit(solution)/shard_map/ux,cxv->cuv/dot_general | solution.py:54
  82.3 0.5 fusion.32
  82.9 0.5 fusion.20
  83.4 0.9 %copy-done.3 = f32[32,112,256]{2,1,0:T(8,128)S(1)} copy-done((f32[32,112,256]{2,1,0:T(8,128)S(1)}, f32[32,112,256]{2,1,0:T(8,128)}, u32[]{:S(2)}) %copy-start.3) | copy-done | bytes 3670040
  84.4 0.7 multiply_reduce_fusion
  85.1 1.3 %collective-permute-done.8 = f32[112,256]{1,0:T(8,128)S(1)} collective-permute-done((f32[112,256]{1,0:T(8,128)S(1)}, f32[112,256]{1,0:T(8,128)S(1)}, u32[]{:S(2)}, u32[]{:S(2)}) %collective-permute-start.8) | collective-permute-done | bytes 114720 | tf_op jit(solution)/shard_map/ppermute | solution.py:184
  86.5 2.1 %broadcast_multiply_fusion = f32[32,112,256]{2,1,0:T(8,128)} fusion(f32[32,112,256]{2,1,0:T(8,128)S(1)} %get-tuple-element.55, f32[112,256]{1,0:T(8,128)S(1)} %multiply_minimum_fusion), kind=kLoop, calls=%fused_computation.12 | loop fusion | flops 917504 | bytes 7454720 | tf_op jit(solution)/shard_map/mul | solution.py:186
  (62 shorter events, 2.0 us)
Async XLA Ops:
  0.6 0.8 copy-start.11
  0.6 2.7 %copy-start.9 = (f32[128,128,1]{1,0,2:T(8,128)S(1)}, f32[128,128,1]{1,0,2:T(8,128)}, u32[]{:S(2)}) copy-start(f32[128,128,1]{1,0,2:T(8,128)} %constant.146) | copy-start | bytes 196612
  0.7 2.1 %copy-start.2 = (f32[32,112,256]{2,1,0:T(8,128)S(1)}, f32[32,112,256]{2,1,0:T(8,128)}, u32[]{:S(2)}) copy-start(f32[32,112,256]{2,1,0:T(8,128)} %param.22) | copy-start | bytes 11010052
  0.7 3.2 %copy-start.4 = (f32[32,112,256]{2,1,0:T(8,128)S(1)}, f32[32,112,256]{2,1,0:T(8,128)}, u32[]{:S(2)}) copy-start(f32[32,112,256]{2,1,0:T(8,128)} %param.22) | copy-start | bytes 11010052
  2.7 1.6 %copy-start.14 = (f32[112,112,1]{1,0,2:T(8,128)S(1)}, f32[112,112,1]{1,0,2:T(8,128)}, u32[]{:S(2)}) copy-start(f32[112,112,1]{1,0,2:T(8,128)} %constant.147) | copy-start | bytes 150532
  4.4 1.8 %copy-start.7 = (f32[256,256,1]{1,0,2:T(8,128)S(1)}, f32[256,256,1]{1,0,2:T(8,128)}, u32[]{:S(2)}) copy-start(f32[256,256,1]{1,0,2:T(8,128)} %constant.148) | copy-start | bytes 786436
  7.8 3.1 %copy-start = (f32[32,112,256]{2,1,0:T(8,128)}, f32[32,112,256]{2,1,0:T(8,128)S(1)}, u32[]{:S(2)}) copy-start(f32[32,112,256]{2,1,0:T(8,128)S(1)} %fusion) | copy-start | bytes 11010052
  8.1 14.2 %collective-permute-start.2 = (f32[32,24,96]{2,1,0:T(8,128)S(1)}, f32[32,24,96]{2,1,0:T(8,128)S(1)}, u32[]{:S(2)}, u32[]{:S(2)}) collective-permute-start(f32[32,24,96]{2,1,0:T(8,128)S(1)} %pad_maximum_fusion.4), channel_id=1, source_target_pairs={{16,0},{17,1},{18,2},{19,3},{20,4},{21,5},{22,6},{23,7},{24,8},{25... | collective-permute-start | bytes 884744 | tf_op jit(solution)/shard_map/ppermute | solution.py:36
  9.6 23.4 %collective-permute-start = (f32[32,48,128]{2,1,0:T(8,128)S(1)}, f32[32,48,128]{2,1,0:T(8,128)}, u32[]{:S(2)}, u32[]{:S(2)}) collective-permute-start(f32[32,48,128]{2,1,0:T(8,128)S(1)} %slice.373), channel_id=1, source_target_pairs={{2,0},{4,2},{6,4},{8,6},{10,8},{12,10},{14,12},{3,1},{5,3},{7,5},{... | collective-permute-start | bytes 2359304 | tf_op jit(solution)/shard_map/ppermute | solution.py:36
  11.4 18.5 %collective-permute-start.1 = (f32[32,8,384]{2,1,0:T(8,128)S(1)}, f32[32,8,384]{2,1,0:T(8,128)S(1)}, u32[]{:S(2)}, u32[]{:S(2)}) collective-permute-start(f32[32,8,384]{2,1,0:T(8,128)S(1)} %concatenate.57), channel_id=1, source_target_pairs={{16,0},{17,1},{18,2},{19,3},{20,4},{21,5},{22,6},{23,7},{24,8},{25... | collective-permute-start | bytes 1179656 | tf_op jit(solution)/shard_map/ppermute | solution.py:36
  12.8 17.2 %copy-start.8 = (f32[64,208]{1,0:T(8,128)}, f32[64,208]{1,0:T(8,128)S(1)}, u32[]{:S(2)}) copy-start(f32[64,208]{1,0:T(8,128)S(1)} %broadcast_multiply_fusion.1) | copy-start | bytes 159748
  22.5 8.2 %copy-start.1 = (f32[32,112,256]{2,1,0:T(8,128)S(1)}, f32[32,112,256]{2,1,0:T(8,128)}, u32[]{:S(2)}) copy-start(f32[32,112,256]{2,1,0:T(8,128)} %copy-done) | copy-start | bytes 11010052
  24.3 8.7 %copy-start.5 = (f32[32,64,208]{2,1,0:T(8,128)S(1)}, f32[32,64,208]{2,1,0:T(8,128)}, u32[]{:S(2)}) copy-start(f32[32,64,208]{2,1,0:T(8,128)} %param.20) | copy-start | bytes 5111812
  24.3 8.7 %copy-start.6 = (bf16[32,64,208]{2,1,0:T(8,128)(2,1)S(1)}, bf16[32,64,208]{2,1,0:T(8,128)(2,1)}, u32[]{:S(2)}) copy-start(bf16[32,64,208]{2,1,0:T(8,128)(2,1)} %param.21) | copy-start | bytes 2555908
  24.6 18.7 %collective-permute-start.3 = (f32[32,16,240]{2,1,0:T(8,128)S(1)}, f32[32,16,240]{2,1,0:T(8,128)S(1)}, u32[]{:S(2)}, u32[]{:S(2)}) collective-permute-start(f32[32,16,240]{2,1,0:T(8,128)S(1)} %pad_maximum_fusion.1), channel_id=1, source_target_pairs={{2,0},{4,2},{6,4},{8,6},{10,8},{12,10},{14,12},{3,1},{5,3},{7,5},{... | collective-permute-start | bytes 1474568 | tf_op jit(solution)/shard_map/ppermute | solution.py:36
  30.1 2.9 %slice-start.1 = ((f32[64,208]{1,0:T(8,128)}), f32[64,128]{1,0:T(8,128)S(1)}, s32[]{:S(2)}) async-start(f32[64,208]{1,0:T(8,128)} %copy-done.8), calls=%async_computation.1 | async-start | bytes 65536 | tf_op jit(solution)/shard_map/slice | solution.py:151
  31.3 12.2 %slice-start = ((f32[64,208]{1,0:T(8,128)}), f32[64,80]{1,0:T(8,128)S(1)}, s32[]{:S(2)}) async-start(f32[64,208]{1,0:T(8,128)} %copy-done.8), calls=%async_computation | async-start | bytes 65536 | tf_op jit(solution)/shard_map/slice | solution.py:151
  46.0 18.5 %collective-permute-start.5 = (f32[32,16,240]{2,1,0:T(8,128)}, f32[32,16,240]{2,1,0:T(8,128)}, u32[]{:S(2)}, u32[]{:S(2)}) collective-permute-start(f32[32,16,240]{2,1,0:T(8,128)} %pad_maximum_fusion.2), channel_id=1, source_target_pairs={{0,2},{2,4},{4,6},{6,8},{8,10},{10,12},{12,14},{1,3},{3,5},{5,7},{... | collective-permute-start | bytes 1474568 | tf_op jit(solution)/shard_map/ppermute | solution.py:36
  51.4 26.7 %collective-permute-start.7 = (f32[32,48,128]{2,1,0:T(8,128)}, f32[32,48,128]{2,1,0:T(8,128)}, u32[]{:S(2)}, u32[]{:S(2)}) collective-permute-start(f32[32,48,128]{2,1,0:T(8,128)} %slice.400), channel_id=1, source_target_pairs={{0,2},{2,4},{4,6},{6,8},{8,10},{10,12},{12,14},{1,3},{3,5},{5,7},{... | collective-permute-start | bytes 2359304 | tf_op jit(solution)/shard_map/ppermute | solution.py:36
  57.5 14.1 %collective-permute-start.4 = (f32[32,8,384]{2,1,0:T(8,128)}, f32[32,8,384]{2,1,0:T(8,128)S(1)}, u32[]{:S(2)}, u32[]{:S(2)}) collective-permute-start(f32[32,8,384]{2,1,0:T(8,128)} %concatenate.65), channel_id=1, source_target_pairs={{0,16},{1,17},{2,18},{3,19},{4,20},{5,21},{6,22},{7,23},{8,24},{9,... | collective-permute-start | bytes 1179656 | tf_op jit(solution)/shard_map/ppermute | solution.py:36
  66.3 11.8 %collective-permute-start.6 = (f32[32,24,96]{2,1,0:T(8,128)S(1)}, f32[32,24,96]{2,1,0:T(8,128)S(1)}, u32[]{:S(2)}, u32[]{:S(2)}) collective-permute-start(f32[32,24,96]{2,1,0:T(8,128)S(1)} %fusion.36), channel_id=1, source_target_pairs={{0,16},{1,17},{2,18},{3,19},{4,20},{5,21},{6,22},{7,23},{8,24},{9,... | collective-permute-start | bytes 884744 | tf_op jit(solution)/shard_map/ppermute | solution.py:36
  71.6 2.3 %copy-start.15 = (f32[112,64,1]{0,1,2:T(8,128)S(1)}, f32[112,64,1]{0,1,2:T(8,128)}, u32[]{:S(2)}) copy-start(f32[112,64,1]{0,1,2:T(8,128)} %constant.149) | copy-start | bytes 86020
  75.6 5.0 %copy-start.16 = (f32[112,48,1]{0,1,2:T(8,128)S(1)}, f32[112,48,1]{0,1,2:T(8,128)}, u32[]{:S(2)}) copy-start(f32[112,48,1]{0,1,2:T(8,128)} %constant.150) | copy-start | bytes 64516
  80.6 1.7 %copy-start.10 = (f32[128,128,1]{1,0,2:T(8,128)S(1)}, f32[128,128,1]{1,0,2:T(8,128)}, u32[]{:S(2)}) copy-start(f32[128,128,1]{1,0,2:T(8,128)} %constant.146) | copy-start | bytes 196612
  80.6 2.3 %copy-start.12 = (f32[56,56,1]{1,0,2:T(8,128)S(1)}, f32[56,56,1]{1,0,2:T(8,128)}, u32[]{:S(2)}) copy-start(f32[56,56,1]{1,0,2:T(8,128)} %constant.145) | copy-start | bytes 37636
  82.3 2.0 %copy-start.3 = (f32[32,112,256]{2,1,0:T(8,128)S(1)}, f32[32,112,256]{2,1,0:T(8,128)}, u32[]{:S(2)}) copy-start(f32[32,112,256]{2,1,0:T(8,128)} %param.22) | copy-start | bytes 11010052
  84.4 2.0 %copy-start.13 = (f32[112,256]{1,0:T(8,128)S(1)}, f32[112,256]{1,0:T(8,128)}, u32[]{:S(2)}) copy-start(f32[112,256]{1,0:T(8,128)} %param.23) | copy-start | bytes 344068
  85.0 1.4 %collective-permute-start.8 = (f32[112,256]{1,0:T(8,128)S(1)}, f32[112,256]{1,0:T(8,128)S(1)}, u32[]{:S(2)}, u32[]{:S(2)}) collective-permute-start(f32[112,256]{1,0:T(8,128)S(1)} %get-tuple-element.54), channel_id=1, source_target_pairs={{0,1},{1,0},{2,3},{3,2},{4,5},{5,4},{6,7},{7,6},{8,9},{9,8},{10,11... | collective-permute-start | bytes 344072 | tf_op jit(solution)/shard_map/ppermute | solution.py:184
